TPU v7x, 32 devices: a whole 2x2x4 slice. The times are simulated.
32 devices in a mesh: batch: 8 (over y, x, core), heads: 4 (over z).
Axes of the slice: x: 2, y: 2, z: 4, core: 2. Of those that a mesh axis runs over, the one named last changes fastest.
Arguments:
- tokens: bfloat16 [24576, 768], P('batch'), may hold values from -5 to 5
- qkv_weight: bfloat16 [768, 3, 768], P(None, None, 'heads'), may hold values from -0.21875 to 0.21875
- qv_bias: float32 [2, 768], replicated, may hold values from -3 to 3
- conv_weight: float32 [12, 33], replicated, may hold values from -0.875 to 0.875
- out_weight: bfloat16 [768, 768], P('heads'), may hold values from -0.21875 to 0.21875
- out_bias: float32 [768], replicated, may hold values from -1.75 to 1.75
- norm1_gain: float32 [768], replicated, may hold values from 0.5 to 1.5
- norm1_bias: float32 [768], replicated, may hold values from -1.75 to 1.75
- ffn_in_weight: bfloat16 [768, 3072], P(None, ('batch', 'heads')), may hold values from -0.21875 to 0.21875
- ffn_in_bias: bfloat16 [3072], P(('batch', 'heads')), may hold values from -3 to 3
- ffn_out_weight: bfloat16 [3072, 768], P(('batch', 'heads')), may hold values from -0.109375 to 0.109375
- ffn_out_bias: float32 [768], replicated, may hold values from -1.75 to 1.75
- norm2_gain: float32 [768], replicated, may hold values from 0.5 to 1.5
- norm2_bias: float32 [768], replicated, may hold values from -1.75 to 1.75
- cotangent: bfloat16 [24576, 768], P(('batch', 'heads')), may hold values from -12 to 12
- seq_lengths: int32 [24], P('batch'), may hold values from 0 to 3072, as said below
- segment_ids: int32 [24576], P('batch'), may hold values from 0 to 3, as said below
- landmark_bounds: int32 [24, 64], P('batch'), may hold values from 0 to 3024, as said below
Outputs:
- out: bfloat16 [24576, 768], P(('batch', 'heads'))
- input_grad: float32 [24576, 768], P(('batch', 'heads'))
- qkv_weight_grad: float32 [768, 3, 768], P('batch', None, 'heads')
- qv_bias_grad: float32 [2, 768], P(None, 'heads')
- conv_grad: float32 [12, 33], P('heads')
- out_weight_grad: float32 [768, 768], P('heads', 'batch')
- ffn_in_grad: float32 [768, 3072], P(None, ('batch', 'heads'))
- ffn_in_bias_grad: float32 [3072], P(('batch', 'heads'))
- ffn_out_grad: float32 [3072, 768], P(('batch', 'heads'))
- vector_grads: float32 [6, 768], P(None, ('batch', 'heads'))
- condition: float32 [], replicated
Inputs may be any that keep to these rules, and one draw needn't show every extreme that they name: `seq_lengths`: each index of batch holds 3 slots: sequences of 1024 to 3072 tokens first, then empty slots of length 0; the lengths of one index sum to at most 3072; at least one index holds a single sequence of 3072 tokens. `segment_ids`: the live tokens of an index of batch lie in order of slot from its first token slot on, each slot's tokens contiguous; the remaining token slots carry 3. landmark_bounds[s, j] = (j times the length of slot s) // 64.
All inputs are finite; a program needn't handle non-finite values.
Results may differ from a plain program's by a relative error of at most 0.013.
Values may be sent and summed in bfloat16 or wider, within the bound.
A program may use at most 448 MiB of HBM per device.

v0:
```python
from functools import partial

import jax
import jax.numpy as jnp
from jax import lax
from jax.sharding import PartitionSpec as P

HEAD_DIM = 64
PINV_ITERS = 6


best_precision = lax.Precision.HIGHEST
mask_fill = -1000000000.0
norm_eps = 1e-05
contract_rows = (((0,), (0,)), ((), ()))
contract_cols = (((1,), (1,)), ((), ()))


def split_up(x, dim, peers):
    before, after = (x.shape[:dim], x.shape[dim + 1 :])
    return jnp.moveaxis(x.reshape(*before, peers, -1, *after), dim, 0)


def sum_at_owner(x, axis, dim):
    peers = lax.axis_size(axis)
    tiles = lax.all_to_all(split_up(x, dim, peers), axis, 0, 0, tiled=True)
    return jnp.sum(tiles.astype(jnp.float32), axis=0)


def layer_norm(row_data, gain_vec, shift_vec):
    centre = row_data - jnp.mean(row_data, axis=1, keepdims=True)
    spread = jnp.mean(centre * centre, axis=1, keepdims=True)
    return centre * lax.rsqrt(spread + norm_eps) * gain_vec[None, :] + shift_vec[None, :]


def gelu_exact(values):
    return jax.nn.gelu(values, approximate=False)


def pack_layout(lengths, slot_ids, bounds):
    slot_count = lengths.shape[0]
    tok_count = slot_ids.shape[0]
    mark_count = bounds.shape[1]
    starts = jnp.cumsum(lengths) - lengths
    slot_hit = slot_ids[:, None] == jnp.arange(slot_count, dtype=jnp.int32)[None, :]
    tok_start = jnp.sum(jnp.where(slot_hit, starts[None, :], 0), axis=1)
    position = jnp.arange(tok_count, dtype=jnp.int32) - tok_start
    tok_bounds = jnp.sum(jnp.where(slot_hit[:, :, None], bounds[None, :, :], 0), axis=1)
    mark_index = jnp.sum((tok_bounds <= position[:, None]).astype(jnp.int32), axis=1) - 1
    mark_id = slot_ids * mark_count + mark_index
    all_marks = slot_count * mark_count
    member = (jnp.arange(all_marks, dtype=jnp.int32)[:, None] == mark_id[None, :]).astype(
        jnp.float32
    )
    inv_count = 1.0 / jnp.maximum(jnp.sum(member, axis=1), 1.0)
    same_slot = slot_ids[:, None] == (jnp.arange(all_marks, dtype=jnp.int32) // mark_count)[None, :]
    live_tok = (slot_ids < slot_count).astype(jnp.float32)
    live_slot = (lengths > 0).astype(jnp.float32)
    return (member, inv_count, same_slot, slot_ids, live_tok, live_slot)


def batch_mul(left, right):
    return jnp.einsum("...ij,...jk->...ik", left, right, precision=best_precision)


def newton_inverse(middle_kernel):
    mark_count = middle_kernel.shape[-1]
    column_sums = jnp.sum(middle_kernel, axis=-2)
    col_bound = jnp.max(column_sums, axis=-1)
    inverse = jnp.swapaxes(middle_kernel, -1, -2) / col_bound[..., None, None]
    identity_mat = jnp.eye(mark_count, dtype=jnp.float32)
    for sweep_index in range(PINV_ITERS):
        product = batch_mul(middle_kernel, inverse)
        inner_poly = 7.0 * identity_mat - product
        inner_poly = 15.0 * identity_mat - batch_mul(product, inner_poly)
        inner_poly = 13.0 * identity_mat - batch_mul(product, inner_poly)
        inverse = 0.25 * batch_mul(inverse, inner_poly)
    return (inverse, col_bound)


def head_mix(q_rows, k_rows, v_rows, conv_taps, layout):
    member, inv_count, same_slot, token_slot, live_tok, live_slot = layout
    slot_count = live_slot.shape[0]
    tok_count, head_dim = q_rows.shape
    mark_count = member.shape[0] // slot_count
    root_scale = head_dim ** (-0.25)
    q_scaled = q_rows * root_scale
    k_scaled = k_rows * root_scale
    q_marks = jnp.dot(member, q_scaled, precision=best_precision) * inv_count[:, None]
    k_marks = jnp.dot(member, k_scaled, precision=best_precision) * inv_count[:, None]
    first_scores = jnp.where(
        same_slot, jnp.dot(q_scaled, k_marks.T, precision=best_precision), mask_fill
    )
    first_kernel = jax.nn.softmax(first_scores, axis=1)
    q_blocks = q_marks.reshape(slot_count, mark_count, head_dim)
    k_blocks = k_marks.reshape(slot_count, mark_count, head_dim)
    middle_kernel = jax.nn.softmax(
        jnp.einsum("sid,sjd->sij", q_blocks, k_blocks, precision=best_precision), axis=2
    )
    inverse, col_bound = newton_inverse(middle_kernel)
    last_scores = jnp.where(
        same_slot.T, jnp.dot(q_marks, k_scaled.T, precision=best_precision), mask_fill
    )
    last_kernel = jax.nn.softmax(last_scores, axis=1)
    mark_values = jnp.dot(last_kernel, v_rows, precision=best_precision)
    mixed_marks = jnp.einsum(
        "sij,sjd->sid",
        inverse,
        mark_values.reshape(slot_count, mark_count, head_dim),
        precision=best_precision,
    ).reshape(slot_count * mark_count, head_dim)
    attended = jnp.dot(first_kernel, mixed_marks, precision=best_precision)
    half_width = conv_taps.shape[0] // 2
    padded_v = jnp.pad(v_rows, ((half_width, half_width), (0, 0)))
    padded_slot = jnp.pad(token_slot, (half_width, half_width), constant_values=-1)
    convolved = jnp.zeros_like(v_rows)
    for tap_index in range(conv_taps.shape[0]):
        same_seq = (padded_slot[tap_index : tap_index + tok_count] == token_slot).astype(
            jnp.float32
        )
        convolved = (
            convolved
            + conv_taps[tap_index] * padded_v[tap_index : tap_index + tok_count] * same_seq[:, None]
        )
    mixed_rows = (attended + convolved) * live_tok[:, None]
    return (mixed_rows, jnp.sum(col_bound * live_slot))


def heads_mix(layout, q_all, k_all, v_all, conv_all):
    tok_count = q_all.shape[0]
    head_count = conv_all.shape[0]
    head_dim = q_all.shape[1] // head_count

    def split_heads(row_data):
        return jnp.transpose(row_data.reshape(tok_count, head_count, head_dim), (1, 0, 2))

    def one_head(operands):
        return head_mix(operands[0], operands[1], operands[2], operands[3], layout)

    mixed_rows, bound_sums = lax.map(
        jax.checkpoint(one_head),
        (split_heads(q_all), split_heads(k_all), split_heads(v_all), conv_all),
    )
    merged = jnp.transpose(mixed_rows, (1, 0, 2)).reshape(tok_count, head_count * head_dim)
    return (merged, jnp.sum(bound_sums))


def body(
    tokens,
    qkv_weight,
    qv_bias,
    conv_weight,
    out_weight,
    out_bias,
    norm1_gain,
    norm1_bias,
    ffn_in_weight,
    ffn_in_bias,
    ffn_out_weight,
    ffn_out_bias,
    norm2_gain,
    norm2_bias,
    cotangent,
    seq_lengths,
    segment_ids,
    landmark_bounds,
):
    tok_count, model_width = tokens.shape
    head_width = qkv_weight.shape[2]
    heads_here = head_width // HEAD_DIM
    head_total = conv_weight.shape[0]
    kernel_taps = conv_weight.shape[1]
    quarter = tok_count // lax.axis_size("heads")
    head_index = lax.axis_index("heads")
    own_start = head_index * quarter
    layout = pack_layout(seq_lengths, segment_ids, landmark_bounds)
    own_rows_low = lax.dynamic_slice_in_dim(tokens, own_start, quarter, 0)
    own_tokens = own_rows_low.astype(jnp.float32)
    conv_own = lax.dynamic_slice_in_dim(conv_weight, head_index * heads_here, heads_here, 0)
    qv_own = lax.dynamic_slice_in_dim(qv_bias, head_index * head_width, head_width, 1)
    flat_qkv = qkv_weight.reshape(model_width, 3 * head_width)
    projected = jnp.dot(tokens, flat_qkv, preferred_element_type=jnp.float32).reshape(
        tok_count, 3, head_width
    )
    bias_rows = jnp.stack([qv_own[0], jnp.zeros_like(qv_own[0]), qv_own[1]])
    qkv_low = (projected + bias_rows[None, :, :]).astype(jnp.bfloat16)
    qkv_wide = lax.optimization_barrier(qkv_low).astype(jnp.float32)
    (mixed_rows, bound_total), mix_pull = jax.vjp(
        partial(heads_mix, layout), qkv_wide[:, 0], qkv_wide[:, 1], qkv_wide[:, 2], conv_own
    )
    mixed_low = mixed_rows.astype(jnp.bfloat16)
    row_block = mixed_low
    attn_part = lax.psum_scatter(
        jnp.dot(row_block, out_weight, preferred_element_type=jnp.float32).astype(jnp.bfloat16),
        "heads",
        scatter_dimension=0,
        tiled=True,
    ).astype(jnp.float32)
    live_count = jnp.sum(layout[5]) * heads_here
    first_res = own_tokens + attn_part + out_bias[None, :]
    norm1_out, norm1_pull = jax.vjp(layer_norm, first_res, norm1_gain, norm1_bias)
    norm1_low = norm1_out.astype(jnp.bfloat16)
    whole_in, whole_in_bias, whole_out = (
        lax.all_gather(ffn_in_weight, ("batch", "heads"), axis=1, tiled=True),
        lax.all_gather(ffn_in_bias, ("batch", "heads"), axis=0, tiled=True),
        lax.all_gather(ffn_out_weight, ("batch", "heads"), axis=0, tiled=True),
    )
    pre_act = (
        jnp.dot(norm1_low, whole_in, preferred_element_type=jnp.float32)
        + whole_in_bias.astype(jnp.float32)[None, :]
    )
    hidden_act, gelu_pull = jax.vjp(gelu_exact, pre_act)
    hidden_low = hidden_act.astype(jnp.bfloat16)
    ffn_result = (
        jnp.dot(hidden_low, whole_out, preferred_element_type=jnp.float32) + ffn_out_bias[None, :]
    )
    final_out, norm2_pull = jax.vjp(layer_norm, norm1_out + ffn_result, norm2_gain, norm2_bias)
    grad_second, grad_gain_two, grad_shift_two = norm2_pull(cotangent.astype(jnp.float32))
    grad_ffn_low = grad_second.astype(jnp.bfloat16)
    grad_ffn_bias = jnp.sum(grad_ffn_low.astype(jnp.float32), axis=0)
    down_term = lax.dot_general(
        hidden_low, grad_ffn_low, contract_rows, preferred_element_type=jnp.float32
    )
    grad_hidden = lax.dot_general(
        grad_ffn_low, whole_out, contract_cols, preferred_element_type=jnp.float32
    )
    grad_pre = gelu_pull(grad_hidden)[0].astype(jnp.bfloat16)
    grad_in_bias = jnp.sum(grad_pre.astype(jnp.float32), axis=0)
    up_term = lax.dot_general(
        norm1_low, grad_pre, contract_rows, preferred_element_type=jnp.float32
    )
    grad_norm1 = grad_second + lax.dot_general(
        grad_pre, whole_in, contract_cols, preferred_element_type=jnp.float32
    )
    grad_first, grad_gain_one, grad_shift_one = norm1_pull(grad_norm1)
    grad_attn_low = grad_first.astype(jnp.bfloat16)
    grad_out_bias = jnp.sum(grad_attn_low.astype(jnp.float32), axis=0)
    piece_rows = lax.all_gather(grad_attn_low, "heads", axis=0, tiled=True)
    local_grad = lax.dot_general(
        piece_rows, out_weight, contract_cols, preferred_element_type=jnp.float32
    )
    grad_mix = local_grad
    grad_weight = lax.dot_general(
        mixed_low, piece_rows, contract_rows, preferred_element_type=jnp.float32
    )
    grad_mix, out_part = (grad_mix, grad_weight)
    grad_mix_low = lax.optimization_barrier(grad_mix.astype(jnp.bfloat16)).astype(jnp.float32)
    grad_query, grad_key, grad_value, grad_conv = mix_pull(
        (grad_mix_low, jnp.zeros((), jnp.float32))
    )
    grad_qkv = jnp.stack([grad_query, grad_key, grad_value], axis=1).astype(jnp.bfloat16)
    grad_qv_own = jnp.stack(
        [
            jnp.sum(grad_qkv[:, 0].astype(jnp.float32), axis=0),
            jnp.sum(grad_qkv[:, 2].astype(jnp.float32), axis=0),
        ]
    )
    flat_grad = grad_qkv.reshape(tok_count, 3 * head_width)
    qkv_part = lax.dot_general(
        tokens, flat_grad, contract_rows, preferred_element_type=jnp.float32
    ).reshape(model_width, 3, head_width)
    row_block = flat_grad
    input_part = lax.psum_scatter(
        lax.dot_general(
            row_block, flat_qkv, contract_cols, preferred_element_type=jnp.float32
        ).astype(jnp.bfloat16),
        "heads",
        scatter_dimension=0,
        tiled=True,
    ).astype(jnp.float32)
    input_grad = grad_first + input_part
    conv_full = lax.dynamic_update_slice_in_dim(
        jnp.zeros((head_total, kernel_taps), jnp.float32), grad_conv, head_index * heads_here, 0
    )
    bias_full = lax.dynamic_update_slice_in_dim(
        jnp.zeros((2, head_total * HEAD_DIM), jnp.float32), grad_qv_own, head_index * head_width, 1
    )
    qkv_share, out_share = (
        sum_at_owner(qkv_part.astype(jnp.bfloat16), "batch", 0),
        sum_at_owner(out_part.astype(jnp.bfloat16), "batch", 1),
    )
    vector_all = jnp.stack(
        [grad_ffn_bias, grad_gain_two, grad_shift_two, grad_gain_one, grad_shift_one, grad_out_bias]
    )
    up_share, in_bias_share, down_share, vector_share = (
        lax.psum_scatter(up_term, ("batch", "heads"), scatter_dimension=1, tiled=True),
        lax.psum_scatter(grad_in_bias, ("batch", "heads"), scatter_dimension=0, tiled=True),
        lax.psum_scatter(down_term, ("batch", "heads"), scatter_dimension=0, tiled=True),
        lax.psum_scatter(vector_all, ("batch", "heads"), scatter_dimension=1, tiled=True),
    )
    conv_sum, bias_sum, bound_all, count_all = lax.psum(
        (conv_full, bias_full, bound_total, live_count), ("batch", "heads")
    )
    conv_out = lax.dynamic_slice_in_dim(conv_sum, head_index * heads_here, heads_here, 0)
    bias_out = lax.dynamic_slice_in_dim(bias_sum, head_index * head_width, head_width, 1)
    condition = bound_all / count_all
    return (
        final_out.astype(jnp.bfloat16),
        input_grad,
        qkv_share,
        bias_out,
        conv_out,
        out_share,
        up_share,
        in_bias_share,
        down_share,
        vector_share,
        condition,
    )


def solution(mesh):
    in_specs = (
        P("batch", None),
        P(None, None, "heads"),
        P(),
        P(),
        P("heads", None),
        P(),
        P(),
        P(),
        P(None, ("batch", "heads")),
        P(("batch", "heads")),
        P(("batch", "heads"), None),
        P(),
        P(),
        P(),
        P(("batch", "heads"), None),
        P("batch"),
        P("batch"),
        P("batch", None),
    )
    out_specs = (
        P(("batch", "heads"), None),
        P(("batch", "heads"), None),
        P("batch", None, "heads"),
        P(None, "heads"),
        P("heads", None),
        P("heads", "batch"),
        P(None, ("batch", "heads")),
        P(("batch", "heads")),
        P(("batch", "heads"), None),
        P(None, ("batch", "heads")),
        P(),
    )
    return jax.shard_map(body, mesh=mesh, in_specs=in_specs, out_specs=out_specs, check_vma=False)
```

profile of v0, /device:TPU:0, one launch (start us, length us, event | category | flops | bytes accessed | tf_op | source)
XLA Modules:
  0.0 1467.5 jit_solution(8246713149489868916)
XLA Ops:
  19.8 5.5 add_convert_fusion.1
  28.4 4.9 copy.212
  33.3 5.0 copy.213
  40.1 224.6 %while.41 = (s32[]{:T(128)}, bf16[3,3072,64]{1,2,0:T(8,128)(2,1)}, f32[3]{0:T(128)}, f32[3,3072,64]{2,1,0:T(8,128)}, f32[3,3072,64]{2,1,0:T(8,128)}, /*index=5*/...) while((s32[]{:T(128)}, bf16[3,3072,64]{1,2,0:T(8,128)(2,1)}, ...), condition=%wide.region_15.16_spmd.clone.clone.clone, body=%wide.region_5.15_spmd.clone.clone.clone.sunk | while | flops 2994648576 | bytes 44281500 | solution.py:140
  56.1 4.2 fusion.1197
  60.4 4.9 fusion.1196
  93.0 30.5 %fusion.1216 = bf16[3,3072,64]{1,2,0:T(8,128)(2,1)S(1)} fusion(bf16[3,3072,64]{1,2,0:T(8,128)(2,1)S(1)} %copy-done.43, s32[]{:T(128)S(6)} %copy.285, f32[192,64]{1,0:T(8,128)S(1)} %bitcast.1284, f32[3072,192]{0,1:T(8,128)S(1)} %get-tuple-element.2748, f32[3072]{0:T(1024)S(1)} %fusion.1213, f32[3072]{0:T(1024)S(1)} %get-tuple-element.2749, ...), kind=kOutput, calls=%fused_computation.368.clone.1 | convolution fusion | flops 473628672 | bytes 4460680 | tf_op jit(solution)/shard_map/jvp()/while/body/eval_jaxpr/dot_general | solution.py:112
  130.3 4.9 fusion.1196
  162.9 30.5 %fusion.1216 = bf16[3,3072,64]{1,2,0:T(8,128)(2,1)S(1)} fusion(bf16[3,3072,64]{1,2,0:T(8,128)(2,1)S(1)} %copy-done.43, s32[]{:T(128)S(6)} %copy.285, f32[192,64]{1,0:T(8,128)S(1)} %bitcast.1284, f32[3072,192]{0,1:T(8,128)S(1)} %get-tuple-element.2748, f32[3072]{0:T(1024)S(1)} %fusion.1213, f32[3072]{0:T(1024)S(1)} %get-tuple-element.2749, ...), kind=kOutput, calls=%fused_computation.368.clone.1 | convolution fusion | flops 473628672 | bytes 4460680 | tf_op jit(solution)/shard_map/jvp()/while/body/eval_jaxpr/dot_general | solution.py:112
  200.2 4.9 fusion.1196
  232.8 30.5 %fusion.1216 = bf16[3,3072,64]{1,2,0:T(8,128)(2,1)S(1)} fusion(bf16[3,3072,64]{1,2,0:T(8,128)(2,1)S(1)} %copy-done.43, s32[]{:T(128)S(6)} %copy.285, f32[192,64]{1,0:T(8,128)S(1)} %bitcast.1284, f32[3072,192]{0,1:T(8,128)S(1)} %get-tuple-element.2748, f32[3072]{0:T(1024)S(1)} %fusion.1213, f32[3072]{0:T(1024)S(1)} %get-tuple-element.2749, ...), kind=kOutput, calls=%fused_computation.368.clone.1 | convolution fusion | flops 473628672 | bytes 4460680 | tf_op jit(solution)/shard_map/jvp()/while/body/eval_jaxpr/dot_general | solution.py:112
  264.8 4.9 convolution_convert_fusion
  271.2 46.6 %all-reduce.70 = bf16[3072]{0:T(1024)(128)(2,1)S(1)} all-reduce(bf16[3072]{0:T(1024)(128)(2,1)S(1)} %dynamic-update-slice), channel_id=1, replica_groups=mesh['batch'=8,'heads'=4] {'batch','heads'}, use_global_device_ids=true, to_apply=%add.70 | all-reduce | flops 3072 | bytes 12288
  317.8 43.4 %reduce-scatter.6.cloned.1.call-done = bf16[768,768]{1,0:T(8,128)(2,1)} async-done(((bf16[3072,768]{1,0:T(8,128)(2,1)}), bf16[768,768]{1,0:T(8,128)(2,1)}) %reduce-scatter.6.cloned.1.call-update) | async-done | bytes 1179664 | tf_op jit(solution)/shard_map/reduce_scatter | solution.py:193
  365.4 40.0 %all-gather.4.cloned.1.call-done = bf16[768,3072]{0,1:T(8,128)(2,1)} async-done(((bf16[768,96]{0,1:T(8,128)(2,1)}), bf16[768,3072]{0,1:T(8,128)(2,1)}) %all-gather.4.cloned.1.call-update) | async-done | bytes 4718608 | tf_op jit(solution)/shard_map/all_gather | solution.py:204
  405.5 30.0 %multiply_convert_fusion = (bf16[768,3072]{1,0:T(8,128)(2,1)}, f32[768,3072]{1,0:T(8,128)}, f32[768,3072]{1,0:T(8,128)}) fusion(f32[3072]{0:T(1024)S(1)} %convert_element_type.470, bf16[768,3072]{0,1:T(8,128)(2,1)} %all-gather.4.cloned.1.call-done, f32[768]{0:T(1024)S(1)} %copy-done.130, f32[768]{0:T(1024)S(1)} %copy-done.121, f32[768]{0:T(1024)S(1)} %fusion.363, ...), kind=kOutput, calls=%fused_computation.512 | convolution fusion | flops 3784900608 | bytes 30698500 | tf_op jit(solution)/shard_map/dot_general | solution.py:209
  435.5 34.8 %all-gather.6.cloned.1.call-done = bf16[3072,768]{1,0:T(8,128)(2,1)} async-done(((bf16[96,768]{1,0:T(8,128)(2,1)}), bf16[3072,768]{1,0:T(8,128)(2,1)}) %all-gather.6.cloned.1.call-update) | async-done | bytes 4718608 | tf_op jit(solution)/shard_map/all_gather | solution.py:206
  470.3 8.6 fusion.386
  484.6 13.4 convert_reduce_fusion.1
  498.1 8.4 multiply_reduce_fusion.37
  511.1 87.8 %all-gather.8.cloned.1.call-done = bf16[3072,768]{1,0:T(8,128)(2,1)} async-done(((bf16[768,768]{1,0:T(8,128)(2,1)}), bf16[3072,768]{1,0:T(8,128)(2,1)}) %all-gather.8.cloned.1.call-update) | async-done | bytes 4718608 | tf_op jit(solution)/shard_map/all_gather | solution.py:238
  608.8 471.6 %while.40 = (s32[]{:T(128)}, bf16[3,3072,64]{1,2,0:T(8,128)(2,1)}, bf16[3,3072,64]{1,2,0:T(8,128)(2,1)}, bf16[3,3072,64]{1,2,0:T(8,128)(2,1)}, f32[3,33]{1,0:T(4...) while((s32[]{:T(128)}, bf16[3,3072,64]{1,2,0:T(8,128)(2,1)}, ...), condition=%wide.region_72.73_spmd.clone.clone, body=%wide.region_25.72_spmd.clone.clone.sunk | while | flops 7593409024 | bytes 344024704 | solution.py:140
  686.2 4.2 multiply_reduce_fusion.52
  710.4 7.9 multiply_reduce_fusion.55
  718.3 20.7 %add_bitcast_fusion.2 = f32[1,33]{1,0:T(1,128)S(1)} fusion(f32[1]{0:T(128)} %bitcast.1088, f32[1]{0:T(128)} %bitcast.1089, f32[1]{0:T(128)} %bitcast.1090, f32[1]{0:T(128)} %bitcast.1091, f32[1]{0:T(128)} %bitcast.1092, f32[1]{0:T(128)} %bitcast.1093, f32[1]{0:T(128)} %bitcast.1094, f32[1]{0:T(128)} %bitcast.1095, f32[1]{0:T(128)} %bitcast.1096, ...), kind=kLoop, calls=%fused_computation.342.clone.1 | loop fusion | flops 1056 | bytes 264 | tf_op jit(solution)/shard_map/transpose(jvp())/while/body/jit(dynamic_update_index_in_dim)/broadcast_in_dim | solution.py:140
  740.4 6.0 multiply_multiply_fusion.42
  746.5 6.5 multiply_multiply_fusion.41
  753.2 5.9 pad_add_fusion.8
  840.9 4.2 multiply_reduce_fusion.52
  865.0 7.9 multiply_reduce_fusion.55
  872.8 20.8 %add_bitcast_fusion.2 = f32[1,33]{1,0:T(1,128)S(1)} fusion(f32[1]{0:T(128)} %bitcast.1088, f32[1]{0:T(128)} %bitcast.1089, f32[1]{0:T(128)} %bitcast.1090, f32[1]{0:T(128)} %bitcast.1091, f32[1]{0:T(128)} %bitcast.1092, f32[1]{0:T(128)} %bitcast.1093, f32[1]{0:T(128)} %bitcast.1094, f32[1]{0:T(128)} %bitcast.1095, f32[1]{0:T(128)} %bitcast.1096, ...), kind=kLoop, calls=%fused_computation.342.clone.1 | loop fusion | flops 1056 | bytes 264 | tf_op jit(solution)/shard_map/transpose(jvp())/while/body/jit(dynamic_update_index_in_dim)/broadcast_in_dim | solution.py:140
  895.0 6.0 multiply_multiply_fusion.42
  901.1 6.5 multiply_multiply_fusion.41
  907.8 5.9 pad_add_fusion.8
  995.7 4.2 multiply_reduce_fusion.52
  1019.8 7.9 multiply_reduce_fusion.55
  1027.6 20.7 %add_bitcast_fusion.2 = f32[1,33]{1,0:T(1,128)S(1)} fusion(f32[1]{0:T(128)} %bitcast.1088, f32[1]{0:T(128)} %bitcast.1089, f32[1]{0:T(128)} %bitcast.1090, f32[1]{0:T(128)} %bitcast.1091, f32[1]{0:T(128)} %bitcast.1092, f32[1]{0:T(128)} %bitcast.1093, f32[1]{0:T(128)} %bitcast.1094, f32[1]{0:T(128)} %bitcast.1095, f32[1]{0:T(128)} %bitcast.1096, ...), kind=kLoop, calls=%fused_computation.342.clone.1 | loop fusion | flops 1056 | bytes 264 | tf_op jit(solution)/shard_map/transpose(jvp())/while/body/jit(dynamic_update_index_in_dim)/broadcast_in_dim | solution.py:140
  1049.7 6.0 multiply_multiply_fusion.42
  1055.8 6.5 multiply_multiply_fusion.41
  1062.5 5.9 pad_add_fusion.8
  1084.4 5.6 bitcast_convert_fusion
  1091.3 10.5 fusion.366
  1103.1 8.7 fusion.407
  1123.1 7.2 fusion.297
  1135.6 4.3 all-to-all-start
  1142.2 49.4 %all-reduce.73 = (f32[2,768]{1,0:T(2,128)S(1)}, f32[12,33]{1,0:T(8,128)S(1)}, f32[3072]{0:T(1024)S(1)}, f32[6,768]{1,0:T(8,128)S(1)}, f32[]{:T(128)}, /*index=5*/f32[]{:T(128)}) all-reduce(f32[2,768]{1,0:T(2,128)S(1)} %dynamic_update_slice.61, ...), channel_id=1, replica_groups=mesh['batch'=8,'heads'=4] {'batch','heads'}, use_global_device_ids=true, to_apply=%region_77.78 | all-reduce | flops 9614 | bytes 76912 | tf_op jit(solution)/shard_map/psum | solution.py:291
  1202.8 114.4 %reduce-scatter.10.cloned.1.call-done = f32[768,96]{0,1:T(8,128)} async-done(((f32[768,3072]{0,1:T(8,128)}), f32[768,96]{0,1:T(8,128)}) %reduce-scatter.10.cloned.1.call-update) | async-done | bytes 294928 | tf_op jit(solution)/shard_map/reduce_scatter | solution.py:286
  1317.2 141.9 %reduce-scatter.12.cloned.1.call-done = f32[96,768]{1,0:T(8,128)} async-done(((f32[3072,768]{1,0:T(8,128)}), f32[96,768]{1,0:T(8,128)}) %reduce-scatter.12.cloned.1.call-update) | async-done | bytes 294928 | tf_op jit(solution)/shard_map/reduce_scatter | solution.py:288
  (1278 shorter events, 478.7 us)
Async XLA Ops:
  8.0 353.2 %reduce-scatter.6.cloned.1.call-start = ((), (), s32[]{:S(2)}) async-start(), calls=%async_computation.6 | async-start | bytes 5898240 | tf_op jit(solution)/shard_map/reduce_scatter | solution.py:193
  93.0 31.6 %copy-start.126 = (f32[3,33]{1,0:T(4,128)S(1)}, f32[3,33]{1,0:T(4,128)}, u32[]{:S(2)}) copy-start(f32[3,33]{1,0:T(4,128)} %copy-done.125) | copy-start | bytes 1192 | tf_op jit(solution)/shard_map/jvp()/while
  162.9 31.6 %copy-start.126 = (f32[3,33]{1,0:T(4,128)S(1)}, f32[3,33]{1,0:T(4,128)}, u32[]{:S(2)}) copy-start(f32[3,33]{1,0:T(4,128)} %copy-done.125) | copy-start | bytes 1192 | tf_op jit(solution)/shard_map/jvp()/while
  232.8 31.6 %copy-start.126 = (f32[3,33]{1,0:T(4,128)S(1)}, f32[3,33]{1,0:T(4,128)}, u32[]{:S(2)}) copy-start(f32[3,33]{1,0:T(4,128)} %copy-done.125) | copy-start | bytes 1192 | tf_op jit(solution)/shard_map/jvp()/while
  269.7 91.6 %copy-start.95 = (f32[768]{0:T(1024)S(1)}, f32[768]{0:T(1024)}, u32[]{:S(2)}) copy-start(f32[768]{0:T(1024)} %param.27) | copy-start | bytes 9220
  269.7 135.8 %all-gather.4.cloned.1.call-start = ((), (), s32[]{:S(2)}) async-start(), calls=%async_computation.7 | async-start | bytes 4866048 | tf_op jit(solution)/shard_map/all_gather | solution.py:204
  270.3 200.0 %all-gather.6.cloned.1.call-start = ((), (), s32[]{:S(2)}) async-start(), calls=%async_computation.8 | async-start | bytes 4866048 | tf_op jit(solution)/shard_map/all_gather | solution.py:206
  270.9 328.1 %all-gather.8.cloned.1.call-start = ((), (), s32[]{:S(2)}) async-start(), calls=%async_computation.9 | async-start | bytes 5898240 | tf_op jit(solution)/shard_map/all_gather | solution.py:238
  317.8 87.7 %copy-start.121 = (f32[768]{0:T(1024)S(1)}, f32[768]{0:T(1024)}, u32[]{:S(2)}) copy-start(f32[768]{0:T(1024)} %param.28) | copy-start | bytes 9220
  317.8 87.7 %copy-start.130 = (f32[768]{0:T(1024)S(1)}, f32[768]{0:T(1024)}, u32[]{:S(2)}) copy-start(f32[768]{0:T(1024)} %param.29) | copy-start | bytes 9220
  363.4 143.1 %copy-start.99 = (f32[768]{0:T(1024)}, f32[768]{0:T(1024)S(1)}, u32[]{:S(2)}) copy-start(f32[768]{0:T(1024)S(1)} %broadcast_multiply_fusion.5) | copy-start | bytes 9220
  365.4 141.1 %copy-start.106 = (f32[768]{0:T(1024)}, f32[768]{0:T(1024)S(1)}, u32[]{:S(2)}) copy-start(f32[768]{0:T(1024)S(1)} %fusion.363) | copy-start | bytes 9220
  365.4 104.9 %copy-start.129 = (f32[768]{0:T(1024)S(1)}, f32[768]{0:T(1024)}, u32[]{:S(2)}) copy-start(f32[768]{0:T(1024)} %param.33) | copy-start | bytes 9220
  481.6 16.4 %slice-start = ((s8[4718592]{0:T(1024)(128)(4,1)}), s8[4194304]{0:T(1024)(128)(4,1)S(1)}, s32[]{:S(2)}) async-start(s8[4718592]{0:T(1024)(128)(4,1)} %bitcast.1282), calls=%async_computation.13 | async-start | bytes 8388608
  511.1 688.7 %reduce-scatter.8.cloned.1.call-start = ((), (), s32[]{:S(2)}) async-start(), calls=%async_computation.10 | async-start | bytes 5898240 | tf_op jit(solution)/shard_map/reduce_scatter | solution.py:263
  630.7 15.7 %copy-start.62 = (f32[3072]{0:T(1024)}, f32[3072]{0:T(1024)S(1)}, u32[]{:S(2)}) copy-start(f32[3072]{0:T(1024)S(1)} %get-tuple-element.2576) | copy-start | bytes 36868 | tf_op jit(solution)/shard_map/transpose(jvp())/while
  630.7 19.8 %copy-start.56 = (f32[3072]{0:T(1024)}, f32[3072]{0:T(1024)S(1)}, u32[]{:S(2)}) copy-start(f32[3072]{0:T(1024)S(1)} %get-tuple-element.2574) | copy-start | bytes 36868 | tf_op jit(solution)/shard_map/transpose(jvp())/while
  630.7 19.8 %copy-start.58 = (f32[3072]{0:T(1024)}, f32[3072]{0:T(1024)S(1)}, u32[]{:S(2)}) copy-start(f32[3072]{0:T(1024)S(1)} %get-tuple-element.2572) | copy-start | bytes 36868 | tf_op jit(solution)/shard_map/transpose(jvp())/while
  630.7 19.8 %copy-start.60 = (f32[3072]{0:T(1024)}, f32[3072]{0:T(1024)S(1)}, u32[]{:S(2)}) copy-start(f32[3072]{0:T(1024)S(1)} %get-tuple-element.2570) | copy-start | bytes 36868 | tf_op jit(solution)/shard_map/transpose(jvp())/while
  657.3 41.9 %copy-start.87 = (f32[192]{0:T(256)}, f32[192]{0:T(256)S(1)}, u32[]{:S(2)}) copy-start(f32[192]{0:T(256)S(1)} %get-tuple-element.2549) | copy-start | bytes 2308 | tf_op jit(solution)/shard_map/transpose(jvp())/while
  657.8 41.5 %copy-start.91 = (f32[192]{0:T(256)}, f32[192]{0:T(256)S(1)}, u32[]{:S(2)}) copy-start(f32[192]{0:T(256)S(1)} %fusion.1098) | copy-start | bytes 2308 | tf_op jit(solution)/shard_map/transpose(jvp())/while
  710.4 29.9 %copy-start.69 = (f32[3072]{0:T(1024)S(1)}, f32[3072]{0:T(1024)}, u32[]{:S(2)}) copy-start(f32[3072]{0:T(1024)} %copy-done.68) | copy-start | bytes 36868 | tf_op jit(solution)/shard_map/transpose(jvp())/while
  710.4 29.9 %copy-start.71 = (f32[3072]{0:T(1024)S(1)}, f32[3072]{0:T(1024)}, u32[]{:S(2)}) copy-start(f32[3072]{0:T(1024)} %copy-done.70) | copy-start | bytes 36868 | tf_op jit(solution)/shard_map/transpose(jvp())/while
  710.4 29.9 %copy-start.73 = (f32[3072]{0:T(1024)S(1)}, f32[3072]{0:T(1024)}, u32[]{:S(2)}) copy-start(f32[3072]{0:T(1024)} %copy-done.72) | copy-start | bytes 36868 | tf_op jit(solution)/shard_map/transpose(jvp())/while
  785.2 15.7 %copy-start.62 = (f32[3072]{0:T(1024)}, f32[3072]{0:T(1024)S(1)}, u32[]{:S(2)}) copy-start(f32[3072]{0:T(1024)S(1)} %get-tuple-element.2576) | copy-start | bytes 36868 | tf_op jit(solution)/shard_map/transpose(jvp())/while
  785.2 19.8 %copy-start.56 = (f32[3072]{0:T(1024)}, f32[3072]{0:T(1024)S(1)}, u32[]{:S(2)}) copy-start(f32[3072]{0:T(1024)S(1)} %get-tuple-element.2574) | copy-start | bytes 36868 | tf_op jit(solution)/shard_map/transpose(jvp())/while
  785.2 19.8 %copy-start.58 = (f32[3072]{0:T(1024)}, f32[3072]{0:T(1024)S(1)}, u32[]{:S(2)}) copy-start(f32[3072]{0:T(1024)S(1)} %get-tuple-element.2572) | copy-start | bytes 36868 | tf_op jit(solution)/shard_map/transpose(jvp())/while
  785.2 19.8 %copy-start.60 = (f32[3072]{0:T(1024)}, f32[3072]{0:T(1024)S(1)}, u32[]{:S(2)}) copy-start(f32[3072]{0:T(1024)S(1)} %get-tuple-element.2570) | copy-start | bytes 36868 | tf_op jit(solution)/shard_map/transpose(jvp())/while
  812.1 41.7 %copy-start.87 = (f32[192]{0:T(256)}, f32[192]{0:T(256)S(1)}, u32[]{:S(2)}) copy-start(f32[192]{0:T(256)S(1)} %get-tuple-element.2549) | copy-start | bytes 2308 | tf_op jit(solution)/shard_map/transpose(jvp())/while
  812.5 41.2 %copy-start.91 = (f32[192]{0:T(256)}, f32[192]{0:T(256)S(1)}, u32[]{:S(2)}) copy-start(f32[192]{0:T(256)S(1)} %fusion.1098) | copy-start | bytes 2308 | tf_op jit(solution)/shard_map/transpose(jvp())/while
  865.0 30.0 %copy-start.69 = (f32[3072]{0:T(1024)S(1)}, f32[3072]{0:T(1024)}, u32[]{:S(2)}) copy-start(f32[3072]{0:T(1024)} %copy-done.68) | copy-start | bytes 36868 | tf_op jit(solution)/shard_map/transpose(jvp())/while
  865.0 29.9 %copy-start.71 = (f32[3072]{0:T(1024)S(1)}, f32[3072]{0:T(1024)}, u32[]{:S(2)}) copy-start(f32[3072]{0:T(1024)} %copy-done.70) | copy-start | bytes 36868 | tf_op jit(solution)/shard_map/transpose(jvp())/while
  865.0 29.9 %copy-start.73 = (f32[3072]{0:T(1024)S(1)}, f32[3072]{0:T(1024)}, u32[]{:S(2)}) copy-start(f32[3072]{0:T(1024)} %copy-done.72) | copy-start | bytes 36868 | tf_op jit(solution)/shard_map/transpose(jvp())/while
  940.0 15.7 %copy-start.62 = (f32[3072]{0:T(1024)}, f32[3072]{0:T(1024)S(1)}, u32[]{:S(2)}) copy-start(f32[3072]{0:T(1024)S(1)} %get-tuple-element.2576) | copy-start | bytes 36868 | tf_op jit(solution)/shard_map/transpose(jvp())/while
  940.0 19.8 %copy-start.56 = (f32[3072]{0:T(1024)}, f32[3072]{0:T(1024)S(1)}, u32[]{:S(2)}) copy-start(f32[3072]{0:T(1024)S(1)} %get-tuple-element.2574) | copy-start | bytes 36868 | tf_op jit(solution)/shard_map/transpose(jvp())/while
  940.0 19.8 %copy-start.58 = (f32[3072]{0:T(1024)}, f32[3072]{0:T(1024)S(1)}, u32[]{:S(2)}) copy-start(f32[3072]{0:T(1024)S(1)} %get-tuple-element.2572) | copy-start | bytes 36868 | tf_op jit(solution)/shard_map/transpose(jvp())/while
  940.0 19.8 %copy-start.60 = (f32[3072]{0:T(1024)}, f32[3072]{0:T(1024)S(1)}, u32[]{:S(2)}) copy-start(f32[3072]{0:T(1024)S(1)} %get-tuple-element.2570) | copy-start | bytes 36868 | tf_op jit(solution)/shard_map/transpose(jvp())/while
  966.6 41.9 %copy-start.87 = (f32[192]{0:T(256)}, f32[192]{0:T(256)S(1)}, u32[]{:S(2)}) copy-start(f32[192]{0:T(256)S(1)} %get-tuple-element.2549) | copy-start | bytes 2308 | tf_op jit(solution)/shard_map/transpose(jvp())/while
  967.1 41.4 %copy-start.91 = (f32[192]{0:T(256)}, f32[192]{0:T(256)S(1)}, u32[]{:S(2)}) copy-start(f32[192]{0:T(256)S(1)} %fusion.1098) | copy-start | bytes 2308 | tf_op jit(solution)/shard_map/transpose(jvp())/while
  1019.7 29.9 %copy-start.69 = (f32[3072]{0:T(1024)S(1)}, f32[3072]{0:T(1024)}, u32[]{:S(2)}) copy-start(f32[3072]{0:T(1024)} %copy-done.68) | copy-start | bytes 36868 | tf_op jit(solution)/shard_map/transpose(jvp())/while
  1019.7 29.9 %copy-start.71 = (f32[3072]{0:T(1024)S(1)}, f32[3072]{0:T(1024)}, u32[]{:S(2)}) copy-start(f32[3072]{0:T(1024)} %copy-done.70) | copy-start | bytes 36868 | tf_op jit(solution)/shard_map/transpose(jvp())/while
  1019.8 29.9 %copy-start.73 = (f32[3072]{0:T(1024)S(1)}, f32[3072]{0:T(1024)}, u32[]{:S(2)}) copy-start(f32[3072]{0:T(1024)} %copy-done.72) | copy-start | bytes 36868 | tf_op jit(solution)/shard_map/transpose(jvp())/while
  1090.1 227.1 %reduce-scatter.10.cloned.1.call-start = ((), (), s32[]{:S(2)}) async-start(), calls=%async_computation.11 | async-start | bytes 9732096 | tf_op jit(solution)/shard_map/reduce_scatter | solution.py:286
  1101.9 357.2 %reduce-scatter.12.cloned.1.call-start = ((), (), s32[]{:S(2)}) async-start(), calls=%async_computation.12 | async-start | bytes 9732096 | tf_op jit(solution)/shard_map/reduce_scatter | solution.py:288
  1119.2 15.6 %all-to-all-start.1 = ((bf16[8,192,96]{2,1,0:T(8,128)(2,1)}), bf16[8,192,96]{2,1,0:T(8,128)(2,1)S(1)}, u32[]{:S(2)}, u32[]{:S(2)}) async-start(bf16[8,192,96]{2,1,0:T(8,128)(2,1)} %bitcast.526), calls=%async_computation.3 | async-start | bytes 786432 | tf_op jit(solution)/shard_map/all_to_all | solution.py:26
  1135.6 61.7 %all-to-all-start = ((bf16[8,96,3,192]{1,3,2,0:T(8,128)(2,1)}), bf16[8,96,3,192]{1,3,2,0:T(8,128)(2,1)}, u32[]{:S(2)}, u32[]{:S(2)}) async-start(bf16[8,96,3,192]{1,3,2,0:T(8,128)(2,1)} %copy.217), calls=%async_computation.2 | async-start | bytes 2359296 | tf_op jit(solution)/shard_map/all_to_all | solution.py:26
  1139.8 59.9 %copy-start.30 = (f32[768,768]{1,0:T(8,128)S(1)}, f32[768,768]{1,0:T(8,128)}, u32[]{:S(2)}) copy-start(f32[768,768]{1,0:T(8,128)} %copy-done.29) | copy-start | bytes 7077892
  1139.9 59.9 %copy-start.98 = (f32[768]{0:T(1024)S(1)}, f32[768]{0:T(1024)}, u32[]{:S(2)}) copy-start(f32[768]{0:T(1024)} %copy-done.97) | copy-start | bytes 9220
  (288 other events, 1506.7 us)
Sparse Core Ops, SparseCore 0:
  269.8 91.3 reduce-scatter.5
  511.2 87.7 all-gather.7
  1090.2 84.2 reduce-scatter.7
  1180.8 136.3 reduce-scatter.9
  1324.5 134.5 reduce-scatter.11
Sparse Core Ops, SparseCore 1:
  273.0 132.5 all-gather.3
  408.2 62.1 all-gather.5
where the time goes:
time: 1470 us
  matrix products  475 us (32%)
  waiting for transfers between devices  464 us (32%)
  other arithmetic  280 us (19%)
  blocking collectives  96.1 us (7%)
  local copies, waits for them, and re-layouts  95.3 us (6%)
  loops' own time  30 us (2%)
  between operations  19.2 us (1%)
    reduce_scatter x1, waiting for transfers between devices, body(): lax.psum_scatter(down_term, ('batch', 'heads'), scatter_dimension=0, tile...  142 us
    reduce_scatter x1, waiting for transfers between devices, body(): lax.psum_scatter(up_term, ('batch', 'heads'), scatter_dimension=1, tiled=...  114 us
    dot_general x9, matrix products, head_mix(): attended = jnp.dot(first_kernel, mixed_marks, precision=best_precision)  111 us
    reduce_sum x21, other arithmetic, head_mix(): conv_taps[tap_index] * padded_v[tap_index:tap_index + tok_count]  95.5 us
    all_gather x1, waiting for transfers between devices, body(): piece_rows = lax.all_gather(grad_attn_low, 'heads', axis=0, tiled=True)  87.8 us
    dot_general x288, matrix products, batch_mul(): jnp.einsum('...ij,...jk->...ik', left, right, precision=best_precision)  85.9 us
    broadcast_in_dim x3, other arithmetic, heads_mix(): lax.map(jax.checkpoint(one_head), (split_heads(q_all), split_heads(k_all)...  62.2 us
    psum x1, blocking collectives, body(): lax.psum((conv_full, bias_full, bound_total, live_count), ('batch', 'head...  49.4 us
  transfers between devices with their start and end apart: 9, of which 6 were waited for; matrix products, arithmetic and copies ran while one was open for 6% of the time, Pallas kernels for 0%

commit v1 on v0

v1 whole, which is shorter than its diff:
```python
from functools import partial

import jax
import jax.numpy as jnp
from jax import lax
from jax.experimental import pallas as pl
from jax.experimental.pallas import tpu as pltpu
from jax.sharding import PartitionSpec as P

HEAD_DIM = 64
PINV_ITERS = 6
TILE = 512
SUB = 128

f32 = jnp.float32
low = jnp.bfloat16
mask_fill = -1000000000.0


def split(x):
    high = x.astype(low)
    return high, (x - high.astype(f32)).astype(low)


def mul(a, b):
    return lax.dot_general(a, b, (((1,), (0,)), ((), ())), preferred_element_type=f32)


def mul_t(a, b):
    return lax.dot_general(a, b, (((1,), (1,)), ((), ())), preferred_element_type=f32)


def wide(form, left, right):
    left_high, left_low = split(left)
    right_high, right_low = split(right)
    return form(left_high, right_high) + (
        form(left_high, right_low) + form(left_low, right_high)
    )


def block_grid(rows, cols):
    row_block = lax.broadcasted_iota(jnp.int32, (rows, cols), 0) // HEAD_DIM
    col_block = lax.broadcasted_iota(jnp.int32, (rows, cols), 1) // HEAD_DIM
    return row_block == col_block


def spread(x, blocks):
    count = blocks.shape[0] // x.shape[0]
    return jnp.where(blocks, jnp.concatenate([x] * count, axis=0), jnp.zeros_like(x[:1, :1]))


def fold(x, blocks):
    kept = jnp.where(blocks, x, jnp.zeros_like(x[:1, :1]))
    rows = HEAD_DIM
    out = kept[:rows]
    for n in range(1, x.shape[0] // rows):
        out = out + kept[n * rows : (n + 1) * rows]
    return out


def pack_mul(left, right, blocks):
    left_high, left_low = split(left)
    right_high, right_low = split(right)
    right_high, right_low = spread_low(right_high, blocks), spread_low(right_low, blocks)
    return mul(left_high, right_high) + (mul(left_high, right_low) + mul(left_low, right_high))


def pack_mul_t(left, right, blocks):
    left_high, left_low = split(left)
    right_high, right_low = split(right)
    right_high, right_low = spread_low(right_high, blocks), spread_low(right_low, blocks)
    return mul_t(left_high, right_high) + (mul_t(left_high, right_low) + mul_t(left_low, right_high))


def spread_low(x, blocks):
    return spread(x.astype(f32), blocks).astype(low)


def slot_bounds(len_ref, s, slots):
    start = jnp.int32(0)
    for n in range(slots):
        start = start + jnp.where(n < s, len_ref[n], 0)
    return start, start + len_ref[s]


def eye_pack(width):
    row = lax.broadcasted_iota(jnp.int32, (HEAD_DIM, width), 0)
    col = lax.broadcasted_iota(jnp.int32, (HEAD_DIM, width), 1) % HEAD_DIM
    return jnp.where(row == col, 1.0, 0.0).astype(f32)


def lane_mask(start, end, at, width):
    tok = at + lax.broadcasted_iota(jnp.int32, (1, width), 1)
    return (tok >= start) & (tok < end)


def band(taps_row, width):
    row = lax.broadcasted_iota(jnp.int32, (SUB, 3 * SUB), 0)
    col = lax.broadcasted_iota(jnp.int32, (SUB, 3 * SUB), 1)
    off = col - row - (SUB - width // 2)
    out = jnp.zeros((SUB, 3 * SUB), f32)
    for n in range(width):
        out = jnp.where(off == n, taps_row[:, n : n + 1], out)
    return out


def slot_marks(len_ref, at, slots, marks, width):
    rows = slots * marks
    row = lax.broadcasted_iota(jnp.int32, (rows, 1), 0)
    slot = row // marks
    mark = row % marks
    start = jnp.zeros((rows, 1), jnp.int32)
    length = jnp.zeros((rows, 1), jnp.int32)
    for n in range(slots):
        start = start + jnp.where(slot > n, len_ref[n], 0)
        length = jnp.where(slot == n, len_ref[n], length)
    lower = start + (mark * length) // marks
    upper = start + ((mark + 1) * length) // marks
    inv_count = 1.0 / jnp.maximum((upper - lower).astype(f32), 1.0)
    tok = at + lax.broadcasted_iota(jnp.int32, (rows, width), 1)
    member = jnp.where((tok >= lower) & (tok < upper), 1.0, 0.0)
    return member, inv_count


def mix_forward_kernel(
    slots, marks, taps,
    len_ref, tok_ref, weight_ref, bias_ref, conv_ref,
    qkv_ref, first_ref, last_ref, mixed_ref, mark_ref, value_ref, inner_ref,
    denom_ref, middle_ref, steps_ref, inverse_ref, bound_ref,
    vpad, scores, vsum,
):
    step = pl.program_id(0)
    width = first_ref.shape[0]
    heads = width // HEAD_DIM
    tok_count = qkv_ref.shape[1]
    tiles = tok_count // TILE
    packed = slots * marks
    at = pl.multiple_of(step * TILE, TILE)

    @pl.when(step == 0)
    def _():
        mark_ref[...] = jnp.zeros_like(mark_ref)
        vsum[...] = jnp.zeros_like(vsum)
        vpad[:, :SUB] = jnp.zeros((width, SUB), low)
        vpad[:, tok_count + SUB :] = jnp.zeros((width, SUB), low)

    rows = (mul_t(weight_ref[...], tok_ref[...]) + bias_ref[...]).astype(low)
    qkv_ref[:, pl.ds(at, TILE)] = rows
    vpad[:, pl.ds(pl.multiple_of(at + SUB, SUB), TILE)] = rows[2 * width :]
    member, inv_count = slot_marks(len_ref, at, slots, marks, TILE)
    mark_ref[...] += mul_t(member.astype(low), rows[: 2 * width])
    vsum[...] += mul_t(jnp.ones((8, TILE), low), rows[2 * width :])
    first_ref[:, pl.ds(at, TILE)] = jnp.zeros((width, TILE), low)
    last_ref[:, pl.ds(at, TILE)] = jnp.zeros((width, TILE), low)
    mixed_ref[:, pl.ds(at, TILE)] = jnp.zeros((width, TILE), low)

    @pl.when(step == tiles - 1)
    def _():
        mark_ref[...] = mark_ref[...] * inv_count
        head_blocks = block_grid(width, width)
        slot_blocks = block_grid(packed, packed)
        eye = eye_pack(packed)
        scale = HEAD_DIM ** -0.5

        middles, inverses_t, products = [], [], []
        bound_total = jnp.zeros((1, 1), f32)
        lane_slot = lax.broadcasted_iota(jnp.int32, (1, packed), 1) // marks
        for h in range(heads):
            q_marks = mark_ref[:, h * HEAD_DIM : (h + 1) * HEAD_DIM]
            k_marks = mark_ref[:, width + h * HEAD_DIM : width + (h + 1) * HEAD_DIM]
            sim = wide(mul_t, q_marks, k_marks) * scale
            sim = jnp.where(slot_blocks, sim, -1e30)
            sim = jnp.exp(sim - jnp.max(sim, axis=1, keepdims=True))
            sim = sim / jnp.sum(sim, axis=1, keepdims=True)
            middle = fold(sim, slot_blocks)
            col_sums = jnp.sum(middle, axis=0, keepdims=True)
            bound = jnp.zeros((1, packed), f32)
            for s in range(slots):
                top = jnp.max(jnp.where(lane_slot == s, col_sums, 0.0), axis=1, keepdims=True)
                bound = jnp.where(lane_slot == s, top, bound)
                bound_total += jnp.where(len_ref[s] > 0, top, 0.0)
            middle_ref[h] = middle
            middles.append(middle)
            inverses_t.append(middle / bound)
            products.append(pack_mul_t(middle, middle, slot_blocks) / bound)
        bound_ref[...] = jnp.broadcast_to(bound_total, bound_ref.shape)

        def newton(n, carry):
            out = []
            for h in range(heads):
                inverse_t, product = carry[h]
                square = pack_mul(product, product, slot_blocks)
                cube = pack_mul(product, square, slot_blocks)
                fourth = pack_mul(square, square, slot_blocks)
                second = 15.0 * eye - 7.0 * product + square
                third = 13.0 * eye - 15.0 * product + 7.0 * square - cube
                steps_ref[n, 0, h] = product
                steps_ref[n, 1, h] = second
                steps_ref[n, 2, h] = third
                steps_ref[n, 3, h] = inverse_t
                out.append(
                    (
                        0.25 * pack_mul(third, inverse_t, slot_blocks),
                        0.25 * (13.0 * product - 15.0 * square + 7.0 * cube - fourth),
                    )
                )
            return tuple(out)

        final = lax.fori_loop(0, PINV_ITERS, newton, tuple(zip(inverses_t, products)))
        for h in range(heads):
            inverse_ref[h] = final[h][0]

        def one_slot(s, _):
            start, end = slot_bounds(len_ref, s, slots)
            lo, hi = start // TILE, (end + TILE - 1) // TILE
            hi = jnp.where(end > start, hi, lo)
            own = mark_ref[pl.ds(pl.multiple_of(s * marks, marks), marks), :] * scale
            q_block = spread(own[:, :width], head_blocks).astype(low)
            k_block = spread(own[:, width:], head_blocks).astype(low)

            def score_tile(n, top):
                t = pl.multiple_of(n * TILE, TILE)
                mask = lane_mask(start, end, t, TILE)
                sim = mul(k_block, qkv_ref[:width, pl.ds(t, TILE)])
                sim = sim.reshape(heads, marks, TILE)
                sim = jnp.exp(sim - jnp.max(sim, axis=1, keepdims=True))
                sim = sim / jnp.sum(sim, axis=1, keepdims=True)
                sim = sim.reshape(width, TILE)
                old = first_ref[:, pl.ds(t, TILE)].astype(f32)
                first_ref[:, pl.ds(t, TILE)] = jnp.where(mask, sim, old).astype(low)
                sim = mul(q_block, qkv_ref[width : 2 * width, pl.ds(t, TILE)])
                sim = jnp.where(mask, sim, mask_fill)
                scores[:, pl.ds(t, TILE)] = sim
                for c in range(TILE // SUB):
                    top = jnp.maximum(top, sim[:, c * SUB : (c + 1) * SUB])
                return top

            top = lax.fori_loop(lo, hi, score_tile, jnp.full((width, SUB), mask_fill, f32))
            top = jnp.max(top, axis=1, keepdims=True)

            def value_tile(n, carry):
                denom, total = carry
                t = pl.multiple_of(n * TILE, TILE)
                mask = lane_mask(start, end, t, TILE)
                part = jnp.exp(scores[:, pl.ds(t, TILE)] - top)
                old = last_ref[:, pl.ds(t, TILE)].astype(f32)
                last_ref[:, pl.ds(t, TILE)] = jnp.where(mask, part, old).astype(low)
                total = total + mul_t(part.astype(low), qkv_ref[2 * width :, pl.ds(t, TILE)])
                for c in range(TILE // SUB):
                    denom = denom + part[:, c * SUB : (c + 1) * SUB]
                return denom, total

            denom, total = lax.fori_loop(
                lo, hi, value_tile,
                (jnp.zeros((width, SUB), f32), jnp.zeros((width, width), f32)),
            )
            denom = jnp.sum(denom, axis=1, keepdims=True)
            inv = 1.0 / jnp.where(denom > 0.0, denom, 1.0)
            denom_ref[s] = inv
            values = fold(total * inv, head_blocks)
            values = jnp.where(end > start, values, vsum[:1] / tok_count)
            value_ref[pl.ds(pl.multiple_of(s * marks, marks), marks), :] = values
            return 0

        lax.fori_loop(0, slots, one_slot, 0)

        lane_head = lax.broadcasted_iota(jnp.int32, (1, width), 1) // HEAD_DIM
        inner = jnp.zeros((packed, width), f32)
        for h in range(heads):
            inverse = pack_mul_t(eye, final[h][0], slot_blocks)
            own_values = jnp.where(lane_head == h, value_ref[...], 0.0)
            inner = inner + wide(mul, spread(inverse, slot_blocks), own_values)
        inner_ref[...] = inner

        bands = [band(conv_ref[h : h + 1, :], taps).astype(low) for h in range(heads)]

        def out_slot(s, _):
            start, end = slot_bounds(len_ref, s, slots)
            lo, hi = start // TILE, (end + TILE - 1) // TILE
            hi = jnp.where(end > start, hi, lo)
            own = inner_ref[pl.ds(pl.multiple_of(s * marks, marks), marks), :]
            a_block = jnp.transpose(spread(own, head_blocks)).astype(low)

            def out_tile(n, _):
                t = pl.multiple_of(n * TILE, TILE)
                mask = lane_mask(start, end, t, TILE)
                rows = mul(a_block, first_ref[:, pl.ds(t, TILE)])
                rows = rows + convolve(vpad, bands, start, end, t, heads)
                old = mixed_ref[:, pl.ds(t, TILE)].astype(f32)
                mixed_ref[:, pl.ds(t, TILE)] = jnp.where(mask, rows, old).astype(low)
                return 0

            return lax.fori_loop(lo, hi, out_tile, 0)

        lax.fori_loop(0, slots, out_slot, 0)


def windows(padded, start, end, t):
    full = padded[:, pl.ds(t, TILE + 2 * SUB)]
    keep = lane_mask(start, end, t - SUB, TILE + 2 * SUB)
    return jnp.where(keep, full.astype(f32), 0.0).astype(low)


def convolve(padded, bands, start, end, t, heads):
    full = windows(padded, start, end, t)
    out = []
    count = TILE // SUB
    for h in range(heads):
        own = full[h * HEAD_DIM : (h + 1) * HEAD_DIM]
        stack = jnp.concatenate(
            [own[:, c * SUB : (c + 3) * SUB] for c in range(count)], axis=0
        )
        res = mul_t(stack, bands[h])
        out.append(
            jnp.concatenate(
                [res[c * HEAD_DIM : (c + 1) * HEAD_DIM] for c in range(count)], axis=1
            )
        )
    return jnp.concatenate(out, axis=0)


def mix_backward_kernel(
    slots, marks, taps,
    len_ref, grad_ref, qkv_ref, first_ref, last_ref, mark_ref, value_ref, inner_ref,
    denom_ref, middle_ref, steps_ref, inverse_ref, conv_ref,
    out_ref, bias_ref, conv_out_ref,
    gpad, vpad, ds_first, ds_last, conv_grad, d_inner, d_k, d_q, d_value,
):
    width = first_ref.shape[0]
    heads = width // HEAD_DIM
    tok_count = qkv_ref.shape[1]
    packed = slots * marks
    scale = HEAD_DIM ** -0.5
    head_blocks = block_grid(width, width)
    slot_blocks = block_grid(packed, packed)
    eye = eye_pack(packed)
    count = TILE // SUB

    for padded, source in ((gpad, grad_ref[...]), (vpad, qkv_ref[2 * width :, :])):
        padded[:, :SUB] = jnp.zeros((width, SUB), low)
        padded[:, tok_count + SUB :] = jnp.zeros((width, SUB), low)
        padded[:, SUB : tok_count + SUB] = source
    out_ref[...] = jnp.zeros_like(out_ref)
    ds_first[...] = jnp.zeros_like(ds_first)
    ds_last[...] = jnp.zeros_like(ds_last)
    conv_grad[...] = jnp.zeros_like(conv_grad)

    def reach(s):
        start, end = slot_bounds(len_ref, s, slots)
        lo, hi = start // TILE, (end + TILE - 1) // TILE
        return start, end, lo, jnp.where(end > start, hi, lo)

    def own_rows(s):
        return pl.ds(pl.multiple_of(s * marks, marks), marks)

    def first_slot(s, _):
        start, end, lo, hi = reach(s)
        a_block = spread(inner_ref[own_rows(s), :], head_blocks).astype(low)

        def tile(n, carry):
            inner_total, key_total = carry
            t = pl.multiple_of(n * TILE, TILE)
            mask = lane_mask(start, end, t, TILE)
            own_grad = grad_ref[:, pl.ds(t, TILE)]
            kernel_rows = jnp.where(mask, first_ref[:, pl.ds(t, TILE)].astype(f32), 0.0)
            d_kernel = mul(a_block, own_grad)
            prod = (kernel_rows * d_kernel).reshape(heads, marks, TILE)
            row_sum = jnp.sum(prod, axis=1, keepdims=True)
            d_sim = prod - kernel_rows.reshape(heads, marks, TILE) * row_sum
            d_sim = d_sim.reshape(width, TILE)
            d_sim_low = d_sim.astype(low)
            old = ds_first[:, pl.ds(t, TILE)].astype(f32)
            ds_first[:, pl.ds(t, TILE)] = jnp.where(mask, d_sim, old).astype(low)
            inner_total = inner_total + mul_t(kernel_rows.astype(low), own_grad)
            key_total = key_total + mul_t(d_sim_low, qkv_ref[:width, pl.ds(t, TILE)])
            full = windows(vpad, start, end, t)
            grad_own = jnp.where(mask, own_grad.astype(f32), 0.0).astype(low)
            for h in range(heads):
                sel = slice(h * HEAD_DIM, (h + 1) * HEAD_DIM)
                left = jnp.concatenate(
                    [grad_own[sel, c * SUB : (c + 1) * SUB] for c in range(count)], axis=0
                )
                right = jnp.concatenate(
                    [full[sel, c * SUB : (c + 3) * SUB] for c in range(count)], axis=0
                )
                conv_grad[h] += lax.dot_general(
                    left, right, (((0,), (0,)), ((), ())), preferred_element_type=f32
                )
            return inner_total, key_total

        zero = jnp.zeros((width, width), f32)
        inner_total, key_total = lax.fori_loop(lo, hi, tile, (zero, zero))
        d_inner[own_rows(s), :] = fold(inner_total, head_blocks)
        d_k[own_rows(s), :] = fold(key_total, head_blocks) * scale
        return 0

    lax.fori_loop(0, slots, first_slot, 0)

    row = lax.broadcasted_iota(jnp.int32, (SUB, 3 * SUB), 0)
    col = lax.broadcasted_iota(jnp.int32, (SUB, 3 * SUB), 1)
    off = col - row - (SUB - taps // 2)
    tap_lane = lax.broadcasted_iota(jnp.int32, (1, SUB), 1)
    for h in range(heads):
        found = jnp.zeros((1, SUB), f32)
        square = conv_grad[h]
        for n in range(taps):
            part = jnp.sum(jnp.where(off == n, square, 0.0), axis=0, keepdims=True)
            part = jnp.sum(part, axis=1, keepdims=True)
            found = jnp.where(tap_lane == n, part, found)
        conv_out_ref[h : h + 1, :] = found

    lane_head = lax.broadcasted_iota(jnp.int32, (1, width), 1) // HEAD_DIM
    value_total = jnp.zeros((packed, width), f32)
    d_inverses = []
    for h in range(heads):
        own = jnp.where(lane_head == h, d_inner[...], 0.0)
        value_total = value_total + wide(mul, spread(inverse_ref[h], slot_blocks), own)
        d_inverses.append(fold(wide(mul_t, own, value_ref[...]), slot_blocks))
    d_value[...] = value_total

    middles_t = [pack_mul_t(eye, middle_ref[h], slot_blocks) for h in range(heads)]

    def newton(k, carry):
        n = PINV_ITERS - 1 - k
        out = []
        for h in range(heads):
            d_inverse, d_middle = carry[h]
            product = steps_ref[n, 0, h]
            second = steps_ref[n, 1, h]
            third = steps_ref[n, 2, h]
            inverse_t = steps_ref[n, 3, h]
            middle_t = middles_t[h]
            d_third = 0.25 * pack_mul(inverse_t, d_inverse, slot_blocks)
            d_second = -pack_mul(product, d_third, slot_blocks)
            d_first = -pack_mul(product, d_second, slot_blocks)
            d_product = (
                -pack_mul(d_third, second, slot_blocks)
                - pack_mul(d_second, 7.0 * eye - product, slot_blocks)
                - d_first
            )
            d_middle = d_middle + pack_mul(d_product, inverse_t, slot_blocks)
            d_inverse = 0.25 * pack_mul(d_inverse, third, slot_blocks) + pack_mul(
                middle_t, d_product, slot_blocks
            )
            out.append((d_inverse, d_middle))
        return tuple(out)

    zero = jnp.zeros((HEAD_DIM, packed), f32)
    final = lax.fori_loop(0, PINV_ITERS, newton, tuple((x, zero) for x in d_inverses))
    lane_slot = lax.broadcasted_iota(jnp.int32, (1, packed), 1) // marks
    dq_total = jnp.zeros((packed, width), f32)
    dk_total = jnp.zeros((packed, width), f32)
    for h in range(heads):
        d_inverse, d_middle = final[h]
        middle = middle_ref[h]
        first_t = steps_ref[0, 3, h]
        d_inverse_t = pack_mul_t(eye, d_inverse, slot_blocks)
        col_sums = jnp.sum(middle, axis=0, keepdims=True)
        share = jnp.sum(d_inverse_t * first_t, axis=0, keepdims=True)
        bound = jnp.zeros((1, packed), f32)
        d_bound = jnp.zeros((1, packed), f32)
        hits = jnp.zeros((1, packed), f32)
        for s in range(slots):
            mine = lane_slot == s
            top = jnp.max(jnp.where(mine, col_sums, 0.0), axis=1, keepdims=True)
            total = jnp.sum(jnp.where(mine, share, 0.0), axis=1, keepdims=True)
            number = jnp.sum(
                jnp.where(mine & (col_sums == top), 1.0, 0.0), axis=1, keepdims=True
            )
            bound = jnp.where(mine, top, bound)
            d_bound = jnp.where(mine, -total / top, d_bound)
            hits = jnp.where(mine, number, hits)
        d_middle = d_middle + d_inverse_t / bound
        d_middle = d_middle + jnp.where(col_sums == bound, d_bound / hits, 0.0)
        prod = spread(middle * d_middle, slot_blocks)
        d_sim = prod - spread(middle, slot_blocks) * jnp.sum(prod, axis=1, keepdims=True)
        d_sim = d_sim * scale
        own = lane_head == h
        q_marks = jnp.where(own, mark_ref[:, :width], 0.0)
        k_marks = jnp.where(own, mark_ref[:, width:], 0.0)
        dq_total = dq_total + wide(mul, d_sim, k_marks)
        dk_total = dk_total + wide(mul, jnp.transpose(d_sim), q_marks)
    d_q[...] = dq_total
    d_k[...] += dk_total

    flipped = []
    for h in range(heads):
        flipped.append(
            band(
                jnp.concatenate(
                    [conv_ref[h : h + 1, n : n + 1] for n in reversed(range(taps))], axis=1
                ),
                taps,
            ).astype(low)
        )

    def last_slot(s, _):
        start, end, lo, hi = reach(s)
        inv = denom_ref[s]
        own_d = d_value[own_rows(s), :]
        own_v = value_ref[own_rows(s), :]
        d_block = spread(own_d, head_blocks)
        row_sum = jnp.sum(
            d_block * jnp.concatenate([own_v] * heads, axis=0), axis=1, keepdims=True
        )
        row_sum = row_sum * inv
        d_block = d_block * inv
        d_block_t = jnp.transpose(d_block).astype(low)
        d_block = d_block.astype(low)

        def tile(n, query_total):
            t = pl.multiple_of(n * TILE, TILE)
            mask = lane_mask(start, end, t, TILE)
            kernel_rows = jnp.where(mask, last_ref[:, pl.ds(t, TILE)].astype(f32), 0.0)
            v_rows = qkv_ref[2 * width :, pl.ds(t, TILE)]
            d_sim = kernel_rows * (mul(d_block, v_rows) - row_sum)
            d_low = d_sim.astype(low)
            old = ds_last[:, pl.ds(t, TILE)].astype(f32)
            ds_last[:, pl.ds(t, TILE)] = jnp.where(mask, d_sim, old).astype(low)
            dv = mul(d_block_t, kernel_rows.astype(low))
            dv = dv + convolve(gpad, flipped, start, end, t, heads)
            old = out_ref[2 * width :, pl.ds(t, TILE)].astype(f32)
            out_ref[2 * width :, pl.ds(t, TILE)] = jnp.where(mask, dv, old).astype(low)
            return query_total + mul_t(d_low, qkv_ref[width : 2 * width, pl.ds(t, TILE)])

        query_total = lax.fori_loop(lo, hi, tile, jnp.zeros((width, width), f32))
        d_q[own_rows(s), :] += fold(query_total, head_blocks) * scale
        return 0

    lax.fori_loop(0, slots, last_slot, 0)

    inv_count = slot_marks(len_ref, 0, slots, marks, SUB)[1]
    d_q[...] = d_q[...] * inv_count
    d_k[...] = d_k[...] * inv_count

    def final_slot(s, _):
        start, end, lo, hi = reach(s)
        length = end - start
        own = mark_ref[own_rows(s), :] * scale

        def left(block, d_mark):
            wide_rows = jnp.concatenate([spread(block, head_blocks), d_mark], axis=0)
            return jnp.transpose(wide_rows).astype(low)

        q_left = left(own[:, width:], d_q[own_rows(s), :])
        k_left = left(own[:, :width], d_k[own_rows(s), :])
        mark = lax.broadcasted_iota(jnp.int32, (marks, 1), 0)
        lower = start + (mark * length) // marks
        upper = start + ((mark + 1) * length) // marks

        def tile(n, _):
            t = pl.multiple_of(n * TILE, TILE)
            mask = lane_mask(start, end, t, TILE)
            tok = t + lax.broadcasted_iota(jnp.int32, (marks, TILE), 1)
            member = jnp.where((tok >= lower) & (tok < upper), 1.0, 0.0).astype(low)
            for at, lhs, source in ((0, q_left, ds_first), (width, k_left, ds_last)):
                rhs = jnp.concatenate([source[:, pl.ds(t, TILE)], member], axis=0)
                rows = mul(lhs, rhs)
                old = out_ref[at : at + width, pl.ds(t, TILE)].astype(f32)
                out_ref[at : at + width, pl.ds(t, TILE)] = jnp.where(mask, rows, old).astype(low)
            return 0

        return lax.fori_loop(lo, hi, tile, 0)

    lax.fori_loop(0, slots, final_slot, 0)

    def bias_tile(n, carry):
        t = pl.multiple_of(n * TILE, TILE)
        q_sum, v_sum = carry
        q_rows = out_ref[:width, pl.ds(t, TILE)].astype(f32)
        v_rows = out_ref[2 * width :, pl.ds(t, TILE)].astype(f32)
        for c in range(count):
            q_sum = q_sum + q_rows[:, c * SUB : (c + 1) * SUB]
            v_sum = v_sum + v_rows[:, c * SUB : (c + 1) * SUB]
        return q_sum, v_sum

    zero = jnp.zeros((width, SUB), f32)
    q_sum, v_sum = lax.fori_loop(0, tok_count // TILE, bias_tile, (zero, zero))
    bias_ref[:, 0:1] = jnp.sum(q_sum, axis=1, keepdims=True)
    bias_ref[:, 1:2] = jnp.sum(v_sum, axis=1, keepdims=True)


def mix_forward(seq_lengths, tokens, weight_t, bias_col, conv_own, slots, marks):
    tok_count, model = tokens.shape
    width = weight_t.shape[0] // 3
    heads = width // HEAD_DIM
    packed = slots * marks
    taps = conv_own.shape[1]
    whole = lambda *shape: pl.BlockSpec(shape, lambda i, lens: (0,) * len(shape))
    shapes = [
        ((3 * width, tok_count), low),
        ((width, tok_count), low),
        ((width, tok_count), low),
        ((width, tok_count), low),
        ((packed, 2 * width), f32),
        ((packed, width), f32),
        ((packed, width), f32),
        ((slots, width, 1), f32),
        ((heads, HEAD_DIM, packed), f32),
        ((PINV_ITERS, 4, heads, HEAD_DIM, packed), f32),
        ((heads, HEAD_DIM, packed), f32),
        ((8, 128), f32),
    ]
    return pl.pallas_call(
        partial(mix_forward_kernel, slots, marks, taps),
        out_shape=[jax.ShapeDtypeStruct(s, t) for s, t in shapes],
        grid_spec=pltpu.PrefetchScalarGridSpec(
            num_scalar_prefetch=1,
            grid=(tok_count // TILE,),
            in_specs=[
                pl.BlockSpec((TILE, model), lambda i, lens: (i, 0)),
                whole(3 * width, model),
                whole(3 * width, 1),
                whole(heads, taps),
            ],
            out_specs=[whole(*s) for s, _ in shapes],
            scratch_shapes=[
                pltpu.VMEM((width, tok_count + 2 * SUB), low),
                pltpu.VMEM((width, tok_count), f32),
                pltpu.VMEM((8, width), f32),
            ],
        ),
        compiler_params=pltpu.CompilerParams(vmem_limit_bytes=56 * 1024 * 1024),
        name="mix_forward",
    )(seq_lengths, tokens, weight_t, bias_col, conv_own)


def mix_backward(seq_lengths, grad_t, saved, conv_own, slots, marks):
    qkv_t, first, last, mark, value, inner, denom, middle, steps, inverse = saved
    width, tok_count = grad_t.shape
    heads = width // HEAD_DIM
    packed = slots * marks
    taps = conv_own.shape[1]
    args = (grad_t, qkv_t, first, last, mark, value, inner, denom, middle, steps, inverse, conv_own)
    whole = lambda shape: pl.BlockSpec(
        shape, lambda i, lens: (0,) * len(shape), pipeline_mode=pl.Buffered(1)
    )
    shapes = [((3 * width, tok_count), low), ((width, 2), f32), ((heads, SUB), f32)]
    square = pltpu.VMEM((packed, width), f32)
    return pl.pallas_call(
        partial(mix_backward_kernel, slots, marks, taps),
        out_shape=[jax.ShapeDtypeStruct(s, t) for s, t in shapes],
        grid_spec=pltpu.PrefetchScalarGridSpec(
            num_scalar_prefetch=1,
            grid=(1,),
            in_specs=[whole(x.shape) for x in args],
            out_specs=[whole(s) for s, _ in shapes],
            scratch_shapes=[
                pltpu.VMEM((width, tok_count + 2 * SUB), low),
                pltpu.VMEM((width, tok_count + 2 * SUB), low),
                pltpu.VMEM((width, tok_count), low),
                pltpu.VMEM((width, tok_count), low),
                pltpu.VMEM((heads, SUB, 3 * SUB), f32),
                square, square, square, square,
            ],
        ),
        compiler_params=pltpu.CompilerParams(vmem_limit_bytes=56 * 1024 * 1024),
        name="mix_backward",
    )(seq_lengths, *args)


contract_rows = (((0,), (0,)), ((), ()))
contract_cols = (((1,), (1,)), ((), ()))
norm_eps = 1e-05


def split_up(x, dim, peers):
    before, after = (x.shape[:dim], x.shape[dim + 1 :])
    return jnp.moveaxis(x.reshape(*before, peers, -1, *after), dim, 0)


def sum_at_owner(x, axis, dim):
    peers = lax.axis_size(axis)
    tiles = lax.all_to_all(split_up(x, dim, peers), axis, 0, 0, tiled=True)
    return jnp.sum(tiles.astype(f32), axis=0)


def layer_norm(row_data, gain_vec, shift_vec):
    centre = row_data - jnp.mean(row_data, axis=1, keepdims=True)
    spread_row = jnp.mean(centre * centre, axis=1, keepdims=True)
    return centre * lax.rsqrt(spread_row + norm_eps) * gain_vec[None, :] + shift_vec[None, :]


def gelu_exact(values):
    return jax.nn.gelu(values, approximate=False)


def body(
    tokens,
    qkv_weight,
    qv_bias,
    conv_weight,
    out_weight,
    out_bias,
    norm1_gain,
    norm1_bias,
    ffn_in_weight,
    ffn_in_bias,
    ffn_out_weight,
    ffn_out_bias,
    norm2_gain,
    norm2_bias,
    cotangent,
    seq_lengths,
    segment_ids,
    landmark_bounds,
):
    tok_count, model_width = tokens.shape
    head_width = qkv_weight.shape[2]
    heads_here = head_width // HEAD_DIM
    head_total = conv_weight.shape[0]
    kernel_taps = conv_weight.shape[1]
    slots, marks = landmark_bounds.shape
    quarter = tok_count // lax.axis_size("heads")
    head_index = lax.axis_index("heads")
    own_start = head_index * quarter
    both = ("batch", "heads")
    own_rows_low = lax.dynamic_slice_in_dim(tokens, own_start, quarter, 0)
    own_tokens = own_rows_low.astype(f32)
    conv_own = lax.dynamic_slice_in_dim(conv_weight, head_index * heads_here, heads_here, 0)
    qv_own = lax.dynamic_slice_in_dim(qv_bias, head_index * head_width, head_width, 1)
    flat_qkv = qkv_weight.reshape(model_width, 3 * head_width)
    bias_col = jnp.concatenate([qv_own[0], jnp.zeros_like(qv_own[0]), qv_own[1]])[:, None]
    forward = mix_forward(
        seq_lengths, tokens, jnp.transpose(flat_qkv), bias_col, conv_own, slots, marks
    )
    qkv_t, first, last, mixed_t, mark, value, inner, denom, middle, steps, inverse, bound = forward
    bound_total = bound[0, 0]
    attn_part = lax.psum_scatter(
        lax.dot_general(mixed_t, out_weight, contract_rows, preferred_element_type=f32).astype(low),
        "heads",
        scatter_dimension=0,
        tiled=True,
    ).astype(f32)
    live_count = jnp.sum((seq_lengths > 0).astype(f32)) * heads_here
    first_res = own_tokens + attn_part + out_bias[None, :]
    norm1_out, norm1_pull = jax.vjp(layer_norm, first_res, norm1_gain, norm1_bias)
    norm1_low = norm1_out.astype(low)
    ff_own = ffn_out_weight.shape[0]
    bias_row = jnp.zeros((16, model_width), low).at[0, :ff_own].set(ffn_in_bias)
    whole_in = lax.all_gather(ffn_in_weight, both, axis=1, tiled=True)
    out_pack = lax.all_gather(jnp.concatenate([ffn_out_weight, bias_row], axis=0), both, axis=0)
    whole_out = out_pack[:, :ff_own].reshape(-1, model_width)
    whole_in_bias = out_pack[:, ff_own, :ff_own].reshape(-1)
    pre_act = (
        jnp.dot(norm1_low, whole_in, preferred_element_type=f32)
        + whole_in_bias.astype(f32)[None, :]
    )
    hidden_act, gelu_pull = jax.vjp(gelu_exact, pre_act)
    hidden_low = hidden_act.astype(low)
    ffn_result = jnp.dot(hidden_low, whole_out, preferred_element_type=f32) + ffn_out_bias[None, :]
    final_out, norm2_pull = jax.vjp(layer_norm, norm1_out + ffn_result, norm2_gain, norm2_bias)
    grad_second, grad_gain_two, grad_shift_two = norm2_pull(cotangent.astype(f32))
    grad_ffn_low = grad_second.astype(low)
    grad_ffn_bias = jnp.sum(grad_ffn_low.astype(f32), axis=0)
    down_term = lax.dot_general(
        hidden_low, grad_ffn_low, contract_rows, preferred_element_type=f32
    ).astype(low)
    grad_hidden = lax.dot_general(
        grad_ffn_low, whole_out, contract_cols, preferred_element_type=f32
    )
    grad_pre = gelu_pull(grad_hidden)[0].astype(low)
    grad_in_bias = jnp.sum(grad_pre.astype(f32), axis=0)
    up_term = lax.dot_general(
        norm1_low, grad_pre, contract_rows, preferred_element_type=f32
    ).astype(low)
    grad_norm1 = grad_second + lax.dot_general(
        grad_pre, whole_in, contract_cols, preferred_element_type=f32
    )
    grad_first, grad_gain_one, grad_shift_one = norm1_pull(grad_norm1)
    grad_attn_low = grad_first.astype(low)
    grad_out_bias = jnp.sum(grad_attn_low.astype(f32), axis=0)
    piece_rows = lax.all_gather(grad_attn_low, "heads", axis=0, tiled=True)
    grad_mix_t = lax.dot_general(
        out_weight, piece_rows, contract_cols, preferred_element_type=f32
    ).astype(low)
    grad_mix_t, down_term, up_term = lax.optimization_barrier((grad_mix_t, down_term, up_term))
    up_share = lax.psum_scatter(up_term, both, scatter_dimension=1, tiled=True).astype(f32)
    down_share = lax.psum_scatter(down_term, both, scatter_dimension=0, tiled=True).astype(f32)
    saved = (qkv_t, first, last, mark, value, inner, denom, middle, steps, inverse)
    grad_t, grad_bias, grad_conv = mix_backward(
        seq_lengths, grad_mix_t, saved, conv_own, slots, marks
    )
    out_part = lax.dot_general(
        mixed_t, piece_rows, (((1,), (0,)), ((), ())), preferred_element_type=f32
    )
    grad_qv_own = jnp.transpose(grad_bias)
    qkv_part = lax.dot_general(
        tokens, grad_t, (((0,), (1,)), ((), ())), preferred_element_type=f32
    ).reshape(model_width, 3, head_width)
    input_part = lax.psum_scatter(
        lax.dot_general(
            grad_t, flat_qkv, (((0,), (1,)), ((), ())), preferred_element_type=f32
        ).astype(low),
        "heads",
        scatter_dimension=0,
        tiled=True,
    ).astype(f32)
    input_grad = grad_first + input_part
    conv_full = lax.dynamic_update_slice_in_dim(
        jnp.zeros((head_total, kernel_taps), f32),
        grad_conv[:, :kernel_taps],
        head_index * heads_here,
        0,
    )
    bias_full = lax.dynamic_update_slice_in_dim(
        jnp.zeros((2, head_total * HEAD_DIM), f32), grad_qv_own, head_index * head_width, 1
    )
    qkv_share, out_share = (
        sum_at_owner(qkv_part.astype(low), "batch", 0),
        sum_at_owner(out_part.astype(low), "batch", 1),
    )
    vector_all = jnp.stack(
        [grad_ffn_bias, grad_gain_two, grad_shift_two, grad_gain_one, grad_shift_one, grad_out_bias]
    )
    in_bias_share, vector_share = (
        lax.psum_scatter(grad_in_bias, both, scatter_dimension=0, tiled=True),
        lax.psum_scatter(vector_all, both, scatter_dimension=1, tiled=True),
    )
    conv_sum, bias_sum, bound_all, count_all = lax.psum(
        (conv_full, bias_full, bound_total, live_count), both
    )
    conv_out = lax.dynamic_slice_in_dim(conv_sum, head_index * heads_here, heads_here, 0)
    bias_out = lax.dynamic_slice_in_dim(bias_sum, head_index * head_width, head_width, 1)
    condition = bound_all / count_all
    return (
        final_out.astype(low),
        input_grad,
        qkv_share,
        bias_out,
        conv_out,
        out_share,
        up_share,
        in_bias_share,
        down_share,
        vector_share,
        condition,
    )


def solution(mesh):
    in_specs = (
        P("batch", None),
        P(None, None, "heads"),
        P(),
        P(),
        P("heads", None),
        P(),
        P(),
        P(),
        P(None, ("batch", "heads")),
        P(("batch", "heads")),
        P(("batch", "heads"), None),
        P(),
        P(),
        P(),
        P(("batch", "heads"), None),
        P("batch"),
        P("batch"),
        P("batch", None),
    )
    out_specs = (
        P(("batch", "heads"), None),
        P(("batch", "heads"), None),
        P("batch", None, "heads"),
        P(None, "heads"),
        P("heads", None),
        P("heads", "batch"),
        P(None, ("batch", "heads")),
        P(("batch", "heads")),
        P(("batch", "heads"), None),
        P(None, ("batch", "heads")),
        P(),
    )
    return jax.shard_map(body, mesh=mesh, in_specs=in_specs, out_specs=out_specs, check_vma=False)
```

time: 1470 us -> 749 us (0.51)
  matrix products: 475 us -> 102 us
  other arithmetic: 280 us -> 19.5 us
  Pallas kernels: 0 us -> 69.7 us
  local copies, waits for them, and re-layouts: 95.3 us -> 32.5 us
  blocking collectives: 96.1 us -> 50 us
  loops' own time: 30 us -> 0 us
  waiting for transfers between devices: 464 us -> 440 us
    dot_general x383 -> x7, matrix products: 434 us -> 63.2 us  [the longest x1 28.3 us: body(): jnp.dot(norm1_low, whole_in, preferred_element_type=f32)]
    reduce_sum x59 -> x8, other arithmetic: 123 us -> 7.73 us  [the longest x2 2.31 us: layer_norm(): spread_row = jnp.mean(centre * centre, axis=1, keepdims=True)]
    pallas_call x0 -> x2, Pallas kernels: none -> 69.7 us  [the longest x1 37.7 us: mix_backward(): pl.pallas_call(partial(mix_backward_kernel, slots, marks, taps), out_shap...]
    broadcast_in_dim x4 -> x0, other arithmetic: 64.2 us -> none  [the longest x3 62.2 us: heads_mix(): lax.map(jax.checkpoint(one_head), (split_heads(q_all), split_heads(k_all)...]
    unnamed x1 -> x0, blocking collectives: 46.6 us -> none
    mul x15 -> x0, other arithmetic: 37.6 us -> none  [the longest x6 37.4 us: head_mix(): conv_taps[tap_index] * padded_v[tap_index:tap_index + tok_count]]
    reduce_scatter x4 -> x3, waiting for transfers between devices: 300 us -> 267 us  [the longest x1 94.4 us: body(): lax.psum_scatter(down_term, both, scatter_dimension=0, tiled=True)]
    another operation x2 -> x0, loops' own time: 30 us -> none  [heads_mix(): lax.map(jax.checkpoint(one_head), (split_heads(q_all), split_heads(k_all)...]
  transfers between devices with their start and end apart: 9 -> 9, of which waited for: 6 -> 6; matrix products, arithmetic and copies ran while one was open for 6% -> 9% of each run, Pallas kernels for 0% -> 5%
where the time goes in v1:
time: 749 us; the launch traced here: 742 us
  waiting for transfers between devices  440 us (59%)
  matrix products  102 us (14%)
  Pallas kernels  69.7 us (9%)
  blocking collectives  50 us (7%)
  local copies, waits for them, and re-layouts  32.5 us (4%)
  other arithmetic  19.5 us (3%)
  between operations  19.4 us (3%)
  starting transfers between devices  8.8 us (1%)
    reduce_scatter x1, waiting for transfers between devices, body(): lax.psum_scatter(down_term, both, scatter_dimension=0, tiled=True)  94.4 us
    reduce_scatter x1, waiting for transfers between devices, body(): lax.psum_scatter(lax.dot_general(mixed_t, out_weight, contract_rows, pref...  87.6 us
    reduce_scatter x1, waiting for transfers between devices, body(): lax.psum_scatter(lax.dot_general(grad_t, flat_qkv, (((0,), (1,)), ((), ()...  85 us
    all_gather x1, waiting for transfers between devices, body(): piece_rows = lax.all_gather(grad_attn_low, 'heads', axis=0, tiled=True)  69.3 us
    all_gather x1, waiting for transfers between devices, body(): whole_in = lax.all_gather(ffn_in_weight, both, axis=1, tiled=True)  59.3 us
    psum x1, blocking collectives, body(): lax.psum((conv_full, bias_full, bound_total, live_count), both)  50 us
    all_gather x1, waiting for transfers between devices, body(): lax.all_gather(jnp.concatenate([ffn_out_weight, bias_row], axis=0), both,...  42.9 us
    pallas_call x1, Pallas kernels, mix_backward(): pl.pallas_call(partial(mix_backward_kernel, slots, marks, taps), out_shap...  37.7 us
  transfers between devices with their start and end apart: 9, of which 6 were waited for; matrix products, arithmetic and copies ran while one was open for 9% of the time, Pallas kernels for 5%

profile of v1, /device:TPU:0, one launch (start us, length us, event | category | flops | bytes accessed | tf_op | source)
XLA Modules:
  0.0 741.5 jit_solution(17093271071547402039)
XLA Ops:
  8.1 0.8 constant_dynamic-slice_fusion
  9.0 0.9 broadcast_in_dim.44.bias_ref
  9.9 1.3 constant_dynamic-slice_fusion.3.conv_ref
  11.1 32.0 %mix_forward.1 = (bf16[576,3072]{1,0:T(8,128)(2,1)}, bf16[192,3072]{1,0:T(8,128)(2,1)}, bf16[192,3072]{1,0:T(8,128)(2,1)}, bf16[192,3072]{1,0:T(8,128)(2,1)}, f3...) custom-call(s32[3]{0:T(128)} %len_ref.3, ...), custom_call_target="tpu_custom_call" | custom-call | tf_op jit(solution)/shard_map/mix_forward/pallas_call | solution.py:604
  43.1 4.9 convolution_convert_fusion.3
  48.1 0.8 copy-done.7
  50.3 87.6 %reduce-scatter.8.cloned.1.call-done = bf16[768,768]{1,0:T(8,128)(2,1)} async-done(((bf16[3072,768]{1,0:T(8,128)(2,1)}), bf16[768,768]{1,0:T(8,128)(2,1)}) %reduce-scatter.8.cloned.1.call-update) | async-done | bytes 1179664 | tf_op jit(solution)/shard_map/reduce_scatter | solution.py:729
  137.9 2.2 fusion.12
  140.1 1.9 multiply_reduce_fusion.3
  142.0 42.9 %all-gather.9.cloned.1.call-done = bf16[3584,768]{1,0:T(8,128)(2,1)} async-done(((bf16[112,768]{1,0:T(8,128)(2,1)}), bf16[3584,768]{1,0:T(8,128)(2,1)}) %all-gather.9.cloned.1.call-update) | async-done | bytes 5505040 | tf_op jit(solution)/shard_map/all_gather | solution.py:742
  184.9 4.8 slice.41
  189.7 0.9 fusion.17
  190.7 59.3 %all-gather.5.cloned.1.call-done = bf16[768,3072]{0,1:T(8,128)(2,1)} async-done(((bf16[768,96]{0,1:T(8,128)(2,1)}), bf16[768,3072]{0,1:T(8,128)(2,1)}) %all-gather.5.cloned.1.call-update) | async-done | bytes 4718608 | tf_op jit(solution)/shard_map/all_gather | solution.py:741
  250.0 28.3 %multiply_convert_fusion = (bf16[768,3072]{1,0:T(8,128)(2,1)S(1)}, f32[768,3072]{1,0:T(8,128)}, f32[768,3072]{1,0:T(8,128)}) fusion(f32[3072]{0:T(1024)S(1)} %reshape.154, bf16[768,3072]{0,1:T(8,128)(2,1)} %all-gather.5.cloned.1.call-done, f32[768]{0:T(1024)S(1)} %copy-done.17, f32[768]{0:T(1024)S(1)} %copy-done.12, f32[768]{0:T(1024)S(1)} %fusion.18, ...), kind=kOutput, calls=%fused_computation.4 | convolution fusion | flops 3784900608 | bytes 30698500 | tf_op jit(solution)/shard_map/dot_general | solution.py:746
  278.3 2.2 copy-done.18
  280.5 5.5 fusion.29
  286.5 0.8 copy-done.4
  287.3 0.9 fusion.10
  288.3 2.1 fusion.27
  290.7 12.8 %convert_reduce_fusion = (f32[3072]{0:T(1024)S(1)}, bf16[768,3072]{1,0:T(8,128)(2,1)}) fusion(f32[768,3072]{1,0:T(8,128)} %get-tuple-element.115, f32[768,3072]{1,0:T(8,128)} %get-tuple-element.119, f32[3072]{0:T(1024)S(1)} %reshape.154, bf16[768,768]{1,0:T(8,128)(2,1)S(1)} %get-tuple-element.107, bf16[3072,768]{1,0:T(8,128)(2,1)S(1)} %bitcast.48), kind=kOutput, calls=%fused_computation.2 | convolution fusion | flops 3663983616 | bytes 29515776 | tf_op jit(solution)/shard_map/dot_general | solution.py:759
  303.5 7.8 %multiply_reduce_fusion = (f32[768]{0:T(1024)S(1)}, f32[768]{0:T(1024)S(1)}, f32[768]{0:T(1024)S(1)}, f32[768,768]{1,0:T(8,128)S(1)}) fusion(f32[768]{0:T(1024)S(1)} %fusion.18, f32[768]{0:T(1024)S(1)} %broadcast_multiply_fusion.1, f32[768]{0:T(1024)S(1)} %copy-done.9, bf16[768,768]{1,0:T(8,128)(2,1)S(1)} %copy-done.2, bf16[3072,768]{1,0:T(8,128)(2,1)S(1)} %bitcast.46, ...), kind=kOutput, calls=%fused_computation.34 | convolution fusion | flops 3632133888 | bytes 16539652 | tf_op jit(solution)/shard_map/dot_general | solution.py:767
  311.3 1.2 fusion.26
  312.5 1.3 convert_reduce_fusion.2
  314.3 8.7 %convolution_convert_fusion.1 = bf16[3072,768]{1,0:T(8,128)(2,1)} fusion(bf16[768,3072]{1,0:T(8,128)(2,1)} %copy-done.18, bf16[768,768]{1,0:T(8,128)(2,1)} %copy-done.5), kind=kOutput, calls=%fused_computation.19 | convolution fusion | flops 3626237952 | bytes 10616832 | tf_op jit(solution)/shard_map/dot_general | solution.py:756
  323.1 9.4 %convolution_convert_fusion = bf16[768,3072]{1,0:T(8,128)(2,1)} fusion(bf16[768,3072]{1,0:T(8,128)(2,1)} %get-tuple-element.109, f32[768]{0:T(1024)S(1)} %copy-done.17, f32[768]{0:T(1024)S(1)} %copy-done.12, f32[768]{0:T(1024)S(1)} %fusion.18, bf16[768,768]{1,0:T(8,128)(2,1)} %reduce-scatter.8.cloned.1.call-done, f32[768]{0:T(1024)S(1)} %broadcast_multiply_fusion.1, ...), kind=kOutput, calls=%fused_computation.18 | convolution fusion | flops 3631546368 | bytes 11811844 | tf_op jit(solution)/shard_map/dot_general | solution.py:764
  332.5 69.3 %all-gather.7.cloned.1.call-done = bf16[3072,768]{1,0:T(8,128)(2,1)} async-done(((bf16[768,768]{1,0:T(8,128)(2,1)}), bf16[3072,768]{1,0:T(8,128)(2,1)}) %all-gather.7.cloned.1.call-update) | async-done | bytes 4718608 | tf_op jit(solution)/shard_map/all_gather | solution.py:773
  401.7 5.0 fusion.6.grad_ref
  406.8 6.7 copy.43
  414.5 37.7 %mix_backward.1 = (bf16[576,3072]{1,0:T(8,128)(2,1)}, f32[192,2]{1,0:T(8,128)}, f32[3,128]{1,0:T(4,128)}) custom-call(s32[3]{0:T(128)} %len_ref.3, bf16[192,3072]{1,0:T(8,128)(2,1)} %fusion.6.grad_ref, bf16[576,3072]{1,0:T(8,128)(2,1)} %get-tuple-element.43.qkv_ref, bf16[192,3072]{1,0:T(8,128)(2,1)} %get-tuple-element.44.first_ref, ...), custom_call_target="tpu_custom_call" | custom-call | tf_op jit(solution)/shard_map/mix_backward/pallas_call | solution.py:640
  452.2 7.7 %convolution_convert_fusion.2 = bf16[3072,768]{1,0:T(8,128)(2,1)} fusion(bf16[576,3072]{1,0:T(8,128)(2,1)} %get-tuple-element.53, bf16[768,576]{0,1:T(8,128)(2,1)S(1)} %bitcast.52), kind=kOutput, calls=%fused_computation.20 | convolution fusion | flops 2720268288 | bytes 9142272 | tf_op jit(solution)/shard_map/dot_general | solution.py:792
  459.9 4.5 convolution_convert_fusion.6
  464.8 0.8 copy.49
  465.6 3.7 all-to-all-start.1
  469.3 7.3 fusion.14
  476.6 3.2 convert_element_type.115
  479.8 2.6 copy.36
  482.4 4.3 all-to-all-start
  486.7 1.2 slice.39
  489.6 50.0 %all-reduce.3 = (f32[2,768]{1,0:T(2,128)S(1)}, f32[12,33]{1,0:T(8,128)S(1)}, f32[3072]{0:T(1024)S(1)}, f32[6,768]{1,0:T(8,128)S(1)}, f32[]{:T(128)}, /*index=5*/f32[]{:T(128)}) all-reduce(f32[2,768]{1,0:T(2,128)S(1)} %dynamic_update_slice.6, ...), channel_id=1, replica_groups=mesh['batch'=8,'heads'=4] {'batch','heads'}, use_global_device_ids=true, to_apply=%region_11.0 | all-reduce | flops 9614 | bytes 76912 | tf_op jit(solution)/shard_map/psum | solution.py:820
  543.5 0.7 convert_reduce_fusion.5
  544.2 1.6 convert_reduce_fusion.4
  545.8 0.9 copy.40
  546.7 1.1 copy.44
  547.7 0.9 copy.41
  548.6 94.4 %reduce-scatter.12.cloned.1.call-done = bf16[96,768]{1,0:T(8,128)(2,1)} async-done(((bf16[3072,768]{1,0:T(8,128)(2,1)}), bf16[96,768]{1,0:T(8,128)(2,1)}) %reduce-scatter.12.cloned.1.call-update) | async-done | bytes 147472 | tf_op jit(solution)/shard_map/reduce_scatter | solution.py:779
  643.0 1.6 convert_element_type.121
  644.6 85.0 %reduce-scatter.10.cloned.1.call-done = bf16[768,768]{1,0:T(8,128)(2,1)} async-done(((bf16[3072,768]{1,0:T(8,128)(2,1)}), bf16[768,768]{1,0:T(8,128)(2,1)}) %reduce-scatter.10.cloned.1.call-update) | async-done | bytes 1179664 | tf_op jit(solution)/shard_map/reduce_scatter | solution.py:791
  729.6 3.0 convert_add_fusion
  (89 shorter events, 7.8 us)
Async XLA Ops:
  8.0 35.1 %copy-start = (bf16[192,768]{1,0:T(8,128)(2,1)S(1)}, bf16[192,768]{1,0:T(8,128)(2,1)}, u32[]{:S(2)}) copy-start(bf16[192,768]{1,0:T(8,128)(2,1)} %param.24) | copy-start | bytes 884740
  8.0 129.9 %reduce-scatter.8.cloned.1.call-start = ((), (), s32[]{:S(2)}) async-start(), calls=%async_computation.6 | async-start | bytes 5898240 | tf_op jit(solution)/shard_map/reduce_scatter | solution.py:729
  48.0 0.9 copy-start.7
  48.0 0.9 copy-start.15
  48.0 89.9 %copy-start.9 = (f32[768]{0:T(1024)S(1)}, f32[768]{0:T(1024)}, u32[]{:S(2)}) copy-start(f32[768]{0:T(1024)} %param.25) | copy-start | bytes 9220
  48.1 136.8 %all-gather.9.cloned.1.call-start = ((), (), s32[]{:S(2)}) async-start(), calls=%async_computation.11 | async-start | bytes 5677056 | tf_op jit(solution)/shard_map/all_gather | solution.py:742
  49.6 200.4 %all-gather.5.cloned.1.call-start = ((), (), s32[]{:S(2)}) async-start(), calls=%async_computation.7 | async-start | bytes 4866048 | tf_op jit(solution)/shard_map/all_gather | solution.py:741
  50.2 351.5 %all-gather.7.cloned.1.call-start = ((), (), s32[]{:S(2)}) async-start(), calls=%async_computation.8 | async-start | bytes 5898240 | tf_op jit(solution)/shard_map/all_gather | solution.py:773
  137.9 2.2 copy-start.1
  184.9 65.1 %copy-start.12 = (f32[768]{0:T(1024)S(1)}, f32[768]{0:T(1024)}, u32[]{:S(2)}) copy-start(f32[768]{0:T(1024)} %param.26) | copy-start | bytes 9220
  184.9 65.1 %copy-start.17 = (f32[768]{0:T(1024)S(1)}, f32[768]{0:T(1024)}, u32[]{:S(2)}) copy-start(f32[768]{0:T(1024)} %param.27) | copy-start | bytes 9220
  190.7 89.9 %copy-start.16 = (f32[768]{0:T(1024)S(1)}, f32[768]{0:T(1024)}, u32[]{:S(2)}) copy-start(f32[768]{0:T(1024)} %param.31) | copy-start | bytes 9220
  250.0 30.5 %copy-start.2 = (bf16[768,768]{1,0:T(8,128)(2,1)S(1)}, bf16[768,768]{1,0:T(8,128)(2,1)}, u32[]{:S(2)}) copy-start(bf16[768,768]{1,0:T(8,128)(2,1)} %reduce-scatter.8.cloned.1.call-done) | copy-start | bytes 3538948
  250.0 30.5 %copy-start.3 = (bf16[32,96,768]{2,1,0:T(8,128)(2,1)S(1)}, bf16[32,96,768]{2,1,0:T(8,128)(2,1)}, u32[]{:S(2)}) copy-start(bf16[32,96,768]{2,1,0:T(8,128)(2,1)} %slice.41) | copy-start | bytes 14155780
  278.3 2.2 copy-start.18
  286.1 1.3 copy-start.4
  286.1 1.3 copy-start.10
  286.5 1.8 copy-start.11
  288.3 15.2 %slice-start = ((s8[4718592]{0:T(1024)(128)(4,1)}), s8[4194304]{0:T(1024)(128)(4,1)S(1)}, s32[]{:S(2)}) async-start(s8[4718592]{0:T(1024)(128)(4,1)} %bitcast.45), calls=%async_computation.13 | async-start | bytes 8388608
  290.7 12.8 %copy-start.5 = (bf16[768,768]{1,0:T(8,128)(2,1)}, bf16[768,768]{1,0:T(8,128)(2,1)S(1)}, u32[]{:S(2)}) copy-start(bf16[768,768]{1,0:T(8,128)(2,1)S(1)} %get-tuple-element.107) | copy-start | bytes 3538948
  290.7 12.8 %slice-start.1 = ((s8[4718592]{0:T(1024)(128)(4,1)}), s8[524288]{0:T(1024)(128)(4,1)S(1)}, s32[]{:S(2)}) async-start(s8[4718592]{0:T(1024)(128)(4,1)} %bitcast.45), calls=%async_computation.14 | async-start | bytes 1048576
  313.9 232.8 %reduce-scatter.14.cloned.1.call-start = ((), (), s32[]{:S(2)}) async-start(), calls=%async_computation.12 | async-start | bytes 4866048
  413.5 229.5 %reduce-scatter.12.cloned.1.call-start = ((), (), s32[]{:S(2)}) async-start(), calls=%async_computation.10 | async-start | bytes 4866048 | tf_op jit(solution)/shard_map/reduce_scatter | solution.py:779
  414.2 315.4 %reduce-scatter.10.cloned.1.call-start = ((), (), s32[]{:S(2)}) async-start(), calls=%async_computation.9 | async-start | bytes 5898240 | tf_op jit(solution)/shard_map/reduce_scatter | solution.py:791
  414.4 37.7 %copy-start.6 = (bf16[768,3,192]{0,2,1:T(8,128)(2,1)S(1)}, bf16[768,3,192]{0,2,1:T(8,128)(2,1)}, u32[]{:S(2)}) copy-start(bf16[768,3,192]{0,2,1:T(8,128)(2,1)} %param.21) | copy-start | bytes 2654212
  465.6 16.7 %all-to-all-start.1 = ((bf16[8,192,96]{2,1,0:T(8,128)(2,1)}), bf16[8,192,96]{2,1,0:T(8,128)(2,1)S(1)}, u32[]{:S(2)}, u32[]{:S(2)}) async-start(bf16[8,192,96]{2,1,0:T(8,128)(2,1)} %bitcast.42), calls=%async_computation.3 | async-start | bytes 786432 | tf_op jit(solution)/shard_map/all_to_all | solution.py:674
  479.8 8.1 %copy-start.13 = (s32[3]{0:T(128)S(1)}, s32[3]{0:T(128)}, u32[]{:S(2)}) copy-start(s32[3]{0:T(128)} %len_ref.3) | copy-start | bytes 40
  479.8 9.5 %copy-start.8 = (f32[192,2]{1,0:T(8,128)S(1)}, f32[192,2]{1,0:T(8,128)}, u32[]{:S(2)}) copy-start(f32[192,2]{1,0:T(8,128)} %get-tuple-element.54) | copy-start | bytes 4612
  479.8 9.7 %copy-start.14 = (f32[3,128]{1,0:T(4,128)S(1)}, f32[3,128]{1,0:T(4,128)}, u32[]{:S(2)}) copy-start(f32[3,128]{1,0:T(4,128)} %get-tuple-element.55) | copy-start | bytes 4612
  482.4 61.8 %all-to-all-start = ((bf16[8,96,3,192]{1,3,2,0:T(8,128)(2,1)}), bf16[8,96,3,192]{1,3,2,0:T(8,128)(2,1)}, u32[]{:S(2)}, u32[]{:S(2)}) async-start(bf16[8,96,3,192]{1,3,2,0:T(8,128)(2,1)} %copy.36), calls=%async_computation.2 | async-start | bytes 2359296 | tf_op jit(solution)/shard_map/all_to_all | solution.py:674
Sparse Core Ops, SparseCore 0:
  48.2 89.6 reduce-scatter.7
  314.0 87.6 all-gather.6
Sparse Core Ops, SparseCore 1:
  51.9 132.9 all-gather.8
  187.6 62.4 all-gather.4
  413.6 117.4 reduce-scatter.13
  537.5 105.4 reduce-scatter.11
  645.3 84.2 reduce-scatter.9

commit v2 on v1

--- a/solution.py
+++ b/solution.py
@@ -838,7 +838,659 @@
     )
 
 
+def place():
+    b, z = lax.axis_index("batch"), lax.axis_index("heads")
+    core, x, y = b % 2, (b // 2) % 2, b // 4
+    return b, z, b + 1 - 2 * core, b + 2 - 4 * x, b + 4 - 8 * y
+
+
+def remote(src, dst, send, recv, device):
+    return pltpu.make_async_remote_copy(
+        src_ref=src,
+        dst_ref=dst,
+        send_sem=send,
+        recv_sem=recv,
+        device_id=device,
+        device_id_type=pl.DeviceIdType.MESH,
+    )
+
+
+def greet(devices):
+    barrier = pltpu.get_barrier_semaphore()
+    for device in devices:
+        pl.semaphore_signal(
+            barrier, inc=1, device_id=device, device_id_type=pl.DeviceIdType.MESH
+        )
+    pl.semaphore_wait(barrier, len(devices))
+
+
+def exchange_kernel(
+    pieces,
+    mixed_ref, in_ref, down_ref, misc_ref,
+    all_ref, in_all, down_all, misc_all,
+    a_send, a_recv, l_send, l_recv, p_send, p_recv, own_sem,
+):
+    b, z, bc, bx, by = place()
+    peers = [(b, lax.rem(z + i, 4)) for i in (1, 2, 3)]
+    greet(peers + [(bc, z), (bx, z), (by, z)])
+    quarter = all_ref.shape[2]
+    owns = (in_ref, down_ref, misc_ref)
+    alls = (in_all, down_all, misc_all)
+
+    local = [
+        pltpu.make_async_copy(own, everything.at[b, z], own_sem.at[n])
+        for n, (own, everything) in enumerate(zip(owns, alls))
+    ]
+
+    def columns(n):
+        return pl.ds(pl.multiple_of(n * quarter, quarter), quarter)
+
+    local.append(
+        pltpu.make_async_copy(mixed_ref.at[:, columns(z)], all_ref.at[z], own_sem.at[3])
+    )
+    for copy in local:
+        copy.start()
+
+    def line(up, hop, n):
+        array, start, count, _ = pieces[n]
+        rows = pl.ds(start, count)
+        origin = z - hop + 1 if up else z + hop - 1
+        dst = alls[array].at[b, origin, rows]
+        src = owns[array].at[rows] if hop == 1 else dst
+        side = 0 if up else 1
+        return remote(
+            src, dst, l_send.at[side, hop - 1, n], l_recv.at[side, hop - 1, n],
+            (b, z + 1 if up else z - 1),
+        )
+
+    def line_in(up, hop, n):
+        array, start, count, _ = pieces[n]
+        origin = z - hop if up else z + hop
+        dst = alls[array].at[b, origin, pl.ds(start, count)]
+        side = 0 if up else 1
+        return remote(
+            dst, dst, l_send.at[side, hop - 1, n], l_recv.at[side, hop - 1, n],
+            (b, z - 1 if up else z + 1),
+        )
+
+    def has(up, hop):
+        return z >= hop if up else z <= 3 - hop
+
+    def sends(up, hop):
+        return ((z < 3) & (z >= hop - 1)) if up else ((z > 0) & (z <= 4 - hop))
+
+    count = len(pieces)
+    for n in range(count):
+        for up in (True, False):
+
+            @pl.when(sends(up, 1))
+            def _():
+                line(up, 1, n).start()
+
+    def block(n, who):
+        array, start, rows, _ = pieces[n]
+        return alls[array].at[who, :, pl.ds(start, rows)]
+
+    def pair(n, slot, who, device):
+        ref = block(n, who)
+        return remote(ref, ref, p_send.at[n, slot], p_recv.at[n, slot], (device, z))
+
+    both = bx + by - b
+    issued = []
+
+    def first(n):
+        p = by if pieces[n][3] else bx
+        copy = pair(n, 0, b, p)
+        copy.start()
+        issued.append(copy)
+
+    def second(n):
+        p, q = (by, bx) if pieces[n][3] else (bx, by)
+        pair(n, 0, p, p).wait_recv()
+        for slot, who in ((1, b), (2, p)):
+            copy = pair(n, slot, who, q)
+            copy.start()
+            issued.append(copy)
+
+    def third(n):
+        p, q = (by, bx) if pieces[n][3] else (bx, by)
+        pair(n, 1, q, q).wait_recv()
+        pair(n, 2, both, q).wait_recv()
+        for slot, who in enumerate((b, bx, by, both)):
+            copy = pair(n, 3 + slot, who, bc)
+            copy.start()
+            issued.append(copy)
+
+    def fourth(n):
+        flip = bc - b
+        for slot, who in enumerate((b, bx, by, both)):
+            pair(n, 3 + slot, who + flip, bc).wait_recv()
+
+    for copy in local:
+        copy.wait()
+    for n in range(count + 3):
+        if n < count:
+            for hop in (1, 2, 3):
+                for up in (True, False):
+
+                    @pl.when(has(up, hop))
+                    def _():
+                        line_in(up, hop, n).wait_recv()
+
+                    if hop < 3:
+
+                        @pl.when(sends(up, hop + 1))
+                        def _():
+                            line(up, hop + 1, n).start()
+
+            first(n)
+        if n == count - 1:
+            for i, (_, to) in enumerate(peers):
+                copy = remote(
+                    mixed_ref.at[:, columns(to)], all_ref.at[z],
+                    a_send.at[i], a_recv.at[i], (b, to),
+                )
+                copy.start()
+                issued.append(copy)
+        if 0 <= n - 1 < count:
+            second(n - 1)
+        if 0 <= n - 2 < count:
+            third(n - 2)
+        if 0 <= n - 3 < count:
+            fourth(n - 3)
+    for i in (1, 2, 3):
+        source = lax.rem(z + 4 - i, 4)
+        ref = all_ref.at[source]
+        remote(ref, ref, a_send.at[i - 1], a_recv.at[i - 1], (b, source)).wait_recv()
+    for n in range(count):
+        for hop in (1, 2, 3):
+            for up in (True, False):
+
+                @pl.when(sends(up, hop))
+                def _():
+                    line(up, hop, n).wait_send()
+
+    for copy in issued:
+        copy.wait_send()
+
+
+def exchange(mixed_t, in_own, down_own, misc_own):
+    width, tok_count = mixed_t.shape
+    ff, model = in_own.shape
+    misc = misc_own.shape[0]
+    half = ff // 2
+    pieces = (
+        (2, 0, misc, 0),
+        (0, 0, half, 0), (1, 0, half, 1), (0, half, half, 0), (1, half, half, 1),
+    )
+    shape = lambda *s: jax.ShapeDtypeStruct(s, low)
+    vmem = pl.BlockSpec(memory_space=pltpu.VMEM)
+    hbm = pl.BlockSpec(memory_space=pl.ANY)
+    dma = pltpu.SemaphoreType.DMA
+    n = len(pieces)
+    return pl.pallas_call(
+        partial(exchange_kernel, pieces),
+        out_shape=[
+            shape(4, width, tok_count // 4),
+            shape(8, 4, ff, model), shape(8, 4, ff, model), shape(8, 4, misc, model),
+        ],
+        in_specs=[vmem] * 4,
+        out_specs=[hbm] * 4,
+        scratch_shapes=[
+            dma((3,)), dma((3,)), dma((2, 3, n)), dma((2, 3, n)), dma((n, 7)), dma((n, 7)),
+            dma((4,)),
+        ],
+        compiler_params=pltpu.CompilerParams(collective_id=1, has_side_effects=True),
+        name="exchange",
+    )(mixed_t, in_own, down_own, misc_own)
+
+
+def turn_kernel(grad_ref, out_ref, send, recv, own_sem):
+    b, z, _, _, _ = place()
+    peers = [(b, lax.rem(z + i, 4)) for i in (1, 2, 3)]
+    greet(peers)
+    width, quarter = out_ref.shape[0], grad_ref.shape[1]
+
+    def rows(n):
+        return pl.ds(pl.multiple_of(n * width, width), width)
+
+    def columns(n):
+        return pl.ds(pl.multiple_of(n * quarter, quarter), quarter)
+
+    copies = []
+    for i, (_, to) in enumerate(peers):
+        copy = remote(
+            grad_ref.at[rows(to)], out_ref.at[:, columns(z)], send.at[i], recv.at[i], (b, to)
+        )
+        copy.start()
+        copies.append(copy)
+    own = pltpu.make_async_copy(grad_ref.at[rows(z)], out_ref.at[:, columns(z)], own_sem.at[0])
+    own.start()
+    for i in (1, 2, 3):
+        source = lax.rem(z + 4 - i, 4)
+        ref = out_ref.at[:, columns(source)]
+        remote(ref, ref, send.at[i - 1], recv.at[i - 1], (b, source)).wait_recv()
+    for copy in copies:
+        copy.wait_send()
+    own.wait()
+
+
+def turn(grad_all, width):
+    quarter = grad_all.shape[1]
+    dma = pltpu.SemaphoreType.DMA
+    return pl.pallas_call(
+        turn_kernel,
+        out_shape=jax.ShapeDtypeStruct((width, 4 * quarter), low),
+        in_specs=[pl.BlockSpec(memory_space=pltpu.VMEM)],
+        out_specs=pl.BlockSpec(memory_space=pl.ANY),
+        scratch_shapes=[dma((3,)), dma((3,)), dma((1,))],
+        compiler_params=pltpu.CompilerParams(collective_id=2, has_side_effects=True),
+        name="turn",
+    )(grad_all)
+
+
+def tail_kernel(
+    part_ref, first_ref, down_ref, up_ref, outw_ref, qkvw_ref, small_ref,
+    input_ref, down_own, up_own, outw_own, qkvw_own, small_out,
+    up_in, down_in, core_down, core_up, core_outw, core_qkvw,
+    one_down, one_up, one_outw, one_qkvw, two_down, two_up, two_outw, two_qkvw,
+    z_down, z_up, z_outw, small_in,
+    z_send, z_recv, c_send, c_recv, x_send, x_recv, e_send, e_recv, s_send, s_recv,
+):
+    b, z, bc, bx, by = place()
+    both = bx + by - b
+    flip = bc - b
+    peers = [(b, lax.rem(z + i, 4)) for i in (1, 2, 3)]
+    greet(peers + [(bc, z), (bx, z), (by, z)])
+    chunks = up_in.shape[1]
+    size = up_in.shape[2]
+    issued = []
+
+    fulls = (down_ref, up_ref, outw_ref, qkvw_ref)
+    cores = (core_down, core_up, core_outw, core_qkvw)
+    ones = (one_down, one_up, one_outw, one_qkvw)
+    twos = (two_down, two_up, two_outw, two_qkvw)
+    kinds = len(fulls)
+    groups = (b, bx, by, both)
+
+    def at(n, who):
+        return fulls[n].at[:, who] if n == 2 else fulls[n].at[who]
+
+    for slot, who in enumerate(groups):
+        for n in range(kinds):
+            copy = remote(
+                at(n, who + flip), cores[n].at[slot], c_send.at[n, slot], c_recv.at[n, slot],
+                (bc, z),
+            )
+            copy.start()
+            issued.append(copy)
+
+    def flow(up, owner, c):
+        buf = up_in if up else down_in
+        side = 0 if up else 1
+        return remote(
+            buf.at[owner, c], buf.at[owner, c], z_send.at[side, owner, c],
+            z_recv.at[side, owner, c], (b, z + 1 if up else z - 1),
+        )
+
+    def flow_first(up, owner, c):
+        buf = up_in if up else down_in
+        side = 0 if up else 1
+        return remote(
+            part_ref.at[owner, c], buf.at[owner, c], z_send.at[side, owner, c],
+            z_recv.at[side, owner, c], (b, z + 1 if up else z - 1),
+        )
+
+    def z_event(k, c):
+        for up in (True, False):
+            owner = 3 - k if up else k
+            buf = up_in if up else down_in
+            at_end = (z == 0) if up else (z == 3)
+            inner = ((z > 0) & (z < owner)) if up else ((z < 3) & (z > owner))
+
+            @pl.when(at_end)
+            def _():
+                flow_first(up, owner, c).start()
+
+            @pl.when(inner)
+            def _():
+                flow(up, owner, c).wait_recv()
+                buf[owner, c] = (
+                    buf[owner, c].astype(f32) + part_ref[owner, c].astype(f32)
+                ).astype(low)
+                flow(up, owner, c).start()
+
+    def core_event(n):
+        for slot, who in enumerate(groups):
+            ref = cores[n].at[slot]
+            remote(ref, ref, c_send.at[n, slot], c_recv.at[n, slot], (bc, z)).wait_recv()
+            mine = fulls[n][:, who] if n == 2 else fulls[n][who]
+            cores[n][slot] = (cores[n][slot].astype(f32) + mine.astype(f32)).astype(low)
+        first, second = (2, 1) if n % 2 == 0 else (1, 2)
+        partner = by if n % 2 == 0 else bx
+        for i, (src, dst) in enumerate(((first, 0), (3, 1))):
+            copy = remote(
+                cores[n].at[src], ones[n].at[dst], x_send.at[n, i], x_recv.at[n, i], (partner, z)
+            )
+            copy.start()
+            issued.append(copy)
+
+    def one_event(n):
+        first, second = (2, 1) if n % 2 == 0 else (1, 2)
+        partner, other = (by, bx) if n % 2 == 0 else (bx, by)
+        for i, slot in ((0, 0), (1, second)):
+            ref = ones[n].at[i]
+            remote(ref, ref, x_send.at[n, i], x_recv.at[n, i], (partner, z)).wait_recv()
+            ones[n][i] = (ones[n][i].astype(f32) + cores[n][slot].astype(f32)).astype(low)
+        copy = remote(
+            ones[n].at[1], twos[n], x_send.at[n, 2], x_recv.at[n, 2], (other, z)
+        )
+        copy.start()
+        issued.append(copy)
+
+    z_bufs = (z_down, z_up, z_outw)
+
+    def two_event(n):
+        other = bx if n % 2 == 0 else by
+        ref = twos[n]
+        remote(ref, ref, x_send.at[n, 2], x_recv.at[n, 2], (other, z)).wait_recv()
+        if n == 3:
+            qkvw_own[...] = twos[n][...].astype(f32) + ones[n][0].astype(f32)
+            return
+        twos[n][...] = (twos[n][...].astype(f32) + ones[n][0].astype(f32)).astype(low)
+        for i, (_, to) in enumerate(peers):
+            copy = remote(
+                twos[n].at[to], z_bufs[n].at[i], e_send.at[n, i], e_recv.at[n, i], (b, to)
+            )
+            copy.start()
+            issued.append(copy)
+
+    def end_event(n):
+        total = twos[n][z].astype(f32)
+        for i in range(3):
+            source = lax.rem(z + 3 - i, 4)
+            ref = z_bufs[n].at[i]
+            remote(ref, ref, e_send.at[n, i], e_recv.at[n, i], (b, source)).wait_recv()
+            total = total + z_bufs[n][i].astype(f32)
+        (down_own, up_own, outw_own)[n][...] = total
+
+    zf = z + 1 - 2 * (z % 2)
+    zg = z + 2 - 4 * (z // 2)
+    partners = ((bc, z), (bx, z), (by, z), (b, zf), (b, zg))
+
+    def small_start(k):
+        copy = remote(
+            small_out.at[k], small_in.at[k], s_send.at[k], s_recv.at[k], partners[k]
+        )
+        copy.start()
+        issued.append(copy)
+
+    def small_event(k):
+        ref = small_in.at[k]
+        remote(ref, ref, s_send.at[k], s_recv.at[k], partners[k]).wait_recv()
+        small_out[k + 1] = small_out[k] + small_in[k]
+        if k < 4:
+            small_start(k + 1)
+
+    small_out[0] = small_ref[...]
+    small_start(0)
+
+    z_list = [(k, c) for k in range(3) for c in range(chunks)]
+    other = (
+        [partial(core_event, n) for n in (0, 1, 2, 3)]
+        + [partial(small_event, 0), partial(small_event, 1)]
+        + [partial(one_event, n) for n in (0, 1, 2, 3)]
+        + [partial(small_event, 2), partial(small_event, 3)]
+        + [partial(two_event, n) for n in (0, 1, 2, 3)]
+        + [partial(small_event, 4)]
+    )
+    lead = 2
+    for k, c in z_list[:lead]:
+        z_event(k, c)
+    rest = z_list[lead:]
+    for n in range(max(len(rest), len(other))):
+        if n < len(other):
+            other[n]()
+        if n < len(rest):
+            z_event(*rest[n])
+    for n in (0, 1, 2):
+        end_event(n)
+
+    for c in range(chunks):
+        rows = pl.ds(c * size, size)
+        input_ref[rows] = first_ref[rows] + part_ref[z, c].astype(f32)
+
+    for c in range(chunks):
+        rows = pl.ds(c * size, size)
+        for up in (True, False):
+            buf = up_in if up else down_in
+
+            @pl.when((z > 0) if up else (z < 3))
+            def _():
+                side = 0 if up else 1
+                ref = buf.at[z, c]
+                remote(
+                    ref, ref, z_send.at[side, z, c], z_recv.at[side, z, c],
+                    (b, z - 1 if up else z + 1),
+                ).wait_recv()
+                input_ref[rows] += buf[z, c].astype(f32)
+
+    for k, c in z_list:
+        for up in (True, False):
+            owner = 3 - k if up else k
+
+            @pl.when((z < owner) if up else (z > owner))
+            def _():
+                flow(up, owner, c).wait_send()
+
+    for copy in issued:
+        copy.wait_send()
+
+
+def tail(part, first, down, up, outw, qkvw, small):
+    quarter, model = first.shape
+    chunks = 4
+    size = quarter // chunks
+    ff = down.shape[2]
+    on, oh = outw.shape[2:]
+    qn, qh = qkvw.shape[1:]
+    blocks = ((4, ff, model), (4, ff, model), (4, on, oh), (qn, qh))
+    own = lambda *s: jax.ShapeDtypeStruct(s, f32)
+    vm = lambda *s: pltpu.VMEM(s, low)
+    dma = pltpu.SemaphoreType.DMA
+    return pl.pallas_call(
+        tail_kernel,
+        out_shape=[
+            own(quarter, model), own(ff, model), own(ff, model), own(on, oh), own(qn, qh),
+            own(6, *small.shape),
+        ],
+        in_specs=[pl.BlockSpec(memory_space=pltpu.VMEM)] * 7,
+        out_specs=[pl.BlockSpec(memory_space=pltpu.VMEM)] * 6,
+        scratch_shapes=[
+            vm(4, chunks, size, model), vm(4, chunks, size, model),
+            *[vm(4, *s) for s in blocks],
+            *[vm(2, *s) for s in blocks],
+            *[vm(*s) for s in blocks],
+            *[vm(3, *s[1:]) for s in blocks[:3]],
+            pltpu.VMEM((5, *small.shape), f32),
+            dma((2, 4, chunks)), dma((2, 4, chunks)), dma((4, 4)), dma((4, 4)),
+            dma((4, 3)), dma((4, 3)), dma((3, 3)), dma((3, 3)), dma((5,)), dma((5,)),
+        ],
+        compiler_params=pltpu.CompilerParams(
+            collective_id=3, has_side_effects=True, vmem_limit_bytes=62 * 1024 * 1024
+        ),
+        name="tail",
+    )(part.reshape(4, chunks, size, model), first, down, up, outw, qkvw, small)
+
+
+def slice_body(
+    tokens,
+    qkv_weight,
+    qv_bias,
+    conv_weight,
+    out_weight,
+    out_bias,
+    norm1_gain,
+    norm1_bias,
+    ffn_in_weight,
+    ffn_in_bias,
+    ffn_out_weight,
+    ffn_out_bias,
+    norm2_gain,
+    norm2_bias,
+    cotangent,
+    seq_lengths,
+    segment_ids,
+    landmark_bounds,
+):
+    tok_count, model = tokens.shape
+    width = qkv_weight.shape[2]
+    heads_here = width // HEAD_DIM
+    kernel_taps = conv_weight.shape[1]
+    slots, marks = landmark_bounds.shape
+    quarter = tok_count // 4
+    z = lax.axis_index("heads")
+    b = lax.axis_index("batch")
+    own_tokens = lax.dynamic_slice_in_dim(tokens, z * quarter, quarter, 0).astype(f32)
+    conv_own = lax.dynamic_slice_in_dim(conv_weight, z * heads_here, heads_here, 0)
+    qv_own = lax.dynamic_slice_in_dim(qv_bias, z * width, width, 1)
+    flat_qkv = qkv_weight.reshape(model, 3 * width)
+    bias_col = jnp.concatenate([qv_own[0], jnp.zeros_like(qv_own[0]), qv_own[1]])[:, None]
+    forward = mix_forward(
+        seq_lengths, tokens, jnp.transpose(flat_qkv), bias_col, conv_own, slots, marks
+    )
+    qkv_t, first, last, mixed_t, mark, value, inner, denom, middle, steps, inverse, bound = forward
+    ff_own = ffn_out_weight.shape[0]
+    share = width // 8
+    misc_rows = 32
+    misc_own = jnp.concatenate(
+        [
+            lax.dynamic_slice_in_dim(out_weight, b * share, share, 0),
+            jnp.zeros((misc_rows - share, model), low).at[0, :ff_own].set(ffn_in_bias),
+        ],
+        axis=0,
+    )
+    mixed_all, in_all, down_all, misc_all = exchange(
+        mixed_t, jnp.transpose(ffn_in_weight), ffn_out_weight, misc_own
+    )
+    mixed_all = mixed_all.reshape(4 * width, quarter)
+    whole_in = in_all.reshape(-1, model)
+    whole_down = down_all.reshape(-1, model)
+    whole_out = jnp.swapaxes(misc_all[:, :, :share], 0, 1).reshape(4 * width, model)
+    whole_bias = misc_all[:, :, share, :ff_own].reshape(-1).astype(f32)
+
+    attn = lax.dot_general(mixed_all, whole_out, contract_rows, preferred_element_type=f32)
+    first_res = own_tokens + attn + out_bias[None, :]
+    norm1_out, norm1_pull = jax.vjp(layer_norm, first_res, norm1_gain, norm1_bias)
+    norm1_low = norm1_out.astype(low)
+    pre_act = (
+        lax.dot_general(norm1_low, whole_in, contract_cols, preferred_element_type=f32)
+        + whole_bias[None, :]
+    )
+    hidden_act, gelu_pull = jax.vjp(gelu_exact, pre_act)
+    hidden_low = hidden_act.astype(low)
+    ffn_result = jnp.dot(hidden_low, whole_down, preferred_element_type=f32) + ffn_out_bias[None, :]
+    final_out, norm2_pull = jax.vjp(layer_norm, norm1_out + ffn_result, norm2_gain, norm2_bias)
+    grad_second, grad_gain_two, grad_shift_two = norm2_pull(cotangent.astype(f32))
+    grad_ffn_low = grad_second.astype(low)
+    grad_ffn_bias = jnp.sum(grad_ffn_low.astype(f32), axis=0)
+    grad_hidden = lax.dot_general(
+        grad_ffn_low, whole_down, contract_cols, preferred_element_type=f32
+    )
+    grad_pre = gelu_pull(grad_hidden)[0].astype(low)
+    grad_in_bias = jnp.sum(grad_pre.astype(f32), axis=0)
+    grad_norm1 = grad_second + jnp.dot(grad_pre, whole_in, preferred_element_type=f32)
+    grad_first, grad_gain_one, grad_shift_one = norm1_pull(grad_norm1)
+    grad_attn_low = grad_first.astype(low)
+    grad_out_bias = jnp.sum(grad_attn_low.astype(f32), axis=0)
+    grad_mix_all = lax.dot_general(
+        whole_out, grad_attn_low, contract_cols, preferred_element_type=f32
+    ).astype(low)
+    grad_mix_t = turn(grad_mix_all, width)
+    saved = (qkv_t, first, last, mark, value, inner, denom, middle, steps, inverse)
+    grad_t, grad_bias, grad_conv = mix_backward(
+        seq_lengths, grad_mix_t, saved, conv_own, slots, marks
+    )
+    part = lax.dot_general(
+        grad_t, flat_qkv, (((0,), (1,)), ((), ())), preferred_element_type=f32
+    ).astype(low)
+    down_term = lax.dot_general(
+        hidden_low, grad_ffn_low, contract_rows, preferred_element_type=f32
+    ).astype(low)
+    up_term = lax.dot_general(
+        grad_pre, norm1_low, contract_rows, preferred_element_type=f32
+    ).astype(low)
+    out_term = lax.dot_general(
+        grad_attn_low,
+        mixed_all.reshape(4, width, quarter),
+        (((0,), (2,)), ((), ())),
+        preferred_element_type=f32,
+    ).astype(low)
+    out_term = jnp.swapaxes(out_term, 0, 1).reshape(4, 8, model // 8, width)
+    qkv_term = lax.dot_general(
+        tokens, grad_t, (((0,), (1,)), ((), ())), preferred_element_type=f32
+    ).astype(low)
+
+    flat = jnp.concatenate(
+        [
+            grad_in_bias,
+            grad_ffn_bias, grad_gain_two, grad_shift_two,
+            grad_gain_one, grad_shift_one, grad_out_bias,
+        ]
+    )
+    head_total = conv_weight.shape[0]
+    conv_full = lax.dynamic_update_slice_in_dim(
+        jnp.zeros((head_total, kernel_taps), f32), grad_conv[:, :kernel_taps], z * heads_here, 0
+    )
+    bias_full = lax.dynamic_update_slice_in_dim(
+        jnp.zeros((2, 4 * width), f32), jnp.transpose(grad_bias), z * width, 1
+    )
+    live_count = jnp.sum((seq_lengths > 0).astype(f32)) * heads_here
+    scalars = jnp.stack([bound[0, 0], live_count])
+    small = jnp.concatenate([flat, bias_full.reshape(-1), conv_full.reshape(-1), scalars])
+    lanes = 768
+    rows = -(-small.shape[0] // (8 * lanes)) * 8
+    small = jnp.pad(small, (0, rows * lanes - small.shape[0])).reshape(rows, lanes)
+    ff = ff_own * 32
+    input_grad, down_share, up_share, out_share, qkv_share, sums = tail(
+        part,
+        grad_first,
+        down_term.reshape(8, 4, ff_own, model),
+        up_term.reshape(8, 4, ff_own, model),
+        out_term,
+        qkv_term.reshape(8, model // 8, 3 * width),
+        small,
+    )
+    sums = sums[5].reshape(-1)
+    index = b * 4 + z
+    in_bias_share = lax.dynamic_slice_in_dim(sums, index * ff_own, ff_own, 0)
+    vectors = sums[ff : ff + 6 * model].reshape(6, model)
+    vector_share = lax.dynamic_slice_in_dim(vectors, index * (model // 32), model // 32, 1)
+    at = ff + 6 * model
+    bias_sum = sums[at : at + 8 * width].reshape(2, 4 * width)
+    bias_out = lax.dynamic_slice_in_dim(bias_sum, z * width, width, 1)
+    at = at + 8 * width
+    conv_sum = sums[at : at + head_total * kernel_taps].reshape(head_total, kernel_taps)
+    conv_out = lax.dynamic_slice_in_dim(conv_sum, z * heads_here, heads_here, 0)
+    at = at + head_total * kernel_taps
+    condition = sums[at] / sums[at + 1]
+    return (
+        final_out.astype(low),
+        input_grad,
+        qkv_share.reshape(model // 8, 3, width),
+        bias_out,
+        conv_out,
+        jnp.transpose(out_share),
+        jnp.transpose(up_share),
+        in_bias_share,
+        down_share,
+        vector_share,
+        condition,
+    )
+
+
 def solution(mesh):
+    chosen = slice_body if dict(mesh.shape) == {"batch": 8, "heads": 4} else body
     in_specs = (
         P("batch", None),
         P(None, None, "heads"),
@@ -872,4 +1524,4 @@
         P(None, ("batch", "heads")),
         P(),
     )
-    return jax.shard_map(body, mesh=mesh, in_specs=in_specs, out_specs=out_specs, check_vma=False)
+    return jax.shard_map(chosen, mesh=mesh, in_specs=in_specs, out_specs=out_specs, check_vma=False)

time: 749 us -> 446 us (0.60)
  waiting for transfers between devices: 440 us -> 0 us
  Pallas kernels: 69.7 us -> 314 us
  blocking collectives: 50 us -> 0 us
  matrix products: 102 us -> 86.5 us
  between operations: 19.4 us -> 4.65 us
  other arithmetic: 19.5 us -> 7.56 us
  starting transfers between devices: 8.8 us -> 0 us
    reduce_scatter x3 -> x0, waiting for transfers between devices: 267 us -> none  [the longest x1 94.4 us: body(): lax.psum_scatter(down_term, both, scatter_dimension=0, tiled=True)]
    pallas_call x0 -> x3, Pallas kernels: none -> 247 us  [the longest x1 137 us: tail(): pl.pallas_call(tail_kernel, out_shape=[own(quarter, model), own(ff, model...]
    all_gather x3 -> x0, waiting for transfers between devices: 171 us -> none  [the longest x1 69.3 us: body(): piece_rows = lax.all_gather(grad_attn_low, 'heads', axis=0, tiled=True)]
    psum x1 -> x0, blocking collectives: 50 us -> none  [body(): lax.psum((conv_full, bias_full, bound_total, live_count), both)]
    dot_general x11, matrix products: 102 us -> 86.5 us  [the longest x1 28 us: slice_body(): lax.dot_general(norm1_low, whole_in, contract_cols, preferred_element_typ...]
    all_to_all x2 -> x0, starting transfers between devices: 7.93 us -> none  [sum_at_owner(): tiles = lax.all_to_all(split_up(x, dim, peers), axis, 0, 0, tiled=True)]
  transfers between devices with their start and end apart: 9 -> 0, of which waited for: 6 -> 0; matrix products, arithmetic and copies ran while one was open for 9% -> 0% of each run, Pallas kernels for 5% -> 0%
where the time goes in v2:
time: 446 us; the launch traced here: 443 us
  Pallas kernels  314 us (70%)
  matrix products  86.5 us (19%)
  local copies, waits for them, and re-layouts  30.3 us (7%)
  other arithmetic  7.56 us (2%)
  between operations  4.65 us (1%)
    pallas_call x1, Pallas kernels, tail(): pl.pallas_call(tail_kernel, out_shape=[own(quarter, model), own(ff, model...  137 us
    pallas_call x1, Pallas kernels, exchange(): pl.pallas_call(partial(exchange_kernel, pieces), out_shape=[shape(4, widt...  84.8 us
    pallas_call x1, Pallas kernels, mix_backward(): pl.pallas_call(partial(mix_backward_kernel, slots, marks, taps), out_shap...  36.3 us
    pallas_call x1, Pallas kernels, mix_forward(): pl.pallas_call(partial(mix_forward_kernel, slots, marks, taps), out_shape...  31.1 us
    dot_general x1, matrix products, slice_body(): lax.dot_general(norm1_low, whole_in, contract_cols, preferred_element_typ...  28 us
    pallas_call x1, Pallas kernels, turn(): pl.pallas_call(turn_kernel, out_shape=jax.ShapeDtypeStruct((width, 4 * qu...  24.8 us
    dot_general x1, matrix products, slice_body(): lax.dot_general(grad_ffn_low, whole_down, contract_cols, preferred_elemen...  12.9 us
    unnamed x63, local copies, waits for them, and re-layouts  12.1 us

profile of v2, /device:TPU:0, one launch (start us, length us, event | category | flops | bytes accessed | tf_op | source)
XLA Modules:
  0.0 443.5 jit_solution(13565331646308812655)
XLA Ops:
  0.7 0.8 constant_dynamic-slice_fusion
  1.6 0.9 broadcast_in_dim.44.bias_ref
  2.4 1.3 constant_dynamic-slice_fusion.3.conv_ref
  3.7 31.1 %mix_forward.1 = (bf16[576,3072]{1,0:T(8,128)(2,1)}, bf16[192,3072]{1,0:T(8,128)(2,1)}, bf16[192,3072]{1,0:T(8,128)(2,1)}, bf16[192,3072]{1,0:T(8,128)(2,1)}, f3...) custom-call(s32[3]{0:T(128)} %len_ref.3, ...), custom_call_target="tpu_custom_call" | custom-call | tf_op jit(solution)/shard_map/mix_forward/pallas_call | solution.py:604
  34.9 0.6 fusion.15.misc_ref
  35.5 84.8 %exchange.1 = (bf16[4,192,768]{2,1,0:T(8,128)(2,1)}, bf16[8,4,96,768]{3,2,1,0:T(8,128)(2,1)}, bf16[8,4,96,768]{3,2,1,0:T(8,128)(2,1)}, bf16[8,4,32,768]{3,2,1,0:T(8,128)(2,1)}) custom-call(bf16[192,3072]{1,0:T(8,128)(2,1)} %get-tuple-element.48.mixed_ref, bf16[96,768]{1,0:T(8,128)(2,1)} %bitcast.66, bf16[96,768]{1,0:T(8,128)(2,1)} %down_ref.1, ...), custom_call_target="tpu_custom_call" | custom-call | tf_op jit(solution)/shard_map/exchange/pallas_call | solution.py:1031
  120.4 0.9 convert_reduce_fusion.4
  121.3 1.4 slice_bitcast_fusion
  122.7 1.1 copy.34
  123.8 3.4 fusion.28
  127.9 28.0 %multiply_convert_fusion = (bf16[768,3072]{1,0:T(8,128)(2,1)S(1)}, f32[768,3072]{1,0:T(8,128)}, f32[768,3072]{1,0:T(8,128)}) fusion(f32[3072]{0:T(1024)S(1)} %reshape.195, bf16[3072,768]{1,0:T(8,128)(2,1)} %bitcast.73, f32[768,768]{1,0:T(8,128)S(1)} %get-tuple-element.119, f32[768]{0:T(1024)S(1)} %copy-done.21, f32[768]{0:T(1024)S(1)} %copy-done.14, ...), kind=kOutput, calls=%fused_computation.4 | convolution fusion | flops 3782541312 | bytes 30695424 | tf_op jit(solution)/shard_map/dot_general | solution.py:1387
  155.9 2.3 copy-done.22
  158.2 4.1 fusion.29
  162.7 0.8 copy-done.4
  163.5 1.0 fusion.9
  164.5 2.1 fusion.25
  166.9 12.9 %convert_reduce_fusion = (f32[3072]{0:T(1024)S(1)}, bf16[768,3072]{1,0:T(8,128)(2,1)}) fusion(f32[768,3072]{1,0:T(8,128)} %get-tuple-element.112, f32[768,3072]{1,0:T(8,128)} %get-tuple-element.120, f32[3072]{0:T(1024)S(1)} %reshape.195, bf16[768,768]{1,0:T(8,128)(2,1)S(1)} %get-tuple-element.104, bf16[3072,768]{1,0:T(8,128)(2,1)S(1)} %bitcast.80), kind=kOutput, calls=%fused_computation.2 | convolution fusion | flops 3663983616 | bytes 29515776 | tf_op jit(solution)/shard_map/dot_general | solution.py:1397
  179.9 6.4 %multiply_reduce_fusion = (f32[768]{0:T(1024)S(1)}, f32[768]{0:T(1024)S(1)}, f32[768]{0:T(1024)S(1)}, f32[768,768]{1,0:T(8,128)S(1)}) fusion(f32[768,768]{1,0:T(8,128)S(1)} %get-tuple-element.119, f32[768]{0:T(1024)S(1)} %fusion.16, f32[768]{0:T(1024)S(1)} %broadcast_multiply_fusion.1, f32[768]{0:T(1024)S(1)} %copy-done.14, ...), kind=kOutput, calls=%fused_computation.31 | convolution fusion | flops 3629774592 | bytes 16536576 | tf_op jit(solution)/shard_map/dot_general | solution.py:1402
  186.3 0.9 fusion.24
  187.5 1.4 copy-done.2
  188.9 2.2 convolution_convert_fusion.4.grad_ref
  191.1 24.8 %turn.1.grad_ref = bf16[192,3072]{1,0:T(8,128)(2,1)} custom-call(bf16[768,768]{1,0:T(8,128)(2,1)} %convolution_convert_fusion.4.grad_ref), custom_call_target="tpu_custom_call" | custom-call | tf_op jit(solution)/shard_map/turn/pallas_call | solution.py:1081
  215.9 36.3 %mix_backward.1 = (bf16[576,3072]{1,0:T(8,128)(2,1)}, f32[192,2]{1,0:T(8,128)}, f32[3,128]{1,0:T(4,128)}) custom-call(s32[3]{0:T(128)} %len_ref.3, bf16[192,3072]{1,0:T(8,128)(2,1)} %turn.1.grad_ref, bf16[576,3072]{1,0:T(8,128)(2,1)} %get-tuple-element.53.qkv_ref, bf16[192,3072]{1,0:T(8,128)(2,1)} %get-tuple-element.54.first_ref, ...), custom_call_target="tpu_custom_call" | custom-call | tf_op jit(solution)/shard_map/mix_backward/pallas_call | solution.py:640
  252.3 7.9 %convolution_convert_fusion.2 = bf16[3072,768]{1,0:T(8,128)(2,1)} fusion(bf16[576,3072]{1,0:T(8,128)(2,1)} %get-tuple-element.63, bf16[768,576]{0,1:T(8,128)(2,1)S(1)} %bitcast.64), kind=kOutput, calls=%fused_computation.20 | convolution fusion | flops 2720268288 | bytes 9142272 | tf_op jit(solution)/shard_map/dot_general | solution.py:1414
  260.2 8.0 %convolution_convert_fusion.1 = bf16[3072,768]{1,0:T(8,128)(2,1)} fusion(bf16[768,3072]{1,0:T(8,128)(2,1)} %copy-done.22, bf16[768,768]{1,0:T(8,128)(2,1)S(1)} %copy-done.6), kind=kOutput, calls=%fused_computation.19 | convolution fusion | flops 3626237952 | bytes 10616832 | tf_op jit(solution)/shard_map/dot_general | solution.py:1417
  268.2 6.2 %convolution_convert_fusion = bf16[3072,768]{1,0:T(8,128)(2,1)} fusion(bf16[768,3072]{1,0:T(8,128)(2,1)S(1)} %bitcast.83, f32[768,768]{1,0:T(8,128)S(1)} %get-tuple-element.119, f32[768]{0:T(1024)S(1)} %copy-done.21, f32[768]{0:T(1024)S(1)} %copy-done.14, f32[768]{0:T(1024)S(1)} %fusion.16, f32[768]{0:T(1024)S(1)} %broadcast_multiply_fusion.1), kind=kOutput, calls=%fused_computation.18 | convolution fusion | flops 3629187072 | bytes 11808768 | tf_op jit(solution)/shard_map/dot_general | solution.py:1420
  274.3 1.1 fusion.11
  275.5 1.8 copy.37
  277.3 6.3 %fusion.12 = bf16[768,576]{0,1:T(8,128)(2,1)S(1)} fusion(bf16[576,3072]{1,0:T(8,128)(2,1)} %get-tuple-element.63, bf16[3072,768]{1,0:T(8,128)(2,1)} %tok_ref.1), kind=kOutput, calls=%fused_computation.47 | convolution fusion | flops 2718351360 | bytes 9142272 | tf_op jit(solution)/shard_map/dot_general | solution.py:1430
  283.6 1.3 copy.38
  285.5 1.2 slice.61
  286.7 0.6 fusion.18
  287.9 0.7 concatenate.13
  288.6 0.6 reshape.192.small_ref
  289.3 137.4 %tail.1 = (f32[768,768]{1,0:T(8,128)}, f32[96,768]{1,0:T(8,128)}, f32[96,768]{1,0:T(8,128)}, f32[96,192]{1,0:T(8,128)}, f32[96,576]{1,0:T(8,128)}, /*index=5*/f32[6,16,768]{2,1,0:T(8,128)}) custom-call(bf16[4,4,192,768]{3,2,1,0:T(8,128)(2,1)} %bitcast.56, f32[768,768]{1,0:T(8,128)} %copy-done.2, bf16[8,4,96,768]{3,2,1,0:T(8,128)(2,1)} %bitcast.57, ...), custom_call_target="tpu_custom_call" | custom-call | tf_op jit(solution)/shard_map/tail/pallas_call | solution.py:1301
  426.7 1.1 copy.40
  427.8 0.9 copy.41
  428.7 0.7 slice.62
  429.4 0.7 dynamic-slice_bitcast_fusion.1
  430.1 0.8 slice.63
  431.0 0.6 constant_dynamic-slice_fusion.1
  431.5 1.6 copy.42
  433.8 0.8 slice.65
  434.6 0.7 dynamic-slice_bitcast_fusion
  435.2 0.6 fusion.27
  437.2 3.3 copy.50
  440.5 0.7 copy.51
  441.2 0.7 copy.52
  (86 shorter events, 3.1 us)
Async XLA Ops:
  0.6 34.2 %copy-start = (bf16[192,768]{1,0:T(8,128)(2,1)S(1)}, bf16[192,768]{1,0:T(8,128)(2,1)}, u32[]{:S(2)}) copy-start(bf16[192,768]{1,0:T(8,128)(2,1)} %param.24) | copy-start | bytes 884740
  3.7 31.2 %copy-start.17 = (bf16[96]{0:T(256)(128)(2,1)S(1)}, bf16[96]{0:T(256)(128)(2,1)}, u32[]{:S(2)}) copy-start(bf16[96]{0:T(256)(128)(2,1)} %param.29) | copy-start | bytes 580
  121.3 2.5 copy-start.19
  123.8 34.3 %slice-start.2 = ((s8[4718592]{0:T(1024)(128)(4,1)}), s8[4194304]{0:T(1024)(128)(4,1)S(1)}, s32[]{:S(2)}) async-start(s8[4718592]{0:T(1024)(128)(4,1)} %bitcast.77), calls=%async_computation.2 | async-start | bytes 8388608
  127.2 0.7 copy-start.14
  127.2 0.7 copy-start.21
  127.9 30.2 %slice-start.3 = ((s8[4718592]{0:T(1024)(128)(4,1)}), s8[524288]{0:T(1024)(128)(4,1)S(1)}, s32[]{:S(2)}) async-start(s8[4718592]{0:T(1024)(128)(4,1)} %bitcast.77), calls=%async_computation.3 | async-start | bytes 1048576
  127.9 30.2 %copy-start.20 = (f32[768]{0:T(1024)S(1)}, f32[768]{0:T(1024)}, u32[]{:S(2)}) copy-start(f32[768]{0:T(1024)} %param.31) | copy-start | bytes 9220
  155.9 2.3 copy-start.22
  162.2 1.3 copy-start.4
  162.2 1.3 copy-start.12
  162.7 1.8 copy-start.13
  164.5 15.4 %slice-start = ((s8[4718592]{0:T(1024)(128)(4,1)}), s8[524288]{0:T(1024)(128)(4,1)S(1)}, s32[]{:S(2)}) async-start(s8[4718592]{0:T(1024)(128)(4,1)} %bitcast.74), calls=%async_computation | async-start | bytes 1048576
  166.9 13.0 %copy-start.5 = (bf16[768,768]{1,0:T(8,128)(2,1)}, bf16[768,768]{1,0:T(8,128)(2,1)S(1)}, u32[]{:S(2)}) copy-start(bf16[768,768]{1,0:T(8,128)(2,1)S(1)} %get-tuple-element.104) | copy-start | bytes 3538948
  166.9 13.0 %slice-start.1 = ((s8[4718592]{0:T(1024)(128)(4,1)}), s8[4194304]{0:T(1024)(128)(4,1)S(1)}, s32[]{:S(2)}) async-start(s8[4718592]{0:T(1024)(128)(4,1)} %bitcast.74), calls=%async_computation.1 | async-start | bytes 8388608
  187.2 1.7 copy-start.7
  187.5 1.4 copy-start.2
  215.9 36.3 %copy-start.8 = (bf16[768,3,192]{0,2,1:T(8,128)(2,1)S(1)}, bf16[768,3,192]{0,2,1:T(8,128)(2,1)}, u32[]{:S(2)}) copy-start(bf16[768,3,192]{0,2,1:T(8,128)(2,1)} %param.21) | copy-start | bytes 2654212
  252.2 7.9 %copy-start.6 = (bf16[768,768]{1,0:T(8,128)(2,1)S(1)}, bf16[768,768]{1,0:T(8,128)(2,1)}, u32[]{:S(2)}) copy-start(bf16[768,768]{1,0:T(8,128)(2,1)} %copy-done.5) | copy-start | bytes 3538948
  252.2 15.9 %slice-start.4 = ((s8[4718592]{0:T(1024)(128)(4,1)}), s8[4194304]{0:T(1024)(128)(4,1)S(1)}, s32[]{:S(2)}) async-start(s8[4718592]{0:T(1024)(128)(4,1)} %bitcast.82), calls=%async_computation.4 | async-start | bytes 8388608
  260.2 8.0 %slice-start.5 = ((s8[4718592]{0:T(1024)(128)(4,1)}), s8[524288]{0:T(1024)(128)(4,1)S(1)}, s32[]{:S(2)}) async-start(s8[4718592]{0:T(1024)(128)(4,1)} %bitcast.82), calls=%async_computation.5 | async-start | bytes 1048576
  268.2 6.2 %copy-start.3 = (f32[768,768]{1,0:T(8,128)S(1)}, f32[768,768]{1,0:T(8,128)}, u32[]{:S(2)}) copy-start(f32[768,768]{1,0:T(8,128)} %copy-done.2) | copy-start | bytes 7077892
  268.2 6.2 %copy-start.18 = (bf16[4,192,768]{2,1,0:T(8,128)(2,1)S(1)}, bf16[4,192,768]{2,1,0:T(8,128)(2,1)}, u32[]{:S(2)}) copy-start(bf16[4,192,768]{2,1,0:T(8,128)(2,1)} %get-tuple-element.49) | copy-start | bytes 3538948
  277.2 7.7 %copy-start.11 = (f32[192,2]{1,0:T(8,128)S(1)}, f32[192,2]{1,0:T(8,128)}, u32[]{:S(2)}) copy-start(f32[192,2]{1,0:T(8,128)} %get-tuple-element.64) | copy-start | bytes 4612
  277.3 8.0 %copy-start.16 = (f32[3,128]{1,0:T(4,128)S(1)}, f32[3,128]{1,0:T(4,128)}, u32[]{:S(2)}) copy-start(f32[3,128]{1,0:T(4,128)} %get-tuple-element.65) | copy-start | bytes 4612
  277.3 9.4 %copy-start.15 = (s32[3]{0:T(128)S(1)}, s32[3]{0:T(128)}, u32[]{:S(2)}) copy-start(s32[3]{0:T(128)} %len_ref.3) | copy-start | bytes 40
  437.2 4.8 %copy-start.1 = (bf16[192,768]{1,0:T(8,128)(2,1)S(1)}, bf16[192,768]{1,0:T(8,128)(2,1)}, u32[]{:S(2)}) copy-start(bf16[192,768]{1,0:T(8,128)(2,1)} %param.24) | copy-start | bytes 884740
  437.2 3.3 copy-start.10
  437.2 4.0 copy-start.9

commit v3 on v2

--- a/solution.py
+++ b/solution.py
@@ -621,6 +621,9 @@
             ],
         ),
         compiler_params=pltpu.CompilerParams(vmem_limit_bytes=56 * 1024 * 1024),
+        cost_estimate=pl.CostEstimate(
+            flops=20 * 10**9, bytes_accessed=30 * 10**6, transcendentals=10**6
+        ),
         name="mix_forward",
     )(seq_lengths, tokens, weight_t, bias_col, conv_own)
 
@@ -655,6 +658,9 @@
             ],
         ),
         compiler_params=pltpu.CompilerParams(vmem_limit_bytes=56 * 1024 * 1024),
+        cost_estimate=pl.CostEstimate(
+            flops=20 * 10**9, bytes_accessed=30 * 10**6, transcendentals=10**6
+        ),
         name="mix_backward",
     )(seq_lengths, *args)
 
@@ -864,231 +870,6 @@
     pl.semaphore_wait(barrier, len(devices))
 
 
-def exchange_kernel(
-    pieces,
-    mixed_ref, in_ref, down_ref, misc_ref,
-    all_ref, in_all, down_all, misc_all,
-    a_send, a_recv, l_send, l_recv, p_send, p_recv, own_sem,
-):
-    b, z, bc, bx, by = place()
-    peers = [(b, lax.rem(z + i, 4)) for i in (1, 2, 3)]
-    greet(peers + [(bc, z), (bx, z), (by, z)])
-    quarter = all_ref.shape[2]
-    owns = (in_ref, down_ref, misc_ref)
-    alls = (in_all, down_all, misc_all)
-
-    local = [
-        pltpu.make_async_copy(own, everything.at[b, z], own_sem.at[n])
-        for n, (own, everything) in enumerate(zip(owns, alls))
-    ]
-
-    def columns(n):
-        return pl.ds(pl.multiple_of(n * quarter, quarter), quarter)
-
-    local.append(
-        pltpu.make_async_copy(mixed_ref.at[:, columns(z)], all_ref.at[z], own_sem.at[3])
-    )
-    for copy in local:
-        copy.start()
-
-    def line(up, hop, n):
-        array, start, count, _ = pieces[n]
-        rows = pl.ds(start, count)
-        origin = z - hop + 1 if up else z + hop - 1
-        dst = alls[array].at[b, origin, rows]
-        src = owns[array].at[rows] if hop == 1 else dst
-        side = 0 if up else 1
-        return remote(
-            src, dst, l_send.at[side, hop - 1, n], l_recv.at[side, hop - 1, n],
-            (b, z + 1 if up else z - 1),
-        )
-
-    def line_in(up, hop, n):
-        array, start, count, _ = pieces[n]
-        origin = z - hop if up else z + hop
-        dst = alls[array].at[b, origin, pl.ds(start, count)]
-        side = 0 if up else 1
-        return remote(
-            dst, dst, l_send.at[side, hop - 1, n], l_recv.at[side, hop - 1, n],
-            (b, z - 1 if up else z + 1),
-        )
-
-    def has(up, hop):
-        return z >= hop if up else z <= 3 - hop
-
-    def sends(up, hop):
-        return ((z < 3) & (z >= hop - 1)) if up else ((z > 0) & (z <= 4 - hop))
-
-    count = len(pieces)
-    for n in range(count):
-        for up in (True, False):
-
-            @pl.when(sends(up, 1))
-            def _():
-                line(up, 1, n).start()
-
-    def block(n, who):
-        array, start, rows, _ = pieces[n]
-        return alls[array].at[who, :, pl.ds(start, rows)]
-
-    def pair(n, slot, who, device):
-        ref = block(n, who)
-        return remote(ref, ref, p_send.at[n, slot], p_recv.at[n, slot], (device, z))
-
-    both = bx + by - b
-    issued = []
-
-    def first(n):
-        p = by if pieces[n][3] else bx
-        copy = pair(n, 0, b, p)
-        copy.start()
-        issued.append(copy)
-
-    def second(n):
-        p, q = (by, bx) if pieces[n][3] else (bx, by)
-        pair(n, 0, p, p).wait_recv()
-        for slot, who in ((1, b), (2, p)):
-            copy = pair(n, slot, who, q)
-            copy.start()
-            issued.append(copy)
-
-    def third(n):
-        p, q = (by, bx) if pieces[n][3] else (bx, by)
-        pair(n, 1, q, q).wait_recv()
-        pair(n, 2, both, q).wait_recv()
-        for slot, who in enumerate((b, bx, by, both)):
-            copy = pair(n, 3 + slot, who, bc)
-            copy.start()
-            issued.append(copy)
-
-    def fourth(n):
-        flip = bc - b
-        for slot, who in enumerate((b, bx, by, both)):
-            pair(n, 3 + slot, who + flip, bc).wait_recv()
-
-    for copy in local:
-        copy.wait()
-    for n in range(count + 3):
-        if n < count:
-            for hop in (1, 2, 3):
-                for up in (True, False):
-
-                    @pl.when(has(up, hop))
-                    def _():
-                        line_in(up, hop, n).wait_recv()
-
-                    if hop < 3:
-
-                        @pl.when(sends(up, hop + 1))
-                        def _():
-                            line(up, hop + 1, n).start()
-
-            first(n)
-        if n == count - 1:
-            for i, (_, to) in enumerate(peers):
-                copy = remote(
-                    mixed_ref.at[:, columns(to)], all_ref.at[z],
-                    a_send.at[i], a_recv.at[i], (b, to),
-                )
-                copy.start()
-                issued.append(copy)
-        if 0 <= n - 1 < count:
-            second(n - 1)
-        if 0 <= n - 2 < count:
-            third(n - 2)
-        if 0 <= n - 3 < count:
-            fourth(n - 3)
-    for i in (1, 2, 3):
-        source = lax.rem(z + 4 - i, 4)
-        ref = all_ref.at[source]
-        remote(ref, ref, a_send.at[i - 1], a_recv.at[i - 1], (b, source)).wait_recv()
-    for n in range(count):
-        for hop in (1, 2, 3):
-            for up in (True, False):
-
-                @pl.when(sends(up, hop))
-                def _():
-                    line(up, hop, n).wait_send()
-
-    for copy in issued:
-        copy.wait_send()
-
-
-def exchange(mixed_t, in_own, down_own, misc_own):
-    width, tok_count = mixed_t.shape
-    ff, model = in_own.shape
-    misc = misc_own.shape[0]
-    half = ff // 2
-    pieces = (
-        (2, 0, misc, 0),
-        (0, 0, half, 0), (1, 0, half, 1), (0, half, half, 0), (1, half, half, 1),
-    )
-    shape = lambda *s: jax.ShapeDtypeStruct(s, low)
-    vmem = pl.BlockSpec(memory_space=pltpu.VMEM)
-    hbm = pl.BlockSpec(memory_space=pl.ANY)
-    dma = pltpu.SemaphoreType.DMA
-    n = len(pieces)
-    return pl.pallas_call(
-        partial(exchange_kernel, pieces),
-        out_shape=[
-            shape(4, width, tok_count // 4),
-            shape(8, 4, ff, model), shape(8, 4, ff, model), shape(8, 4, misc, model),
-        ],
-        in_specs=[vmem] * 4,
-        out_specs=[hbm] * 4,
-        scratch_shapes=[
-            dma((3,)), dma((3,)), dma((2, 3, n)), dma((2, 3, n)), dma((n, 7)), dma((n, 7)),
-            dma((4,)),
-        ],
-        compiler_params=pltpu.CompilerParams(collective_id=1, has_side_effects=True),
-        name="exchange",
-    )(mixed_t, in_own, down_own, misc_own)
-
-
-def turn_kernel(grad_ref, out_ref, send, recv, own_sem):
-    b, z, _, _, _ = place()
-    peers = [(b, lax.rem(z + i, 4)) for i in (1, 2, 3)]
-    greet(peers)
-    width, quarter = out_ref.shape[0], grad_ref.shape[1]
-
-    def rows(n):
-        return pl.ds(pl.multiple_of(n * width, width), width)
-
-    def columns(n):
-        return pl.ds(pl.multiple_of(n * quarter, quarter), quarter)
-
-    copies = []
-    for i, (_, to) in enumerate(peers):
-        copy = remote(
-            grad_ref.at[rows(to)], out_ref.at[:, columns(z)], send.at[i], recv.at[i], (b, to)
-        )
-        copy.start()
-        copies.append(copy)
-    own = pltpu.make_async_copy(grad_ref.at[rows(z)], out_ref.at[:, columns(z)], own_sem.at[0])
-    own.start()
-    for i in (1, 2, 3):
-        source = lax.rem(z + 4 - i, 4)
-        ref = out_ref.at[:, columns(source)]
-        remote(ref, ref, send.at[i - 1], recv.at[i - 1], (b, source)).wait_recv()
-    for copy in copies:
-        copy.wait_send()
-    own.wait()
-
-
-def turn(grad_all, width):
-    quarter = grad_all.shape[1]
-    dma = pltpu.SemaphoreType.DMA
-    return pl.pallas_call(
-        turn_kernel,
-        out_shape=jax.ShapeDtypeStruct((width, 4 * quarter), low),
-        in_specs=[pl.BlockSpec(memory_space=pltpu.VMEM)],
-        out_specs=pl.BlockSpec(memory_space=pl.ANY),
-        scratch_shapes=[dma((3,)), dma((3,)), dma((1,))],
-        compiler_params=pltpu.CompilerParams(collective_id=2, has_side_effects=True),
-        name="turn",
-    )(grad_all)
-
-
 def tail_kernel(
     part_ref, first_ref, down_ref, up_ref, outw_ref, qkvw_ref, small_ref,
     input_ref, down_own, up_own, outw_own, qkvw_own, small_out,
@@ -1323,6 +1104,293 @@
     )(part.reshape(4, chunks, size, model), first, down, up, outw, qkvw, small)
 
 
+def cumulative(x):
+    t = 1.0 / (1.0 + 0.23164189 * jnp.abs(x))
+    density = jnp.exp(-0.5 * x * x) * 0.3989422804
+    poly = t * (
+        0.319381530 + t * (-0.356563782 + t * (1.781477937 + t * (-1.821255978 + t * 1.330274429)))
+    )
+    upper = density * poly
+    return jnp.where(x >= 0.0, 1.0 - upper, upper), density
+
+
+def normed(x):
+    centre = x - jnp.mean(x, axis=1, keepdims=True)
+    scale = lax.rsqrt(jnp.mean(centre * centre, axis=1, keepdims=True) + norm_eps)
+    return centre * scale, scale
+
+
+def norm_back(grad, gain, rows, scale):
+    e = grad * gain
+    return scale * (
+        e - jnp.mean(e, axis=1, keepdims=True) - rows * jnp.mean(e * rows, axis=1, keepdims=True)
+    )
+
+
+def middle_kernel(
+    pieces, share,
+    mixed_ref, own0, own1, own2, own3, tok_ref, cot_ref, vec_ref,
+    out_ref, first_ref, attn_ref, hidden_ref, pre_ref, norm_ref, ffn_ref, all_ref, grad_ref,
+    sums_ref, bin_ref,
+    packs, wof, wo, slope, total, turned,
+    a_send, a_recv, f_send, f_recv, p_send, p_recv, g_send, g_recv, own_sem, own_turn,
+):
+    b, z, bc, bx, by = place()
+    both = bx + by - b
+    peers = [(b, lax.rem(z + i, 4)) for i in (1, 2, 3)]
+    greet(peers + [(bc, z), (bx, z), (by, z)])
+    width, quarter = all_ref.shape[1:]
+    model = tok_ref.shape[1]
+    owns = (own0, own1, own2, own3)
+    origins = [lax.rem(z + 4 - i, 4) for i in range(4)]
+    issued = []
+
+    def columns(n):
+        return pl.ds(pl.multiple_of(n * quarter, quarter), quarter)
+
+    for i, (_, to) in enumerate(peers):
+        copy = remote(
+            mixed_ref.at[:, columns(to)], all_ref.at[z], a_send.at[i], a_recv.at[i], (b, to)
+        )
+        copy.start()
+        issued.append(copy)
+    local = [
+        pltpu.make_async_copy(own, packs.at[b, origin], own_sem.at[i])
+        for i, (own, origin) in enumerate(zip(owns, origins))
+    ]
+    local.append(
+        pltpu.make_async_copy(mixed_ref.at[:, columns(z)], all_ref.at[z], own_sem.at[4])
+    )
+    count = len(pieces)
+
+    def near(n):
+        return by if pieces[n][2] else bx
+
+    def far(n):
+        return bx if pieces[n][2] else by
+
+    for n in range(count):
+        rows = pl.ds(*pieces[n][:2])
+        for i in range(4):
+            copy = remote(
+                owns[i].at[rows], packs.at[b, origins[i], rows],
+                f_send.at[n, i], f_recv.at[n, i], (near(n), z),
+            )
+            copy.start()
+            issued.append(copy)
+    for copy in local:
+        copy.start()
+
+    def pair(n, slot, who, device):
+        ref = packs.at[who, :, pl.ds(*pieces[n][:2])]
+        return remote(ref, ref, p_send.at[n, slot], p_recv.at[n, slot], (device, z))
+
+    def send(n, slot, who, device):
+        copy = pair(n, slot, who, device)
+        copy.start()
+        issued.append(copy)
+
+    for copy in local:
+        copy.wait()
+    for n in range(count):
+        send(n, 0, b, far(n))
+        send(n, 2, b, bc)
+    for n in range(count):
+        rows = pl.ds(*pieces[n][:2])
+        for i in range(4):
+            ref = packs.at[near(n), origins[i], rows]
+            remote(ref, ref, f_send.at[n, i], f_recv.at[n, i], (near(n), z)).wait_recv()
+        send(n, 1, near(n), far(n))
+        send(n, 3, near(n), bc)
+    for n in range(count):
+        pair(n, 0, far(n), far(n)).wait_recv()
+        send(n, 4, far(n), bc)
+    for n in range(count):
+        pair(n, 1, both, far(n)).wait_recv()
+        send(n, 5, both, bc)
+    flip = bc - b
+    for n in range(count):
+        pair(n, 2, bc, bc).wait_recv()
+        pair(n, 3, near(n) + flip, bc).wait_recv()
+        pair(n, 4, far(n) + flip, bc).wait_recv()
+        pair(n, 5, both + flip, bc).wait_recv()
+    for i in (1, 2, 3):
+        ref = all_ref.at[origins[i]]
+        remote(ref, ref, a_send.at[i - 1], a_recv.at[i - 1], (b, origins[i])).wait_recv()
+
+    ff = (packs.shape[2] - 32) // 2
+    group = 4 * ff
+    for q in range(8):
+        for s in range(4):
+            wof[pl.ds(s * width + q * share, share), :] = packs[
+                q, s, pl.ds(2 * ff, share), :
+            ].astype(f32)
+    wo[...] = wof[...].astype(low).reshape(wo.shape)
+    ff_bias = []
+    for q in range(8):
+        row = jnp.zeros((1, group), f32)
+        for s in range(4):
+            row = row + packs[q, s, 2 * ff + share : 2 * ff + share + 1, :group].astype(f32)
+        ff_bias.append(row)
+    out_bias, gain1, shift1, down_bias, gain2, shift2 = [
+        vec_ref[n : n + 1, :] for n in range(6)
+    ]
+    sums_ref[...] = jnp.zeros_like(sums_ref)
+    bin_ref[...] = jnp.zeros_like(bin_ref)
+    for q in range(8):
+        bin_ref[1:2, q * group : (q + 1) * group] = ff_bias[q]
+    size = turned.shape[2]
+    span = 2 * group
+
+    def weights(c, start):
+        return jnp.concatenate(
+            [
+                packs[2 * c + n, :, pl.ds(start, ff), :].reshape(group, model)
+                for n in range(2)
+            ],
+            axis=0,
+        )
+
+    def row_sum(n, x):
+        sums_ref[n : n + 1, :] += jnp.sum(x, axis=0, keepdims=True)
+
+    def turn_copy(r, i):
+        to = lax.rem(z + i, 4)
+        src = turned.at[r, pl.ds(pl.multiple_of(to * width, width), width)]
+        dst = grad_ref.at[:, pl.ds(pl.multiple_of(z * quarter + r * size, size), size)]
+        return remote(src, dst, g_send.at[r, i - 1], g_recv.at[r, i - 1], (b, to))
+
+    def turn_own(r):
+        src = turned.at[r, pl.ds(pl.multiple_of(z * width, width), width)]
+        dst = grad_ref.at[:, pl.ds(pl.multiple_of(z * quarter + r * size, size), size)]
+        return pltpu.make_async_copy(src, dst, own_turn.at[r])
+
+    def row_tile(r, _):
+        at = pl.multiple_of(r * size, size)
+        rows = pl.ds(at, size)
+        attn = jnp.zeros((size, model), f32)
+        for s in range(4):
+            attn = attn + lax.dot_general(
+                all_ref[s, :, rows], wo[s], (((0,), (0,)), ((), ())), preferred_element_type=f32
+            )
+        n1, scale1 = normed(tok_ref[rows, :].astype(f32) + attn + out_bias)
+        norm1 = n1 * gain1 + shift1
+        norm_low = norm1.astype(low)
+        norm_ref[rows, :] = norm_low
+        total[...] = jnp.zeros_like(total)
+
+        def forward(c, _):
+            lanes = pl.ds(pl.multiple_of(c * span, span), span)
+            act = mul_t(norm_low, weights(c, 0)) + bin_ref[1:2, lanes]
+            phi, density = cumulative(act)
+            hidden = (act * phi).astype(low)
+            hidden_ref[rows, lanes] = hidden
+            slope[:, lanes] = phi + act * density
+            total[...] += mul(hidden, weights(c, ff))
+            return 0
+
+        lax.fori_loop(0, 4, forward, 0)
+        n2, scale2 = normed(norm1 + total[...] + down_bias)
+        out_ref[rows, :] = (n2 * gain2 + shift2).astype(low)
+        cot = cot_ref[rows, :].astype(f32)
+        row_sum(1, cot * n2)
+        row_sum(2, cot)
+        grad2 = norm_back(cot, gain2, n2, scale2)
+        grad_low = grad2.astype(low)
+        ffn_ref[rows, :] = grad_low
+        row_sum(0, grad_low.astype(f32))
+        total[...] = grad2
+
+        def backward(c, _):
+            lanes = pl.ds(pl.multiple_of(c * span, span), span)
+            grad = (slope[:, lanes] * mul_t(grad_low, weights(c, ff))).astype(low)
+            pre_ref[rows, lanes] = grad
+            bin_ref[0:1, lanes] += jnp.sum(grad.astype(f32), axis=0, keepdims=True)
+            total[...] += mul(grad, weights(c, 0))
+            return 0
+
+        lax.fori_loop(0, 4, backward, 0)
+        grad1 = total[...]
+        row_sum(3, grad1 * n1)
+        row_sum(4, grad1)
+        first = norm_back(grad1, gain1, n1, scale1)
+        first_ref[rows, :] = first
+        attn_low = first.astype(low)
+        attn_ref[rows, :] = attn_low
+        row_sum(5, attn_low.astype(f32))
+        for s in range(4):
+            turned[r, pl.ds(s * width, width), :] = mul_t(wo[s], attn_low).astype(low)
+        for i in (1, 2, 3):
+            turn_copy(r, i).start()
+        turn_own(r).start()
+        return 0
+
+    tiles = quarter // size
+    lax.fori_loop(0, tiles, row_tile, 0)
+
+    def finish(r, _):
+        for i in (1, 2, 3):
+            source = origins[i]
+            ref = grad_ref.at[:, pl.ds(pl.multiple_of(source * quarter + r * size, size), size)]
+            remote(ref, ref, g_send.at[r, i - 1], g_recv.at[r, i - 1], (b, source)).wait_recv()
+            turn_copy(r, i).wait_send()
+        turn_own(r).wait()
+        return 0
+
+    lax.fori_loop(0, tiles, finish, 0)
+    for copy in issued:
+        copy.wait_send()
+
+
+def ffn_middle(mixed_t, packs, tok, cot, vectors, ff, share):
+    width, tok_count = mixed_t.shape
+    quarter, model = tok.shape
+    size = quarter // 3
+    rows = packs[0].shape[0]
+    half = ff // 2
+    pieces = (
+        (2 * ff, rows - 2 * ff, 0),
+        (0, half, 0), (ff, half, 1), (half, half, 0), (ff + half, half, 1),
+    )
+    n = len(pieces)
+    shape = jax.ShapeDtypeStruct
+    vmem = pl.BlockSpec(memory_space=pltpu.VMEM)
+    hbm = pl.BlockSpec(memory_space=pl.ANY)
+    dma = pltpu.SemaphoreType.DMA
+    return pl.pallas_call(
+        partial(middle_kernel, pieces, share),
+        out_shape=[
+            shape((quarter, model), low),
+            shape((quarter, model), f32),
+            shape((quarter, model), low),
+            shape((quarter, 32 * ff), low),
+            shape((quarter, 32 * ff), low),
+            shape((quarter, model), low),
+            shape((quarter, model), low),
+            shape((4, width, quarter), low),
+            shape((width, tok_count), low),
+            shape((8, model), f32),
+            shape((8, 32 * ff), f32),
+        ],
+        in_specs=[hbm] + [vmem] * 7,
+        out_specs=[vmem] * 8 + [hbm] + [vmem] * 2,
+        scratch_shapes=[
+            pltpu.VMEM((8, 4, rows, model), low),
+            pltpu.VMEM((4 * width, model), f32),
+            pltpu.VMEM((4, width, model), low),
+            pltpu.VMEM((size, 32 * ff), f32),
+            pltpu.VMEM((size, model), f32),
+            pltpu.VMEM((3, 4 * width, size), low),
+            dma((3,)), dma((3,)), dma((n, 4)), dma((n, 4)), dma((n, 6)), dma((n, 6)),
+            dma((3, 3)), dma((3, 3)), dma((5,)), dma((3,)),
+        ],
+        compiler_params=pltpu.CompilerParams(
+            collective_id=1, has_side_effects=True, vmem_limit_bytes=62 * 1024 * 1024
+        ),
+        name="middle",
+    )(mixed_t, *packs, tok, cot, vectors)
+
+
 def slice_body(
     tokens,
     qkv_weight,
@@ -1351,62 +1419,44 @@
     quarter = tok_count // 4
     z = lax.axis_index("heads")
     b = lax.axis_index("batch")
-    own_tokens = lax.dynamic_slice_in_dim(tokens, z * quarter, quarter, 0).astype(f32)
+    own_low = lax.dynamic_slice_in_dim(tokens, z * quarter, quarter, 0)
     conv_own = lax.dynamic_slice_in_dim(conv_weight, z * heads_here, heads_here, 0)
     qv_own = lax.dynamic_slice_in_dim(qv_bias, z * width, width, 1)
     flat_qkv = qkv_weight.reshape(model, 3 * width)
     bias_col = jnp.concatenate([qv_own[0], jnp.zeros_like(qv_own[0]), qv_own[1]])[:, None]
-    forward = mix_forward(
-        seq_lengths, tokens, jnp.transpose(flat_qkv), bias_col, conv_own, slots, marks
-    )
-    qkv_t, first, last, mixed_t, mark, value, inner, denom, middle, steps, inverse, bound = forward
     ff_own = ffn_out_weight.shape[0]
     share = width // 8
-    misc_rows = 32
+    bias_row = lax.dynamic_update_slice_in_dim(
+        jnp.zeros((4 * ff_own,), low), ffn_in_bias, z * ff_own, 0
+    )
     misc_own = jnp.concatenate(
         [
             lax.dynamic_slice_in_dim(out_weight, b * share, share, 0),
-            jnp.zeros((misc_rows - share, model), low).at[0, :ff_own].set(ffn_in_bias),
+            jnp.zeros((32 - share, model), low).at[0, : 4 * ff_own].set(bias_row),
         ],
         axis=0,
     )
-    mixed_all, in_all, down_all, misc_all = exchange(
-        mixed_t, jnp.transpose(ffn_in_weight), ffn_out_weight, misc_own
-    )
-    mixed_all = mixed_all.reshape(4 * width, quarter)
-    whole_in = in_all.reshape(-1, model)
-    whole_down = down_all.reshape(-1, model)
-    whole_out = jnp.swapaxes(misc_all[:, :, :share], 0, 1).reshape(4 * width, model)
-    whole_bias = misc_all[:, :, share, :ff_own].reshape(-1).astype(f32)
-
-    attn = lax.dot_general(mixed_all, whole_out, contract_rows, preferred_element_type=f32)
-    first_res = own_tokens + attn + out_bias[None, :]
-    norm1_out, norm1_pull = jax.vjp(layer_norm, first_res, norm1_gain, norm1_bias)
-    norm1_low = norm1_out.astype(low)
-    pre_act = (
-        lax.dot_general(norm1_low, whole_in, contract_cols, preferred_element_type=f32)
-        + whole_bias[None, :]
-    )
-    hidden_act, gelu_pull = jax.vjp(gelu_exact, pre_act)
-    hidden_low = hidden_act.astype(low)
-    ffn_result = jnp.dot(hidden_low, whole_down, preferred_element_type=f32) + ffn_out_bias[None, :]
-    final_out, norm2_pull = jax.vjp(layer_norm, norm1_out + ffn_result, norm2_gain, norm2_bias)
-    grad_second, grad_gain_two, grad_shift_two = norm2_pull(cotangent.astype(f32))
-    grad_ffn_low = grad_second.astype(low)
-    grad_ffn_bias = jnp.sum(grad_ffn_low.astype(f32), axis=0)
-    grad_hidden = lax.dot_general(
-        grad_ffn_low, whole_down, contract_cols, preferred_element_type=f32
-    )
-    grad_pre = gelu_pull(grad_hidden)[0].astype(low)
-    grad_in_bias = jnp.sum(grad_pre.astype(f32), axis=0)
-    grad_norm1 = grad_second + jnp.dot(grad_pre, whole_in, preferred_element_type=f32)
-    grad_first, grad_gain_one, grad_shift_one = norm1_pull(grad_norm1)
-    grad_attn_low = grad_first.astype(low)
-    grad_out_bias = jnp.sum(grad_attn_low.astype(f32), axis=0)
-    grad_mix_all = lax.dot_general(
-        whole_out, grad_attn_low, contract_cols, preferred_element_type=f32
-    ).astype(low)
-    grad_mix_t = turn(grad_mix_all, width)
+    pack = jnp.concatenate([jnp.transpose(ffn_in_weight), ffn_out_weight, misc_own], axis=0)
+    packs = [pack] + [
+        lax.ppermute(pack, "heads", [(n, (n + i) % 4) for n in range(4)]) for i in (1, 2, 3)
+    ]
+    forward = mix_forward(
+        seq_lengths, tokens, jnp.transpose(flat_qkv), bias_col, conv_own, slots, marks
+    )
+    qkv_t, first, last, mixed_t, mark, value, inner, denom, middle, steps, inverse, bound = forward
+    vectors = jnp.concatenate(
+        [
+            jnp.stack(
+                [out_bias, norm1_gain, norm1_bias, ffn_out_bias, norm2_gain, norm2_bias]
+            ),
+            jnp.zeros((2, model), f32),
+        ]
+    )
+    (
+        final_low, grad_first, grad_attn_low, hidden_low, grad_pre, norm1_low, grad_ffn_low,
+        mixed_all, grad_mix_t, vector_sums, bias_sums,
+    ) = ffn_middle(mixed_t, packs, own_low, cotangent, vectors, ff_own, share)
+    grad_in_bias = bias_sums[0]
     saved = (qkv_t, first, last, mark, value, inner, denom, middle, steps, inverse)
     grad_t, grad_bias, grad_conv = mix_backward(
         seq_lengths, grad_mix_t, saved, conv_own, slots, marks
@@ -1422,7 +1472,7 @@
     ).astype(low)
     out_term = lax.dot_general(
         grad_attn_low,
-        mixed_all.reshape(4, width, quarter),
+        mixed_all,
         (((0,), (2,)), ((), ())),
         preferred_element_type=f32,
     ).astype(low)
@@ -1434,8 +1484,7 @@
     flat = jnp.concatenate(
         [
             grad_in_bias,
-            grad_ffn_bias, grad_gain_two, grad_shift_two,
-            grad_gain_one, grad_shift_one, grad_out_bias,
+            vector_sums[:6].reshape(-1),
         ]
     )
     head_total = conv_weight.shape[0]
@@ -1475,7 +1524,7 @@
     at = at + head_total * kernel_taps
     condition = sums[at] / sums[at + 1]
     return (
-        final_out.astype(low),
+        final_low,
         input_grad,
         qkv_share.reshape(model // 8, 3, width),
         bias_out,

time: 446 us -> 383 us (0.86)
  matrix products: 86.5 us -> 28.6 us
  starting transfers between devices: 0 us -> 7.1 us
  Pallas kernels: 314 us -> 308 us
  other arithmetic: 7.56 us -> 1.69 us
    dot_general x7 -> x1, matrix products: 58.1 us -> 2.36 us  [slice_body(): lax.dot_general(grad_attn_low, mixed_all, (((0,), (2,)), ((), ())), prefe...]
    pallas_call x2 -> x1, Pallas kernels: 110 us -> 101 us  [ffn_middle(): pl.pallas_call(partial(middle_kernel, pieces, share), out_shape=[shape((q...]
    ppermute x0 -> x3, starting transfers between devices: none -> 7.1 us  [slice_body(): lax.ppermute(pack, 'heads', [(n, (n + i) % 4) for n in range(4)])]
    reduce_sum x7 -> x0, other arithmetic: 5.31 us -> none  [the longest x2 2.99 us: layer_norm(): centre = row_data - jnp.mean(row_data, axis=1, keepdims=True)]
    unnamed x63 -> x56, local copies, waits for them, and re-layouts: 12.1 us -> 8.33 us
  transfers between devices with their start and end apart: 0 -> 3, of which waited for: 0 -> 0; matrix products, arithmetic and copies ran while one was open for 0% -> 2% of each run, Pallas kernels for 0% -> 8%
where the time goes in v3:
time: 383 us; the launch traced here: 380 us
  Pallas kernels  308 us (80%)
  local copies, waits for them, and re-layouts  30.1 us (8%)
  matrix products  28.6 us (7%)
  starting transfers between devices  7.1 us (2%)
  between operations  4.19 us (1%)
    pallas_call x1, Pallas kernels, tail(): pl.pallas_call(tail_kernel, out_shape=[own(quarter, model), own(ff, model...  137 us
    pallas_call x1, Pallas kernels, ffn_middle(): pl.pallas_call(partial(middle_kernel, pieces, share), out_shape=[shape((q...  101 us
    pallas_call x1, Pallas kernels, mix_backward(): pl.pallas_call(partial(mix_backward_kernel, slots, marks, taps), out_shap...  37.7 us
    pallas_call x1, Pallas kernels, mix_forward(): pl.pallas_call(partial(mix_forward_kernel, slots, marks, taps), out_shape...  32.1 us
    unnamed x56, local copies, waits for them, and re-layouts  8.33 us
    dot_general x1, matrix products, slice_body(): lax.dot_general(grad_pre, norm1_low, contract_rows, preferred_element_typ...  8.22 us
  transfers between devices with their start and end apart: 3, of which 0 were waited for; matrix products, arithmetic and copies ran while one was open for 2% of the time, Pallas kernels for 8%

profile of v3, /device:TPU:0, one launch (start us, length us, event | category | flops | bytes accessed | tf_op | source)
XLA Modules:
  0.0 379.7 jit_solution(6917287553668734416)
XLA Ops:
  0.7 0.9 copy-done
  1.6 0.8 dynamic_update_slice.12
  2.4 1.0 fusion.4.own0
  3.4 3.2 collective-permute-start
  6.6 2.6 collective-permute-start.1
  9.2 1.4 collective-permute-start.2
  10.5 0.8 constant_dynamic-slice_fusion
  11.4 0.9 broadcast_in_dim.17.bias_ref
  12.3 1.3 constant_dynamic-slice_fusion.4.conv_ref
  13.6 32.1 %mix_forward.1 = (bf16[576,3072]{1,0:T(8,128)(2,1)}, bf16[192,3072]{1,0:T(8,128)(2,1)}, bf16[192,3072]{1,0:T(8,128)(2,1)}, bf16[192,3072]{1,0:T(8,128)(2,1)}, f3...) custom-call(s32[3]{0:T(128)} %len_ref.3, ...), custom_call_target="tpu_custom_call" | custom-call | flops 20000000000 | bytes 30000000 | tf_op jit(solution)/shard_map/mix_forward/pallas_call | solution.py:604
  45.9 1.2 slice.61
  47.1 0.6 fusion.5
  48.4 0.6 concatenate.16.vec_ref
  49.0 2.4 constant_dynamic-slice_fusion.2.tok_ref
  51.4 0.7 copy-done.5
  52.1 0.1 copy-done.6
  52.3 0.1 copy-done.7
  52.4 100.8 %middle.1 = (bf16[768,768]{1,0:T(8,128)(2,1)}, f32[768,768]{1,0:T(8,128)}, bf16[768,768]{1,0:T(8,128)(2,1)}, bf16[768,3072]{1,0:T(8,128)(2,1)}, bf16[768,3072]{1...) custom-call(bf16[192,3072]{1,0:T(8,128)(2,1)} %get-tuple-element.55., ...), custom_call_target="tpu_custom_call" | custom-call | tf_op jit(solution)/shard_map/middle/pallas_call | solution.py:1360
  153.2 37.7 %mix_backward.1 = (bf16[576,3072]{1,0:T(8,128)(2,1)}, f32[192,2]{1,0:T(8,128)}, f32[3,128]{1,0:T(4,128)}) custom-call(s32[3]{0:T(128)} %len_ref.3, bf16[192,3072]{1,0:T(8,128)(2,1)} %get-tuple-element.57.grad_ref, bf16[576,3072]{1,0:T(8,128)(2,1)} %get-tuple-element.58.qkv_ref, bf16[192,3072]{1,0:T(8,128)(2,1)} %get-tuple-element.59.first_ref, ...), custom_call_target="tpu_custom_call" | custom-call | flops 20000000000 | bytes 30000000 | tf_op jit(solution)/shard_map/mix_backward/pallas_call | solution.py:643
  191.0 1.0 copy.35
  191.9 0.1 dynamic_update_slice.13
  192.1 0.8 dynamic_update_slice.14
  193.0 0.9 slice.58
  193.9 0.7 concatenate.17
  194.6 0.6 reshape.111.small_ref
  195.3 2.4 fusion
  197.6 1.5 copy.33
  199.2 6.4 %fusion.1 = bf16[768,576]{0,1:T(8,128)(2,1)S(1)} fusion(bf16[576,3072]{1,0:T(8,128)(2,1)} %get-tuple-element.68, bf16[3072,768]{1,0:T(8,128)(2,1)} %tok_ref.1), kind=kOutput, calls=%fused_computation.6 | convolution fusion | flops 2718351360 | bytes 9142272 | tf_op jit(solution)/shard_map/dot_general | solution.py:1480
  205.7 5.9 %convolution_convert_fusion.2 = bf16[3072,768]{1,0:T(8,128)(2,1)} fusion(bf16[576,3072]{1,0:T(8,128)(2,1)S(1)} %copy-done.22, bf16[768,576]{0,1:T(8,128)(2,1)S(1)} %bitcast.61), kind=kOutput, calls=%fused_computation.2 | convolution fusion | flops 2720268288 | bytes 9142272 | tf_op jit(solution)/shard_map/dot_general | solution.py:1464
  211.6 1.3 copy.34
  212.9 8.2 %convolution_convert_fusion = bf16[3072,768]{1,0:T(8,128)(2,1)} fusion(bf16[768,3072]{1,0:T(8,128)(2,1)} %get-tuple-element.72, bf16[768,768]{1,0:T(8,128)(2,1)S(1)} %copy-done.18), kind=kOutput, calls=%fused_computation | convolution fusion | flops 3626237952 | bytes 10616832 | tf_op jit(solution)/shard_map/dot_general | solution.py:1470
  221.1 5.6 %convolution_convert_fusion.1 = bf16[3072,768]{1,0:T(8,128)(2,1)} fusion(bf16[768,3072]{1,0:T(8,128)(2,1)S(1)} %bitcast.59, bf16[768,768]{1,0:T(8,128)(2,1)S(1)} %copy-done.17), kind=kOutput, calls=%fused_computation.1 | convolution fusion | flops 3626237952 | bytes 10616832 | tf_op jit(solution)/shard_map/dot_general | solution.py:1467
  226.8 137.3 %tail.1 = (f32[768,768]{1,0:T(8,128)}, f32[96,768]{1,0:T(8,128)}, f32[96,768]{1,0:T(8,128)}, f32[96,192]{1,0:T(8,128)}, f32[96,576]{1,0:T(8,128)}, /*index=5*/f32[6,16,768]{2,1,0:T(8,128)}) custom-call(bf16[4,4,192,768]{3,2,1,0:T(8,128)(2,1)} %bitcast.43, f32[768,768]{1,0:T(8,128)} %get-tuple-element.69.first_ref, bf16[8,4,96,768]{3,2,1,0:T(8,128)(2,1)} %bitcast.45, ...), custom_call_target="tpu_custom_call" | custom-call | tf_op jit(solution)/shard_map/tail/pallas_call | solution.py:1082
  364.1 0.9 slice.63
  365.0 0.6 fusion.6
  365.6 0.8 slice.65
  366.4 0.7 slice.62
  367.1 1.1 copy.36
  368.2 0.9 copy.37
  369.1 0.6 constant_dynamic-slice_fusion.1
  369.7 0.6 dynamic_slice.35
  370.3 1.6 copy.38
  372.0 0.7 dynamic-slice_bitcast_fusion.1
  374.0 0.7 dynamic-slice_bitcast_fusion
  374.7 1.0 copy.46
  375.7 1.4 copy.47
  377.1 0.7 copy.48
  377.8 0.7 copy.49
  (69 shorter events, 0.4 us)
Async XLA Ops:
  0.6 1.0 copy-start
  3.4 42.3 %copy-start.3 = (bf16[224,768]{1,0:T(8,128)(2,1)}, bf16[224,768]{1,0:T(8,128)(2,1)S(1)}, u32[]{:S(2)}) copy-start(bf16[224,768]{1,0:T(8,128)(2,1)S(1)} %fusion.4.own0) | copy-start | bytes 1032196
  3.4 48.0 %collective-permute-start = (bf16[224,768]{1,0:T(8,128)(2,1)S(1)}, bf16[224,768]{1,0:T(8,128)(2,1)S(1)}, u32[]{:S(2)}, u32[]{:S(2)}) collective-permute-start(bf16[224,768]{1,0:T(8,128)(2,1)S(1)} %fusion.4.own0), channel_id=1, source_target_pairs={{0,1},{1,2},{2,3},{3,0},{4,5},{5,6},{6,7},{7,4},{8,9},{9,10},{10,1... | collective-permute-start | bytes 1032200 | tf_op jit(solution)/shard_map/ppermute | solution.py:1441
  6.6 44.8 %collective-permute-start.1 = (bf16[224,768]{1,0:T(8,128)(2,1)S(1)}, bf16[224,768]{1,0:T(8,128)(2,1)S(1)}, u32[]{:S(2)}, u32[]{:S(2)}) collective-permute-start(bf16[224,768]{1,0:T(8,128)(2,1)S(1)} %fusion.4.own0), channel_id=1, source_target_pairs={{0,2},{1,3},{2,0},{3,1},{4,6},{5,7},{6,4},{7,5},{8,10},{9,11},{10,... | collective-permute-start | bytes 1032200 | tf_op jit(solution)/shard_map/ppermute | solution.py:1441
  9.2 42.2 %collective-permute-start.2 = (bf16[224,768]{1,0:T(8,128)(2,1)S(1)}, bf16[224,768]{1,0:T(8,128)(2,1)S(1)}, u32[]{:S(2)}, u32[]{:S(2)}) collective-permute-start(bf16[224,768]{1,0:T(8,128)(2,1)S(1)} %fusion.4.own0), channel_id=1, source_target_pairs={{0,3},{1,0},{2,1},{3,2},{4,7},{5,4},{6,5},{7,6},{8,11},{9,8},{10,9... | collective-permute-start | bytes 1032200 | tf_op jit(solution)/shard_map/ppermute | solution.py:1441
  13.6 32.2 %copy-start.11 = (f32[768]{0:T(1024)S(1)}, f32[768]{0:T(1024)}, u32[]{:S(2)}) copy-start(f32[768]{0:T(1024)} %param.25) | copy-start | bytes 9220
  13.6 32.2 %copy-start.12 = (f32[768]{0:T(1024)S(1)}, f32[768]{0:T(1024)}, u32[]{:S(2)}) copy-start(f32[768]{0:T(1024)} %param.26) | copy-start | bytes 9220
  13.6 32.2 %copy-start.13 = (f32[768]{0:T(1024)S(1)}, f32[768]{0:T(1024)}, u32[]{:S(2)}) copy-start(f32[768]{0:T(1024)} %param.27) | copy-start | bytes 9220
  13.6 32.3 %copy-start.14 = (f32[768]{0:T(1024)S(1)}, f32[768]{0:T(1024)}, u32[]{:S(2)}) copy-start(f32[768]{0:T(1024)} %param.31) | copy-start | bytes 9220
  13.6 32.3 %copy-start.15 = (f32[768]{0:T(1024)S(1)}, f32[768]{0:T(1024)}, u32[]{:S(2)}) copy-start(f32[768]{0:T(1024)} %param.32) | copy-start | bytes 9220
  13.6 32.3 %copy-start.16 = (f32[768]{0:T(1024)S(1)}, f32[768]{0:T(1024)}, u32[]{:S(2)}) copy-start(f32[768]{0:T(1024)} %param.33) | copy-start | bytes 9220
  13.6 33.5 %copy-start.21 = (s32[3]{0:T(128)S(1)}, s32[3]{0:T(128)}, u32[]{:S(2)}) copy-start(s32[3]{0:T(128)} %len_ref.3) | copy-start | bytes 40
  51.4 0.7 copy-start.5
  51.4 0.9 copy-start.6
  51.4 0.9 copy-start.7
  153.2 39.8 %copy-start.10 = (f32[8,768]{1,0:T(8,128)S(1)}, f32[8,768]{1,0:T(8,128)}, u32[]{:S(2)}) copy-start(f32[8,768]{1,0:T(8,128)} %get-tuple-element.77) | copy-start | bytes 73732
  153.2 42.1 %copy-start.19 = (bf16[768,768]{1,0:T(8,128)(2,1)S(1)}, bf16[768,768]{1,0:T(8,128)(2,1)}, u32[]{:S(2)}) copy-start(bf16[768,768]{1,0:T(8,128)(2,1)} %get-tuple-element.74) | copy-start | bytes 3538948
  199.2 6.5 %copy-start.20 = (bf16[768,3,192]{0,2,1:T(8,128)(2,1)S(1)}, bf16[768,3,192]{0,2,1:T(8,128)(2,1)}, u32[]{:S(2)}) copy-start(bf16[768,3,192]{0,2,1:T(8,128)(2,1)} %param.21) | copy-start | bytes 2654212
  199.2 6.5 %copy-start.22 = (bf16[576,3072]{1,0:T(8,128)(2,1)S(1)}, bf16[576,3072]{1,0:T(8,128)(2,1)}, u32[]{:S(2)}) copy-start(bf16[576,3072]{1,0:T(8,128)(2,1)} %get-tuple-element.68) | copy-start | bytes 10616836
  205.7 7.2 %copy-start.18 = (bf16[768,768]{1,0:T(8,128)(2,1)S(1)}, bf16[768,768]{1,0:T(8,128)(2,1)}, u32[]{:S(2)}) copy-start(bf16[768,768]{1,0:T(8,128)(2,1)} %get-tuple-element.73) | copy-start | bytes 3538948
  211.6 9.5 %slice-start = ((s8[4718592]{0:T(1024)(128)(4,1)}), s8[524288]{0:T(1024)(128)(4,1)S(1)}, s32[]{:S(2)}) async-start(s8[4718592]{0:T(1024)(128)(4,1)} %bitcast.58), calls=%async_computation | async-start | bytes 1048576
  212.9 8.2 %slice-start.1 = ((s8[4718592]{0:T(1024)(128)(4,1)}), s8[4194304]{0:T(1024)(128)(4,1)S(1)}, s32[]{:S(2)}) async-start(s8[4718592]{0:T(1024)(128)(4,1)} %bitcast.58), calls=%async_computation.1 | async-start | bytes 8388608
  212.9 8.2 %copy-start.17 = (bf16[768,768]{1,0:T(8,128)(2,1)S(1)}, bf16[768,768]{1,0:T(8,128)(2,1)}, u32[]{:S(2)}) copy-start(bf16[768,768]{1,0:T(8,128)(2,1)} %get-tuple-element.71) | copy-start | bytes 3538948
  364.0 10.6 %copy-start.4 = (bf16[768,768]{1,0:T(8,128)(2,1)S(1)}, bf16[768,768]{1,0:T(8,128)(2,1)}, u32[]{:S(2)}) copy-start(bf16[768,768]{1,0:T(8,128)(2,1)} %get-tuple-element.124) | copy-start | bytes 3538948
  372.0 3.7 copy-start.2
  374.7 3.9 %copy-start.1 = (bf16[192,768]{1,0:T(8,128)(2,1)S(1)}, bf16[192,768]{1,0:T(8,128)(2,1)}, u32[]{:S(2)}) copy-start(bf16[192,768]{1,0:T(8,128)(2,1)} %param.24) | copy-start | bytes 884740
  375.7 1.4 copy-start.9
  375.7 2.1 copy-start.8

commit v4 on v3

--- a/solution.py
+++ b/solution.py
@@ -576,8 +576,9 @@
 
     zero = jnp.zeros((width, SUB), f32)
     q_sum, v_sum = lax.fori_loop(0, tok_count // TILE, bias_tile, (zero, zero))
-    bias_ref[:, 0:1] = jnp.sum(q_sum, axis=1, keepdims=True)
-    bias_ref[:, 1:2] = jnp.sum(v_sum, axis=1, keepdims=True)
+    bias_ref[...] = jnp.zeros_like(bias_ref)
+    bias_ref[0:1, :] = jnp.sum(jnp.transpose(q_sum), axis=0, keepdims=True)
+    bias_ref[1:2, :] = jnp.sum(jnp.transpose(v_sum), axis=0, keepdims=True)
 
 
 def mix_forward(seq_lengths, tokens, weight_t, bias_col, conv_own, slots, marks):
@@ -638,7 +639,7 @@
     whole = lambda shape: pl.BlockSpec(
         shape, lambda i, lens: (0,) * len(shape), pipeline_mode=pl.Buffered(1)
     )
-    shapes = [((3 * width, tok_count), low), ((width, 2), f32), ((heads, SUB), f32)]
+    shapes = [((3 * width, tok_count), low), ((8, width), f32), ((heads, SUB), f32)]
     square = pltpu.VMEM((packed, width), f32)
     return pl.pallas_call(
         partial(mix_backward_kernel, slots, marks, taps),
@@ -790,7 +791,7 @@
     out_part = lax.dot_general(
         mixed_t, piece_rows, (((1,), (0,)), ((), ())), preferred_element_type=f32
     )
-    grad_qv_own = jnp.transpose(grad_bias)
+    grad_qv_own = grad_bias[:2]
     qkv_part = lax.dot_general(
         tokens, grad_t, (((0,), (1,)), ((), ())), preferred_element_type=f32
     ).reshape(model_width, 3, head_width)
@@ -871,114 +872,259 @@
 
 
 def tail_kernel(
-    part_ref, first_ref, down_ref, up_ref, outw_ref, qkvw_ref, small_ref,
-    input_ref, down_own, up_own, outw_own, qkvw_own, small_out,
-    up_in, down_in, core_down, core_up, core_outw, core_qkvw,
+    len_ref,
+    gt_hbm, wq_hbm, we_hbm, hid_hbm, pre_hbm, n1_hbm, gf_hbm, ga_hbm, mx_hbm, tok_hbm, first_hbm,
+    sums_ref, bin_ref, qv_ref, conv_ref, bound_ref,
+    input_ref, down_own, up_own, outw_own, qkvw_own, in_bias, vector_own, qv_own, conv_own, ratio,
+    small_out,
+    gt, wq, we, hid, pre, n1, gf, ga, mx, tok,
+    q_in, r_out, r_in, s_in, out_down, out_up, full_outw, full_qkvw, acc_qkvw,
+    core_down, core_up, core_outw, core_qkvw,
     one_down, one_up, one_outw, one_qkvw, two_down, two_up, two_outw, two_qkvw,
     z_down, z_up, z_outw, small_in,
-    z_send, z_recv, c_send, c_recv, x_send, x_recv, e_send, e_recv, s_send, s_recv,
+    load_sem, q_send, q_recv, r_send, r_recv, t_send, t_recv, c_send, c_recv, x_send, x_recv, e_send, e_recv, s_send, s_recv,
 ):
     b, z, bc, bx, by = place()
     both = bx + by - b
     flip = bc - b
     peers = [(b, lax.rem(z + i, 4)) for i in (1, 2, 3)]
+    issued = []
+    loads = [
+        pltpu.make_async_copy(src, dst, load_sem.at[n])
+        for n, (src, dst) in enumerate(
+            (
+                (gt_hbm, gt), (wq_hbm, wq), (pre_hbm, pre), (n1_hbm, n1), (hid_hbm, hid),
+                (gf_hbm, gf), (we_hbm, we), (mx_hbm, mx), (ga_hbm, ga), (tok_hbm, tok),
+                (first_hbm, input_ref),
+            )
+        )
+    ]
+    for copy in loads:
+        copy.start()
     greet(peers + [(bc, z), (bx, z), (by, z)])
-    chunks = up_in.shape[1]
-    size = up_in.shape[2]
-    issued = []
-
-    fulls = (down_ref, up_ref, outw_ref, qkvw_ref)
+    chunks, size = r_in.shape[1:3]
+    quarter = chunks * size
+    ff = down_own.shape[0]
+    group = 4 * ff
+
+    zf = z + 1 - 2 * (z % 2)
+    zg = z + 2 - 4 * (z // 2)
+    partners = ((bc, z), (bx, z), (by, z), (b, zf), (b, zg))
+
+    def small_start(k):
+        copy = remote(
+            small_out.at[k], small_in.at[k], s_send.at[k], s_recv.at[k], partners[k]
+        )
+        copy.start()
+        issued.append(copy)
+
+    def small_event(k):
+        ref = small_in.at[k]
+        remote(ref, ref, s_send.at[k], s_recv.at[k], partners[k]).wait_recv()
+        small_out[k + 1] = small_out[k] + small_in[k]
+        if k < 4:
+            small_start(k + 1)
+
+    model = input_ref.shape[1]
+    bias_rows = bin_ref.shape[1] // model
+    at_vec, at_qv = bias_rows, bias_rows + 6
+    heads, taps = conv_own.shape
+    at_conv = at_qv + 8
+    at_end = at_conv + 4 * heads
+    width = qv_own.shape[1]
+    small_out[0] = jnp.zeros(small_out.shape[1:], f32)
+    for n in range(bias_rows):
+        small_out[0, n : n + 1, :] = bin_ref[0:1, n * model : (n + 1) * model]
+    small_out[0, at_vec : at_vec + 6, :] = sums_ref[0:6, :]
+    live = jnp.int32(0)
+    for n in range(len_ref.shape[0]):
+        live = live + jnp.where(len_ref[n] > 0, heads, 0)
+    lane = lax.broadcasted_iota(jnp.int32, (1, 128), 1)
+    small_out[0, at_end : at_end + 1, 0:128] = jnp.where(
+        lane == 0, bound_ref[0:1, :], jnp.where(lane == 1, live.astype(f32), 0.0)
+    )
+    for n in range(4):
+
+        @pl.when(z == n)
+        def _():
+            for r in range(2):
+                row = at_qv + 2 * n + r
+                small_out[0, row : row + 1, :width] = qv_ref[r : r + 1, :]
+            for r in range(heads):
+                row = at_conv + heads * n + r
+                small_out[0, row : row + 1, 0:128] = conv_ref[r : r + 1, :]
+
+    small_start(0)
+
+    is_end = (z == 0) | (z == 3)
+    low_side = z < 2
+    to_inner = jnp.where(low_side, 1, 2)
+    across = jnp.where(z == 1, 2, 1)
+    to_end = jnp.where(low_side, 0, 3)
+
+    def owner(k):
+        return jnp.where(low_side, 3 - k, k)
+
+    def columns(who, c):
+        return pl.ds(pl.multiple_of(who * quarter + c * size, size), size)
+
+    def times(x, w):
+        return lax.dot_general(x, w, (((0,), (0,)), ((), ())), preferred_element_type=f32)
+
+    def part(who, c):
+        return times(gt[:, columns(who, c)], wq[...])
+
+    def q_copy(k, c):
+        return remote(
+            gt.at[:, columns(owner(k), c)], q_in.at[k, c], q_send.at[k, c], q_recv.at[k, c],
+            (b, to_inner),
+        )
+
+    def q_wait(k, c):
+        ref = q_in.at[k, c]
+        remote(ref, ref, q_send.at[k, c], q_recv.at[k, c], (b, to_end)).wait_recv()
+
+    def r_copy(k, c):
+        return remote(
+            r_out.at[k, c], r_in.at[k, c], r_send.at[k, c], r_recv.at[k, c], (b, across)
+        )
+
+    def t_copy(c):
+        return remote(r_in.at[0, c], s_in.at[c], t_send.at[c], t_recv.at[c], (b, to_end))
+
+    def first_hop(k, c):
+        @pl.when(jnp.logical_not(is_end))
+        def _():
+            own = part(owner(k), c)
+            q_wait(k, c)
+            r_out[k, c] = (own + times(q_in[k, c], we[...])).astype(low)
+            r_copy(k, c).start()
+
+    def last_hop(c):
+        @pl.when(jnp.logical_not(is_end))
+        def _():
+            own = part(to_end, c)
+            r_copy(0, c).wait_recv()
+            r_in[0, c] = (r_in[0, c].astype(f32) + own).astype(low)
+            t_copy(c).start()
+
     cores = (core_down, core_up, core_outw, core_qkvw)
     ones = (one_down, one_up, one_outw, one_qkvw)
     twos = (two_down, two_up, two_outw, two_qkvw)
-    kinds = len(fulls)
-    groups = (b, bx, by, both)
-
-    def at(n, who):
-        return fulls[n].at[:, who] if n == 2 else fulls[n].at[who]
-
-    for slot, who in enumerate(groups):
-        for n in range(kinds):
-            copy = remote(
-                at(n, who + flip), cores[n].at[slot], c_send.at[n, slot], c_recv.at[n, slot],
-                (bc, z),
-            )
-            copy.start()
-            issued.append(copy)
-
-    def flow(up, owner, c):
-        buf = up_in if up else down_in
-        side = 0 if up else 1
+    outs = (out_down, out_up)
+    left = (hid, pre)
+    right = (gf, n1)
+
+    def who(slot):
+        return b + (slot % 2) * (bx - b) + (slot // 2) * (by - b)
+
+    def term(n, owner):
+        at = pl.ds(pl.multiple_of(owner * group, group), group)
+        return lax.dot_general(
+            left[n][:, at], right[n][...], (((0,), (0,)), ((), ())), preferred_element_type=f32
+        )
+
+    def core_copy(n, slot):
+        if n < 2:
+            src = outs[n].at[slot]
+        elif n == 2:
+            src = full_outw.at[:, who(slot) + flip]
+        else:
+            src = full_qkvw.at[who(slot) + flip]
+        return remote(src, cores[n].at[slot], c_send.at[n, slot], c_recv.at[n, slot], (bc, z))
+
+    def give(n, slot):
+        if n < 2:
+            value = term(n, who(slot) + flip).astype(low)
+            outs[n][slot] = value.reshape(outs[n].shape[1:])
+        core_copy(n, slot).start()
+
+    def keep(n, slot):
+        if n < 2:
+            own = term(n, who(slot)).reshape(outs[n].shape[1:])
+        elif n == 2:
+            own = full_outw[:, who(slot)].astype(f32)
+        else:
+            own = full_qkvw[who(slot)].astype(f32)
+        core_copy(n, slot).wait_recv()
+        cores[n][slot] = (cores[n][slot].astype(f32) + own).astype(low)
+
+    def side_copy(n, dst, src):
+        partner = by if n % 2 == 0 else bx
         return remote(
-            buf.at[owner, c], buf.at[owner, c], z_send.at[side, owner, c],
-            z_recv.at[side, owner, c], (b, z + 1 if up else z - 1),
+            cores[n].at[src], ones[n].at[dst], x_send.at[n, dst], x_recv.at[n, dst], (partner, z)
         )
 
-    def flow_first(up, owner, c):
-        buf = up_in if up else down_in
-        side = 0 if up else 1
-        return remote(
-            part_ref.at[owner, c], buf.at[owner, c], z_send.at[side, owner, c],
-            z_recv.at[side, owner, c], (b, z + 1 if up else z - 1),
-        )
-
-    def z_event(k, c):
-        for up in (True, False):
-            owner = 3 - k if up else k
-            buf = up_in if up else down_in
-            at_end = (z == 0) if up else (z == 3)
-            inner = ((z > 0) & (z < owner)) if up else ((z < 3) & (z > owner))
-
-            @pl.when(at_end)
+    def small_group(n):
+        def one(i, _):
+            give(n, 3 - i)
+            return 0
+
+        lax.fori_loop(0, 4, one, 0)
+
+    def small_keep(n):
+        def one(i, _):
+            keep(n, 3 - i)
+            return 0
+
+        lax.fori_loop(0, 4, one, 0)
+        side_copy(n, 1, 3).start()
+        side_copy(n, 0, 2 if n % 2 == 0 else 1).start()
+
+    def half(h, _):
+        def out(i, _):
+            give(1, 3 - 2 * i - h)
+            give(0, 3 - i - 2 * h)
+            return 0
+
+        lax.fori_loop(0, 2, out, 0)
+
+        @pl.when(h == 1)
+        def _():
+            first_hop(0, 1)
+
+        def own(i, _):
+            slot_up, slot_down = 3 - 2 * i - h, 3 - i - 2 * h
+            keep(1, slot_up)
+
+            @pl.when(h == 0)
             def _():
-                flow_first(up, owner, c).start()
-
-            @pl.when(inner)
+                side_copy(1, 1 - i, slot_up).start()
+
+            keep(0, slot_down)
+
+            @pl.when(h == 0)
             def _():
-                flow(up, owner, c).wait_recv()
-                buf[owner, c] = (
-                    buf[owner, c].astype(f32) + part_ref[owner, c].astype(f32)
-                ).astype(low)
-                flow(up, owner, c).start()
-
-    def core_event(n):
-        for slot, who in enumerate(groups):
-            ref = cores[n].at[slot]
-            remote(ref, ref, c_send.at[n, slot], c_recv.at[n, slot], (bc, z)).wait_recv()
-            mine = fulls[n][:, who] if n == 2 else fulls[n][who]
-            cores[n][slot] = (cores[n][slot].astype(f32) + mine.astype(f32)).astype(low)
-        first, second = (2, 1) if n % 2 == 0 else (1, 2)
-        partner = by if n % 2 == 0 else bx
-        for i, (src, dst) in enumerate(((first, 0), (3, 1))):
-            copy = remote(
-                cores[n].at[src], ones[n].at[dst], x_send.at[n, i], x_recv.at[n, i], (partner, z)
-            )
-            copy.start()
-            issued.append(copy)
+                side_copy(0, 1 - i, slot_down).start()
+
+            return 0
+
+        lax.fori_loop(0, 2, own, 0)
+        return 0
 
     def one_event(n):
-        first, second = (2, 1) if n % 2 == 0 else (1, 2)
+        second = 1 if n % 2 == 0 else 2
         partner, other = (by, bx) if n % 2 == 0 else (bx, by)
-        for i, slot in ((0, 0), (1, second)):
-            ref = ones[n].at[i]
-            remote(ref, ref, x_send.at[n, i], x_recv.at[n, i], (partner, z)).wait_recv()
-            ones[n][i] = (ones[n][i].astype(f32) + cores[n][slot].astype(f32)).astype(low)
-        copy = remote(
-            ones[n].at[1], twos[n], x_send.at[n, 2], x_recv.at[n, 2], (other, z)
-        )
+        ref = ones[n].at[1]
+        remote(ref, ref, x_send.at[n, 1], x_recv.at[n, 1], (partner, z)).wait_recv()
+        ones[n][1] = (ones[n][1].astype(f32) + cores[n][second].astype(f32)).astype(low)
+        copy = remote(ones[n].at[1], twos[n], x_send.at[n, 2], x_recv.at[n, 2], (other, z))
         copy.start()
         issued.append(copy)
 
     z_bufs = (z_down, z_up, z_outw)
 
     def two_event(n):
-        other = bx if n % 2 == 0 else by
+        partner, other = (by, bx) if n % 2 == 0 else (bx, by)
+        ref = ones[n].at[0]
+        remote(ref, ref, x_send.at[n, 0], x_recv.at[n, 0], (partner, z)).wait_recv()
         ref = twos[n]
         remote(ref, ref, x_send.at[n, 2], x_recv.at[n, 2], (other, z)).wait_recv()
+        own = ones[n][0].astype(f32) + cores[n][0].astype(f32)
         if n == 3:
-            qkvw_own[...] = twos[n][...].astype(f32) + ones[n][0].astype(f32)
+            qkvw_own[...] = twos[n][...].astype(f32) + own
             return
-        twos[n][...] = (twos[n][...].astype(f32) + ones[n][0].astype(f32)).astype(low)
+        twos[n][...] = (twos[n][...].astype(f32) + own).astype(low)
         for i, (_, to) in enumerate(peers):
             copy = remote(
                 twos[n].at[to], z_bufs[n].at[i], e_send.at[n, i], e_recv.at[n, i], (b, to)
@@ -993,115 +1139,194 @@
             ref = z_bufs[n].at[i]
             remote(ref, ref, e_send.at[n, i], e_recv.at[n, i], (b, source)).wait_recv()
             total = total + z_bufs[n][i].astype(f32)
+        if n > 0:
+            total = jnp.transpose(total)
         (down_own, up_own, outw_own)[n][...] = total
 
-    zf = z + 1 - 2 * (z % 2)
-    zg = z + 2 - 4 * (z // 2)
-    partners = ((bc, z), (bx, z), (by, z), (b, zf), (b, zg))
-
-    def small_start(k):
-        copy = remote(
-            small_out.at[k], small_in.at[k], s_send.at[k], s_recv.at[k], partners[k]
-        )
-        copy.start()
-        issued.append(copy)
-
-    def small_event(k):
-        ref = small_in.at[k]
-        remote(ref, ref, s_send.at[k], s_recv.at[k], partners[k]).wait_recv()
-        small_out[k + 1] = small_out[k] + small_in[k]
-        if k < 4:
-            small_start(k + 1)
-
-    small_out[0] = small_ref[...]
-    small_start(0)
-
-    z_list = [(k, c) for k in range(3) for c in range(chunks)]
-    other = (
-        [partial(core_event, n) for n in (0, 1, 2, 3)]
-        + [partial(small_event, 0), partial(small_event, 1)]
-        + [partial(one_event, n) for n in (0, 1, 2, 3)]
-        + [partial(small_event, 2), partial(small_event, 3)]
-        + [partial(two_event, n) for n in (0, 1, 2, 3)]
-        + [partial(small_event, 4)]
-    )
-    lead = 2
-    for k, c in z_list[:lead]:
-        z_event(k, c)
-    rest = z_list[lead:]
-    for n in range(max(len(rest), len(other))):
-        if n < len(other):
-            other[n]()
-        if n < len(rest):
-            z_event(*rest[n])
-    for n in (0, 1, 2):
+    def projections():
+        on, oh = full_outw.shape[2:]
+        for s in range(4):
+            value = jnp.transpose(mul(mx[s], ga[...]))
+            full_outw[s] = value.astype(low).reshape(full_outw.shape[1:])
+        acc_qkvw[...] = jnp.zeros_like(acc_qkvw)
+        span = quarter
+
+        def one(n, _):
+            at = pl.ds(pl.multiple_of(n * span, span), span)
+            acc_qkvw[...] += mul(gt[:, at], tok[at, :])
+            return 0
+
+        lax.fori_loop(0, 4, one, 0)
+        full_qkvw[...] = jnp.transpose(acc_qkvw[...]).astype(low).reshape(full_qkvw.shape)
+
+    loads[0].wait()
+
+    @pl.when(is_end)
+    def _():
+        for k in range(3):
+            for c in range(chunks):
+                q_copy(k, c).start()
+
+    for n in range(1, 7):
+        loads[n].wait()
+
+    def both_halves(h, _):
+        half(h, 0)
+
+        @pl.when(h == 0)
+        def _():
+            first_hop(0, 0)
+
+        return 0
+
+    lax.fori_loop(0, 2, both_halves, 0)
+    first_hop(0, 2)
+    last_hop(0)
+    one_event(1)
+    one_event(0)
+    for n in (7, 8, 9):
+        loads[n].wait()
+    projections()
+    first_hop(1, 0)
+    last_hop(1)
+    small_group(2)
+    small_group(3)
+    small_event(0)
+    first_hop(1, 1)
+    last_hop(2)
+    small_keep(2)
+    small_keep(3)
+    small_event(1)
+    first_hop(1, 2)
+    two_event(1)
+    two_event(0)
+    small_event(2)
+    one_event(2)
+    one_event(3)
+    small_event(3)
+    two_event(2)
+    two_event(3)
+    small_event(4)
+    loads[10].wait()
+
+    def own_rows(c, _):
+        rows = pl.ds(pl.multiple_of(c * size, size), size)
+        input_ref[rows, :] += part(z, c)
+
+        @pl.when(is_end)
+        def _():
+            ref = s_in.at[c]
+            remote(ref, ref, t_send.at[c], t_recv.at[c], (b, to_inner)).wait_recv()
+            input_ref[rows, :] += s_in[c].astype(f32)
+
+        @pl.when(jnp.logical_not(is_end))
+        def _():
+            r_copy(1, c).wait_recv()
+            q_wait(2, c)
+            input_ref[rows, :] += r_in[1, c].astype(f32) + times(q_in[2, c], we[...])
+
+        return 0
+
+    lax.fori_loop(0, chunks, own_rows, 0)
+    for n in (1, 0, 2):
         end_event(n)
 
-    for c in range(chunks):
-        rows = pl.ds(c * size, size)
-        input_ref[rows] = first_ref[rows] + part_ref[z, c].astype(f32)
-
-    for c in range(chunks):
-        rows = pl.ds(c * size, size)
-        for up in (True, False):
-            buf = up_in if up else down_in
-
-            @pl.when((z > 0) if up else (z < 3))
-            def _():
-                side = 0 if up else 1
-                ref = buf.at[z, c]
-                remote(
-                    ref, ref, z_send.at[side, z, c], z_recv.at[side, z, c],
-                    (b, z - 1 if up else z + 1),
-                ).wait_recv()
-                input_ref[rows] += buf[z, c].astype(f32)
-
-    for k, c in z_list:
-        for up in (True, False):
-            owner = 3 - k if up else k
-
-            @pl.when((z < owner) if up else (z > owner))
-            def _():
-                flow(up, owner, c).wait_send()
-
+    @pl.when(is_end)
+    def _():
+        for k in range(3):
+            for c in range(chunks):
+                q_copy(k, c).wait_send()
+
+    @pl.when(jnp.logical_not(is_end))
+    def _():
+        for c in range(chunks):
+            r_copy(0, c).wait_send()
+            r_copy(1, c).wait_send()
+            t_copy(c).wait_send()
+
+    final = small_out.at[5]
+    in_bias[...] = jnp.zeros_like(in_bias)
+    index = b * 4 + z
+    per_row = model // ff
+    for n in range(bias_rows):
+
+        @pl.when(index // per_row == n)
+        def _():
+            row = pltpu.roll(final[n : n + 1, :], (model - (index % per_row) * ff) % model, 1)
+            in_bias[...] = row[:, :ff]
+
+    share = vector_own.shape[1]
+    vectors = final[at_vec : at_vec + 6, :]
+    vector_own[...] = pltpu.roll(vectors, (model - index * share) % model, 1)[:, :share]
+    for n in range(4):
+
+        @pl.when(z == n)
+        def _():
+            qv_own[...] = final[at_qv + 2 * n : at_qv + 2 * n + 2, :width]
+            conv_own[...] = final[at_conv + heads * n : at_conv + heads * (n + 1), :taps]
+
+    ratio[...] = final[at_end : at_end + 1, 0:1] / final[at_end : at_end + 1, 1:2]
+
+    for n in range(4):
+        for dst in range(2):
+            side_copy(n, dst, dst).wait_send()
+        for slot in range(4):
+            core_copy(n, slot).wait_send()
     for copy in issued:
         copy.wait_send()
 
 
-def tail(part, first, down, up, outw, qkvw, small):
+def tail(
+    lengths, gt, wq, we, hid, pre, n1, gf, ga, mx, tok, first, sums, bins, qv_grad, conv_grad, bound,
+    taps,
+):
     quarter, model = first.shape
-    chunks = 4
+    chunks = 3
     size = quarter // chunks
-    ff = down.shape[2]
-    on, oh = outw.shape[2:]
-    qn, qh = qkvw.shape[1:]
+    ff = hid.shape[1] // 32
+    width = mx.shape[1]
+    heads = width // HEAD_DIM
+    on, oh = model // 8, width
+    qn, qh = model // 8, gt.shape[0]
     blocks = ((4, ff, model), (4, ff, model), (4, on, oh), (qn, qh))
     own = lambda *s: jax.ShapeDtypeStruct(s, f32)
     vm = lambda *s: pltpu.VMEM(s, low)
     dma = pltpu.SemaphoreType.DMA
+    sources = (gt, wq, we, hid, pre, n1, gf, ga, mx, tok)
+    small = -(-(bins.shape[1] // model + 15 + 4 * heads) // 8) * 8
+    vmem = pl.BlockSpec(memory_space=pltpu.VMEM)
     return pl.pallas_call(
         tail_kernel,
         out_shape=[
-            own(quarter, model), own(ff, model), own(ff, model), own(on, oh), own(qn, qh),
-            own(6, *small.shape),
+            own(quarter, model), own(ff, model), own(model, ff), own(oh, on), own(qn, qh),
+            own(1, ff), own(6, model // 32), own(2, width), own(heads, taps), own(1, 1),
         ],
-        in_specs=[pl.BlockSpec(memory_space=pltpu.VMEM)] * 7,
-        out_specs=[pl.BlockSpec(memory_space=pltpu.VMEM)] * 6,
+        in_specs=[pl.BlockSpec(memory_space=pltpu.SMEM)]
+        + [pl.BlockSpec(memory_space=pl.ANY)] * 11
+        + [vmem] * 5,
+        out_specs=[vmem] * 10,
         scratch_shapes=[
-            vm(4, chunks, size, model), vm(4, chunks, size, model),
+            pltpu.VMEM((6, small, model), f32),
+            *[vm(*x.shape) for x in sources],
+            vm(3, chunks, qh, size), vm(2, chunks, size, model), vm(2, chunks, size, model),
+            vm(chunks, size, model),
+            vm(4, *blocks[0]), vm(4, *blocks[1]),
+            vm(4, 8, on, oh), vm(8, qn, qh), pltpu.VMEM((qh, model), f32),
             *[vm(4, *s) for s in blocks],
             *[vm(2, *s) for s in blocks],
             *[vm(*s) for s in blocks],
             *[vm(3, *s[1:]) for s in blocks[:3]],
-            pltpu.VMEM((5, *small.shape), f32),
-            dma((2, 4, chunks)), dma((2, 4, chunks)), dma((4, 4)), dma((4, 4)),
+            pltpu.VMEM((5, small, model), f32),
+            dma((11,)),
+            dma((3, chunks)), dma((3, chunks)), dma((2, chunks)), dma((2, chunks)),
+            dma((chunks,)), dma((chunks,)), dma((4, 4)), dma((4, 4)),
             dma((4, 3)), dma((4, 3)), dma((3, 3)), dma((3, 3)), dma((5,)), dma((5,)),
         ],
         compiler_params=pltpu.CompilerParams(
-            collective_id=3, has_side_effects=True, vmem_limit_bytes=62 * 1024 * 1024
+            collective_id=3, has_side_effects=True, vmem_limit_bytes=63 * 1024 * 1024
         ),
         name="tail",
-    )(part.reshape(4, chunks, size, model), first, down, up, outw, qkvw, small)
+    )(lengths, *sources, first, sums, bins, qv_grad, conv_grad, bound)
 
 
 def cumulative(x):
@@ -1129,10 +1354,11 @@
 
 def middle_kernel(
     pieces, share,
-    mixed_ref, own0, own1, own2, own3, tok_ref, cot_ref, vec_ref,
+    mixed_ref, own0, own1, own2, own3, tok_hbm, cot_ref,
+    out_bias_ref, gain1_ref, shift1_ref, down_bias_ref, gain2_ref, shift2_ref,
     out_ref, first_ref, attn_ref, hidden_ref, pre_ref, norm_ref, ffn_ref, all_ref, grad_ref,
     sums_ref, bin_ref,
-    packs, wof, wo, slope, total, turned,
+    tok_ref, packs, wof, wo, slope, total, turned,
     a_send, a_recv, f_send, f_recv, p_send, p_recv, g_send, g_recv, own_sem, own_turn,
 ):
     b, z, bc, bx, by = place()
@@ -1140,7 +1366,7 @@
     peers = [(b, lax.rem(z + i, 4)) for i in (1, 2, 3)]
     greet(peers + [(bc, z), (bx, z), (by, z)])
     width, quarter = all_ref.shape[1:]
-    model = tok_ref.shape[1]
+    model = tok_hbm.shape[1]
     owns = (own0, own1, own2, own3)
     origins = [lax.rem(z + 4 - i, 4) for i in range(4)]
     issued = []
@@ -1160,6 +1386,11 @@
     ]
     local.append(
         pltpu.make_async_copy(mixed_ref.at[:, columns(z)], all_ref.at[z], own_sem.at[4])
+    )
+    local.append(
+        pltpu.make_async_copy(
+            tok_hbm.at[pl.ds(pl.multiple_of(z * quarter, quarter), quarter)], tok_ref, own_sem.at[5]
+        )
     )
     count = len(pieces)
 
@@ -1232,9 +1463,8 @@
         for s in range(4):
             row = row + packs[q, s, 2 * ff + share : 2 * ff + share + 1, :group].astype(f32)
         ff_bias.append(row)
-    out_bias, gain1, shift1, down_bias, gain2, shift2 = [
-        vec_ref[n : n + 1, :] for n in range(6)
-    ]
+    out_bias, gain1, shift1 = out_bias_ref[...], gain1_ref[...], shift1_ref[...]
+    down_bias, gain2, shift2 = down_bias_ref[...], gain2_ref[...], shift2_ref[...]
     sums_ref[...] = jnp.zeros_like(sums_ref)
     bin_ref[...] = jnp.zeros_like(bin_ref)
     for q in range(8):
@@ -1342,9 +1572,9 @@
         copy.wait_send()
 
 
-def ffn_middle(mixed_t, packs, tok, cot, vectors, ff, share):
+def ffn_middle(mixed_t, packs, tokens, cot, vectors, ff, share):
     width, tok_count = mixed_t.shape
-    quarter, model = tok.shape
+    quarter, model = tok_count // 4, tokens.shape[1]
     size = quarter // 3
     rows = packs[0].shape[0]
     half = ff // 2
@@ -1372,9 +1602,10 @@
             shape((8, model), f32),
             shape((8, 32 * ff), f32),
         ],
-        in_specs=[hbm] + [vmem] * 7,
+        in_specs=[hbm] + [vmem] * 4 + [hbm] + [vmem] * 7,
         out_specs=[vmem] * 8 + [hbm] + [vmem] * 2,
         scratch_shapes=[
+            pltpu.VMEM((quarter, model), low),
             pltpu.VMEM((8, 4, rows, model), low),
             pltpu.VMEM((4 * width, model), f32),
             pltpu.VMEM((4, width, model), low),
@@ -1382,13 +1613,13 @@
             pltpu.VMEM((size, model), f32),
             pltpu.VMEM((3, 4 * width, size), low),
             dma((3,)), dma((3,)), dma((n, 4)), dma((n, 4)), dma((n, 6)), dma((n, 6)),
-            dma((3, 3)), dma((3, 3)), dma((5,)), dma((3,)),
+            dma((3, 3)), dma((3, 3)), dma((6,)), dma((3,)),
         ],
         compiler_params=pltpu.CompilerParams(
             collective_id=1, has_side_effects=True, vmem_limit_bytes=62 * 1024 * 1024
         ),
         name="middle",
-    )(mixed_t, *packs, tok, cot, vectors)
+    )(mixed_t, *packs, tokens, cot, *vectors)
 
 
 def slice_body(
@@ -1411,18 +1642,16 @@
     segment_ids,
     landmark_bounds,
 ):
-    tok_count, model = tokens.shape
+    model = tokens.shape[1]
     width = qkv_weight.shape[2]
     heads_here = width // HEAD_DIM
     kernel_taps = conv_weight.shape[1]
     slots, marks = landmark_bounds.shape
-    quarter = tok_count // 4
     z = lax.axis_index("heads")
     b = lax.axis_index("batch")
-    own_low = lax.dynamic_slice_in_dim(tokens, z * quarter, quarter, 0)
     conv_own = lax.dynamic_slice_in_dim(conv_weight, z * heads_here, heads_here, 0)
     qv_own = lax.dynamic_slice_in_dim(qv_bias, z * width, width, 1)
-    flat_qkv = qkv_weight.reshape(model, 3 * width)
+    weight_t = jnp.transpose(qkv_weight.reshape(model, 3 * width))
     bias_col = jnp.concatenate([qv_own[0], jnp.zeros_like(qv_own[0]), qv_own[1]])[:, None]
     ff_own = ffn_out_weight.shape[0]
     share = width // 8
@@ -1441,100 +1670,43 @@
         lax.ppermute(pack, "heads", [(n, (n + i) % 4) for n in range(4)]) for i in (1, 2, 3)
     ]
     forward = mix_forward(
-        seq_lengths, tokens, jnp.transpose(flat_qkv), bias_col, conv_own, slots, marks
+        seq_lengths, tokens, weight_t, bias_col, conv_own, slots, marks
     )
     qkv_t, first, last, mixed_t, mark, value, inner, denom, middle, steps, inverse, bound = forward
-    vectors = jnp.concatenate(
-        [
-            jnp.stack(
-                [out_bias, norm1_gain, norm1_bias, ffn_out_bias, norm2_gain, norm2_bias]
-            ),
-            jnp.zeros((2, model), f32),
-        ]
-    )
+    vectors = [
+        v[None, :]
+        for v in (out_bias, norm1_gain, norm1_bias, ffn_out_bias, norm2_gain, norm2_bias)
+    ]
     (
         final_low, grad_first, grad_attn_low, hidden_low, grad_pre, norm1_low, grad_ffn_low,
         mixed_all, grad_mix_t, vector_sums, bias_sums,
-    ) = ffn_middle(mixed_t, packs, own_low, cotangent, vectors, ff_own, share)
-    grad_in_bias = bias_sums[0]
+    ) = ffn_middle(mixed_t, packs, tokens, cotangent, vectors, ff_own, share)
     saved = (qkv_t, first, last, mark, value, inner, denom, middle, steps, inverse)
+    held, grad_mix_t = lax.optimization_barrier((weight_t, grad_mix_t))
+    weight_end = lax.ppermute(held, "heads", [(0, 1), (3, 2)])
     grad_t, grad_bias, grad_conv = mix_backward(
         seq_lengths, grad_mix_t, saved, conv_own, slots, marks
     )
-    part = lax.dot_general(
-        grad_t, flat_qkv, (((0,), (1,)), ((), ())), preferred_element_type=f32
-    ).astype(low)
-    down_term = lax.dot_general(
-        hidden_low, grad_ffn_low, contract_rows, preferred_element_type=f32
-    ).astype(low)
-    up_term = lax.dot_general(
-        grad_pre, norm1_low, contract_rows, preferred_element_type=f32
-    ).astype(low)
-    out_term = lax.dot_general(
-        grad_attn_low,
-        mixed_all,
-        (((0,), (2,)), ((), ())),
-        preferred_element_type=f32,
-    ).astype(low)
-    out_term = jnp.swapaxes(out_term, 0, 1).reshape(4, 8, model // 8, width)
-    qkv_term = lax.dot_general(
-        tokens, grad_t, (((0,), (1,)), ((), ())), preferred_element_type=f32
-    ).astype(low)
-
-    flat = jnp.concatenate(
-        [
-            grad_in_bias,
-            vector_sums[:6].reshape(-1),
-        ]
-    )
-    head_total = conv_weight.shape[0]
-    conv_full = lax.dynamic_update_slice_in_dim(
-        jnp.zeros((head_total, kernel_taps), f32), grad_conv[:, :kernel_taps], z * heads_here, 0
-    )
-    bias_full = lax.dynamic_update_slice_in_dim(
-        jnp.zeros((2, 4 * width), f32), jnp.transpose(grad_bias), z * width, 1
-    )
-    live_count = jnp.sum((seq_lengths > 0).astype(f32)) * heads_here
-    scalars = jnp.stack([bound[0, 0], live_count])
-    small = jnp.concatenate([flat, bias_full.reshape(-1), conv_full.reshape(-1), scalars])
-    lanes = 768
-    rows = -(-small.shape[0] // (8 * lanes)) * 8
-    small = jnp.pad(small, (0, rows * lanes - small.shape[0])).reshape(rows, lanes)
-    ff = ff_own * 32
-    input_grad, down_share, up_share, out_share, qkv_share, sums = tail(
-        part,
-        grad_first,
-        down_term.reshape(8, 4, ff_own, model),
-        up_term.reshape(8, 4, ff_own, model),
-        out_term,
-        qkv_term.reshape(8, model // 8, 3 * width),
-        small,
-    )
-    sums = sums[5].reshape(-1)
-    index = b * 4 + z
-    in_bias_share = lax.dynamic_slice_in_dim(sums, index * ff_own, ff_own, 0)
-    vectors = sums[ff : ff + 6 * model].reshape(6, model)
-    vector_share = lax.dynamic_slice_in_dim(vectors, index * (model // 32), model // 32, 1)
-    at = ff + 6 * model
-    bias_sum = sums[at : at + 8 * width].reshape(2, 4 * width)
-    bias_out = lax.dynamic_slice_in_dim(bias_sum, z * width, width, 1)
-    at = at + 8 * width
-    conv_sum = sums[at : at + head_total * kernel_taps].reshape(head_total, kernel_taps)
-    conv_out = lax.dynamic_slice_in_dim(conv_sum, z * heads_here, heads_here, 0)
-    at = at + head_total * kernel_taps
-    condition = sums[at] / sums[at + 1]
+    (
+        input_grad, down_share, up_share, out_share, qkv_share,
+        in_bias_share, vector_share, bias_out, conv_out, condition,
+    ) = tail(
+        seq_lengths, grad_t, weight_t, weight_end, hidden_low, grad_pre, norm1_low, grad_ffn_low,
+        grad_attn_low, mixed_all, tokens, grad_first, vector_sums, bias_sums, grad_bias,
+        grad_conv, bound, kernel_taps,
+    )
     return (
         final_low,
         input_grad,
         qkv_share.reshape(model // 8, 3, width),
         bias_out,
         conv_out,
-        jnp.transpose(out_share),
-        jnp.transpose(up_share),
-        in_bias_share,
+        out_share,
+        up_share,
+        in_bias_share.reshape(ff_own),
         down_share,
         vector_share,
-        condition,
+        condition.reshape(()),
     )
 
 

time: 383 us -> 311 us (0.81)
  Pallas kernels: 308 us -> 274 us
  matrix products: 28.6 us -> 0 us
  local copies, waits for them, and re-layouts: 30.1 us -> 21.2 us
    pallas_call x1, Pallas kernels: 137 us -> 103 us  [tail(): pl.pallas_call(tail_kernel, out_shape=[own(quarter, model), own(ff, model...]
    dot_general x5 -> x0, matrix products: 28.6 us -> none  [the longest x1 8.22 us: slice_body(): lax.dot_general(grad_pre, norm1_low, contract_rows, preferred_element_typ...]
    slice x7 -> x0, local copies, waits for them, and re-layouts: 5.13 us -> none  [the longest x1 1.2 us: slice_body(): scalars = jnp.stack([bound[0, 0], live_count])]
    dynamic_slice x5 -> x0, local copies, waits for them, and re-layouts: 4.86 us -> none  [the longest x1 2.36 us: slice_body(): own_low = lax.dynamic_slice_in_dim(tokens, z * quarter, quarter, 0)]
    ppermute x0 -> x1, starting transfers between devices: none -> 4.6 us  [slice_body(): weight_end = lax.ppermute(held, 'heads', [(0, 1), (3, 2)])]
    unnamed x56 -> x52, local copies, waits for them, and re-layouts: 8.33 us -> 12.7 us
  transfers between devices with their start and end apart: 3 -> 4, of which waited for: 0 -> 0; matrix products, arithmetic and copies ran while one was open for 2% -> 2% of each run, Pallas kernels for 8% -> 22%
where the time goes in v4:
time: 311 us; the launch traced here: 310 us
  Pallas kernels  274 us (88%)
  local copies, waits for them, and re-layouts  21.2 us (7%)
  starting transfers between devices  10.8 us (3%)
    pallas_call x1, Pallas kernels, ffn_middle(): pl.pallas_call(partial(middle_kernel, pieces, share), out_shape=[shape((q...  104 us
    pallas_call x1, Pallas kernels, tail(): pl.pallas_call(tail_kernel, out_shape=[own(quarter, model), own(ff, model...  103 us
    pallas_call x1, Pallas kernels, mix_backward(): pl.pallas_call(partial(mix_backward_kernel, slots, marks, taps), out_shap...  35.9 us
    pallas_call x1, Pallas kernels, mix_forward(): pl.pallas_call(partial(mix_forward_kernel, slots, marks, taps), out_shape...  31.1 us
    unnamed x52, local copies, waits for them, and re-layouts  12.7 us
  transfers between devices with their start and end apart: 4, of which 0 were waited for; matrix products, arithmetic and copies ran while one was open for 2% of the time, Pallas kernels for 22%

profile of v4, /device:TPU:0, one launch (start us, length us, event | category | flops | bytes accessed | tf_op | source)
XLA Modules:
  0.0 309.7 jit_solution(16019746151224998722)
XLA Ops:
  0.6 0.0 copy-start
  0.7 0.9 copy-done
  1.6 0.8 dynamic_update_slice.6
  2.4 1.0 fusion.1.own0
  3.4 5.2 %collective-permute-start.2 = (bf16[224,768]{1,0:T(8,128)(2,1)S(1)}, bf16[224,768]{1,0:T(8,128)(2,1)S(1)}, u32[]{:S(2)}, u32[]{:S(2)}) collective-permute-start(bf16[224,768]{1,0:T(8,128)(2,1)S(1)} %fusion.1.own0), channel_id=1, source_target_pairs={{0,3},{1,0},{2,1},{3,2},{4,7},{5,4},{6,5},{7,6},{8,11},{9,8},{10,9... | collective-permute-start | bytes 1032200 | tf_op jit(solution)/shard_map/ppermute | solution.py:1670
  8.6 0.0 collective-permute-start.1
  8.6 1.0 collective-permute-start
  9.6 0.8 constant_dynamic-slice_fusion
  10.5 0.1 pad_maximum_fusion
  10.5 0.9 broadcast_in_dim.37.bias_ref
  11.4 1.3 constant_dynamic-slice_fusion.2.conv_ref
  12.7 0.0 copy-start.15
  12.7 0.0 copy-start.16
  12.7 31.1 %mix_forward.1 = (bf16[576,3072]{1,0:T(8,128)(2,1)}, bf16[192,3072]{1,0:T(8,128)(2,1)}, bf16[192,3072]{1,0:T(8,128)(2,1)}, bf16[192,3072]{1,0:T(8,128)(2,1)}, f3...) custom-call(s32[3]{0:T(128)} %len_ref.5, ...), custom_call_target="tpu_custom_call" | custom-call | flops 20000000000 | bytes 30000000 | tf_op jit(solution)/shard_map/mix_forward/pallas_call | solution.py:605
  43.8 0.6 broadcast_in_dim.31.out_bias_ref
  44.4 0.6 broadcast_in_dim.32.gain1_ref
  45.0 0.6 broadcast_in_dim.33.shift1_ref
  45.6 0.6 broadcast_in_dim.34.down_bias_ref
  46.2 0.6 broadcast_in_dim.35.gain2_ref
  46.8 0.6 broadcast_in_dim.36.shift2_ref
  47.4 0.0 collective-permute-done.2.own3
  47.4 0.0 collective-permute-done.1.own2
  47.4 0.0 collective-permute-done.own1
  47.4 0.0 copy-start.8
  47.4 0.8 copy-done.8
  48.2 0.0 copy-done.6
  48.2 0.1 copy-done.7
  48.3 104.0 %middle.1 = (bf16[768,768]{1,0:T(8,128)(2,1)}, f32[768,768]{1,0:T(8,128)}, bf16[768,768]{1,0:T(8,128)(2,1)}, bf16[768,3072]{1,0:T(8,128)(2,1)}, bf16[768,3072]{1...) custom-call(bf16[192,3072]{1,0:T(8,128)(2,1)} %get-tuple-element.61., ...), custom_call_target="tpu_custom_call" | custom-call | tf_op jit(solution)/shard_map/middle/pallas_call | solution.py:1590
  152.4 4.6 %collective-permute-start.3 = (bf16[576,768]{1,0:T(8,128)(2,1)S(1)}, bf16[576,768]{1,0:T(8,128)(2,1)S(1)}, u32[]{:S(2)}, u32[]{:S(2)}) collective-permute-start(bf16[576,768]{1,0:T(8,128)(2,1)S(1)} %bitcast.13), channel_id=1, source_target_pairs={{0,1},{3,2},{4,5},{7,6},{8,9},{11,10},{12,13},{15,14},{16,17},{19,... | collective-permute-start | bytes 2654216 | tf_op jit(solution)/shard_map/ppermute | solution.py:1686
  157.0 35.9 %mix_backward.1 = (bf16[576,3072]{1,0:T(8,128)(2,1)}, f32[8,192]{1,0:T(8,128)}, f32[3,128]{1,0:T(4,128)}) custom-call(s32[3]{0:T(128)} %len_ref.5, bf16[192,3072]{1,0:T(8,128)(2,1)} %get-tuple-element.64.grad_ref, bf16[576,3072]{1,0:T(8,128)(2,1)} %get-tuple-element.65.qkv_ref, bf16[192,3072]{1,0:T(8,128)(2,1)} %get-tuple-element.66.first_ref, ...), custom_call_target="tpu_custom_call" | custom-call | flops 20000000000 | bytes 30000000 | tf_op jit(solution)/shard_map/mix_backward/pallas_call | solution.py:644
  192.9 0.0 collective-permute-done.3.we_hbm
  192.9 0.0 copy-start.5
  192.9 0.9 copy-done.5
  193.8 103.1 %tail.1 = (f32[768,768]{1,0:T(8,128)}, f32[96,768]{1,0:T(8,128)}, f32[768,96]{1,0:T(8,128)}, f32[192,96]{1,0:T(8,128)}, f32[96,576]{1,0:T(8,128)}, /*index=5*/f3...) custom-call(s32[3]{0:T(128)} %len_ref.5, ...), custom_call_target="tpu_custom_call" | custom-call | tf_op jit(solution)/shard_map/tail/pallas_call | solution.py:1298
  296.9 0.0 copy-start.3
  296.9 1.2 copy.30
  298.1 0.9 copy.31
  299.0 1.9 copy.32
  300.9 1.0 copy.43
  301.9 1.1 copy-done.1
  303.0 1.4 copy.44
  304.4 0.6 copy.45
  305.0 0.0 copy-done.18
  305.0 0.6 copy.46
  305.6 0.6 copy.47
  306.2 0.5 copy.48
  306.7 0.7 copy.49
  307.5 0.6 copy.50
  (32 shorter events, 0.1 us)
Async XLA Ops:
  0.6 1.0 copy-start
  3.4 40.4 %copy-start.2 = (bf16[224,768]{1,0:T(8,128)(2,1)}, bf16[224,768]{1,0:T(8,128)(2,1)S(1)}, u32[]{:S(2)}) copy-start(bf16[224,768]{1,0:T(8,128)(2,1)S(1)} %fusion.1.own0) | copy-start | bytes 1032196
  3.4 43.9 %collective-permute-start.2 = (bf16[224,768]{1,0:T(8,128)(2,1)S(1)}, bf16[224,768]{1,0:T(8,128)(2,1)S(1)}, u32[]{:S(2)}, u32[]{:S(2)}) collective-permute-start(bf16[224,768]{1,0:T(8,128)(2,1)S(1)} %fusion.1.own0), channel_id=1, source_target_pairs={{0,3},{1,0},{2,1},{3,2},{4,7},{5,4},{6,5},{7,6},{8,11},{9,8},{10,9... | collective-permute-start | bytes 1032200 | tf_op jit(solution)/shard_map/ppermute | solution.py:1670
  8.6 38.8 %collective-permute-start.1 = (bf16[224,768]{1,0:T(8,128)(2,1)S(1)}, bf16[224,768]{1,0:T(8,128)(2,1)S(1)}, u32[]{:S(2)}, u32[]{:S(2)}) collective-permute-start(bf16[224,768]{1,0:T(8,128)(2,1)S(1)} %fusion.1.own0), channel_id=1, source_target_pairs={{0,2},{1,3},{2,0},{3,1},{4,6},{5,7},{6,4},{7,5},{8,10},{9,11},{10,... | collective-permute-start | bytes 1032200 | tf_op jit(solution)/shard_map/ppermute | solution.py:1670
  8.6 38.8 %collective-permute-start = (bf16[224,768]{1,0:T(8,128)(2,1)S(1)}, bf16[224,768]{1,0:T(8,128)(2,1)S(1)}, u32[]{:S(2)}, u32[]{:S(2)}) collective-permute-start(bf16[224,768]{1,0:T(8,128)(2,1)S(1)} %fusion.1.own0), channel_id=1, source_target_pairs={{0,1},{1,2},{2,3},{3,0},{4,5},{5,6},{6,7},{7,4},{8,9},{9,10},{10,1... | collective-permute-start | bytes 1032200 | tf_op jit(solution)/shard_map/ppermute | solution.py:1670
  12.7 31.1 %copy-start.11 = (f32[768]{0:T(1024)S(1)}, f32[768]{0:T(1024)}, u32[]{:S(2)}) copy-start(f32[768]{0:T(1024)} %param.25) | copy-start | bytes 9220
  12.7 31.7 %copy-start.12 = (f32[768]{0:T(1024)S(1)}, f32[768]{0:T(1024)}, u32[]{:S(2)}) copy-start(f32[768]{0:T(1024)} %param.26) | copy-start | bytes 9220
  12.7 32.3 %copy-start.13 = (f32[768]{0:T(1024)S(1)}, f32[768]{0:T(1024)}, u32[]{:S(2)}) copy-start(f32[768]{0:T(1024)} %param.27) | copy-start | bytes 9220
  12.7 32.9 %copy-start.14 = (f32[768]{0:T(1024)S(1)}, f32[768]{0:T(1024)}, u32[]{:S(2)}) copy-start(f32[768]{0:T(1024)} %param.31) | copy-start | bytes 9220
  12.7 33.5 %copy-start.15 = (f32[768]{0:T(1024)S(1)}, f32[768]{0:T(1024)}, u32[]{:S(2)}) copy-start(f32[768]{0:T(1024)} %param.32) | copy-start | bytes 9220
  12.7 34.1 %copy-start.16 = (f32[768]{0:T(1024)S(1)}, f32[768]{0:T(1024)}, u32[]{:S(2)}) copy-start(f32[768]{0:T(1024)} %param.33) | copy-start | bytes 9220
  47.4 0.9 copy-start.6
  47.4 0.9 copy-start.7
  47.4 0.8 copy-start.8
  48.3 104.0 %copy-start.4 = (bf16[768,3,192]{0,2,1:T(8,128)(2,1)S(1)}, bf16[768,3,192]{0,2,1:T(8,128)(2,1)}, u32[]{:S(2)}) copy-start(bf16[768,3,192]{0,2,1:T(8,128)(2,1)} %param.21) | copy-start | bytes 2654212
  152.4 40.6 %collective-permute-start.3 = (bf16[576,768]{1,0:T(8,128)(2,1)S(1)}, bf16[576,768]{1,0:T(8,128)(2,1)S(1)}, u32[]{:S(2)}, u32[]{:S(2)}) collective-permute-start(bf16[576,768]{1,0:T(8,128)(2,1)S(1)} %bitcast.13), channel_id=1, source_target_pairs={{0,1},{3,2},{4,5},{7,6},{8,9},{11,10},{12,13},{15,14},{16,17},{19,... | collective-permute-start | bytes 2654216 | tf_op jit(solution)/shard_map/ppermute | solution.py:1686
  192.9 0.9 copy-start.5
  296.9 3.9 %copy-start.3 = (bf16[768,768]{1,0:T(8,128)(2,1)S(1)}, bf16[768,768]{1,0:T(8,128)(2,1)}, u32[]{:S(2)}) copy-start(bf16[768,768]{1,0:T(8,128)(2,1)} %get-tuple-element.134) | copy-start | bytes 3538948
  300.9 2.1 copy-start.1
  303.0 1.4 copy-start.19
  303.0 2.0 copy-start.18
  303.0 2.6 copy-start.10
  303.0 3.2 %copy-start.20 = (f32[1,96]{1,0:T(1,128)S(1)}, f32[1,96]{1,0:T(1,128)}, u32[]{:S(2)}) copy-start(f32[1,96]{1,0:T(1,128)} %get-tuple-element.95) | copy-start | bytes 1156
  303.0 3.8 %copy-start.9 = (f32[96,768]{1,0:T(8,128)S(1)}, f32[96,768]{1,0:T(8,128)}, u32[]{:S(2)}) copy-start(f32[96,768]{1,0:T(8,128)} %get-tuple-element.142) | copy-start | bytes 884740
  303.0 4.5 %copy-start.17 = (f32[6,24]{1,0:T(8,128)S(1)}, f32[6,24]{1,0:T(8,128)}, u32[]{:S(2)}) copy-start(f32[6,24]{1,0:T(8,128)} %get-tuple-element.143) | copy-start | bytes 1732
